TPU v7x, 512 devices: a whole 4x8x8 slice. The times are simulated.
512 devices in a mesh: section: 64 (over z_lo, y, core), dp: 8 (over x, z_hi).
Axes of the slice: x: 4, y: 8, z: 8 (z_hi: 2, z_lo: 4; z = z_hi * 4 + z_lo), core: 2. Of those that a mesh axis runs over, the one named last changes fastest.
Arguments:
- layer_in: bfloat16 [64, 1024, 5120], P('section', 'dp'), may hold values from -6 to 6
- latent: bfloat16 [64, 1024, 384], P('section', 'dp'), may hold values from -6 to 6
- mix_grad: bfloat16 [64, 1024, 5120], P('section', 'dp'), may hold values from -0.1875 to 0.1875
- down_proj: bfloat16 [64, 5120, 384], P('section', 'dp'), may hold values from -0.078125 to 0.078125
- up_proj: bfloat16 [64, 384, 5120], P('section', None, 'dp'), may hold values from -0.3125 to 0.3125
- norm_gain: bfloat16 [64, 5120], P('section', 'dp'), may hold values from 0.5 to 1.5
- mix_weight: float32 [64, 8], P('section'), may hold values from 0.2 to 1
Outputs:
- up_grad: bfloat16 [64, 384, 5120], P('section', None, 'dp')
- down_grad: bfloat16 [64, 5120, 384], P('section', 'dp')
- gain_grad: float32 [64, 5120], P('section', 'dp')
- mixing_grad: float32 [64, 8], P('section')
All inputs are finite; a program needn't handle non-finite values.
Results may differ from a plain program's by a relative error of at most 0.0064.
Values may be sent and summed in bfloat16 or wider, within the bound.
No kernel may reach another device: no remote copies, remote signals or barrier semaphores. Data moves between devices by JAX's collectives and lax.ppermute only.
A program may use at most 128 MiB of HBM per device.

v0:
```python
import jax
import jax.numpy as jnp
from jax import lax
from jax.sharding import PartitionSpec as P

MIXES = 8


epsilon = 1e-06
root_coef = 0.7978845608028654


def in_order(pieces, dim):
    lengths = list(pieces.shape[1:])
    lengths[dim] *= pieces.shape[0]
    return jnp.moveaxis(pieces, 0, dim).reshape(lengths)


def copy_for_each(shard, axis):
    copies = jnp.broadcast_to(shard, (lax.axis_size(axis), *shard.shape))
    return lax.all_to_all(copies, axis, split_axis=0, concat_axis=0, tiled=True)


def gathered_copies(shard, axis, dim):
    return in_order(copy_for_each(shard, axis), dim)


def of_everyone(shard, axis):
    return copy_for_each(shard, axis).sum(axis=0)


def from_behind(value, axis, steps):
    count = lax.axis_size(axis)
    initial, last = (max(0, -steps), min(count, count - steps))
    return lax.ppermute(value, axis, [(source, source + steps) for source in range(initial, last)])


def in_blocks(shard, dim, size):
    before, after = (shard.shape[:dim], shard.shape[dim + 1 :])
    return jnp.moveaxis(shard.reshape(*before, size, -1, *after), dim, 0)


def summed_on_arrival(shard, axis, dim):
    pieces = in_blocks(shard, dim, lax.axis_size(axis))
    arrived = lax.all_to_all(pieces, axis, split_axis=0, concat_axis=0, tiled=True)
    return arrived.sum(axis=0)


def gelu_pair(values):
    tangent = jnp.tanh(root_coef * (values + 0.044715 * values * values * values))
    result = 0.5 * values * (1.0 + tangent)
    slopes = 0.5 * (1.0 + tangent) + 0.5 * values * (1.0 - tangent * tangent) * root_coef * (
        1.0 + 3.0 * 0.044715 * values * values
    )
    return (result, slopes)


def local(layer_in, latent, mix_grad, down_proj, up_proj, norm_gain, mix_weight):
    width = layer_in.shape[2]
    own_rows = layer_in.shape[1]
    cols_in, cols_grad = (
        lax.all_to_all(layer_in[0], "dp", split_axis=1, concat_axis=0, tiled=True),
        lax.all_to_all(mix_grad[0], "dp", split_axis=1, concat_axis=0, tiled=True),
    )
    latent_all = gathered_copies(latent[0], "dp", 0)
    inputs = cols_in.astype(jnp.float32)
    partial_sq = jnp.sum(inputs * inputs, axis=1)
    total_sq = of_everyone(partial_sq, "dp")
    inv_rms = lax.rsqrt(total_sq / width + epsilon)[:, None]
    scaled = inputs * inv_rms
    normed = (scaled * norm_gain[0].astype(jnp.float32)).astype(jnp.bfloat16)
    activated, slopes = gelu_pair(latent_all.astype(jnp.float32))
    act_half = activated.astype(jnp.bfloat16)
    up_block = up_proj[0]
    layer_out = inputs + jnp.dot(act_half, up_block, preferred_element_type=jnp.float32)
    weights = mix_weight[0]
    stride = lax.axis_size("section") // MIXES

    def absorb(grad_sum, piece, member):
        values = piece.astype(jnp.float32)
        return (grad_sum + weights[member] * values, jnp.sum(values * layer_out))

    grad_sum, first = absorb(jnp.zeros(inputs.shape, jnp.float32), cols_grad, 0)
    products = [first]
    for member in range(1, MIXES):
        arrived = from_behind(cols_grad, "section", -member * stride)
        grad_sum, product = absorb(grad_sum, arrived, member)
        products.append(product)
    grad_half = grad_sum.astype(jnp.bfloat16)
    up_grad = jnp.einsum(
        "tr,tc->rc", act_half, grad_half, preferred_element_type=jnp.float32
    ).astype(jnp.bfloat16)
    act_partial = jnp.einsum("tc,rc->tr", grad_half, up_block, preferred_element_type=jnp.float32)
    own_part = summed_on_arrival(act_partial, "dp", 0)
    own_slopes = lax.dynamic_slice_in_dim(slopes, lax.axis_index("dp") * own_rows, own_rows, 0)
    own_grad = (own_part * own_slopes).astype(jnp.bfloat16)
    latent_grad = gathered_copies(own_grad, "dp", 0)
    mixing = of_everyone(jnp.stack(products), "dp")
    down_grad = jnp.einsum(
        "tc,tr->cr", normed, latent_grad, preferred_element_type=jnp.float32
    ).astype(jnp.bfloat16)
    norm_grad = jnp.einsum(
        "tr,cr->tc", latent_grad, down_proj[0], preferred_element_type=jnp.float32
    )
    gain_grad = jnp.sum(norm_grad * scaled, axis=0)
    return (up_grad[None], down_grad[None], gain_grad[None], mixing[None])


def solution(mesh):
    return jax.shard_map(
        local,
        mesh=mesh,
        in_specs=(
            P("section", "dp", None),
            P("section", "dp", None),
            P("section", "dp", None),
            P("section", "dp", None),
            P("section", None, "dp"),
            P("section", "dp"),
            P("section", None),
        ),
        out_specs=(
            P("section", None, "dp"),
            P("section", "dp", None),
            P("section", "dp"),
            P("section", None),
        ),
        check_vma=False,
    )
```

profile of v0, /device:TPU:24, one launch (start us, length us, event | category | flops | bytes accessed | tf_op | source)
XLA Modules:
  0.0 498.5 jit_solution(2492502299701871320)
XLA Ops:
  0.6 1.6 copy.24
  2.4 35.4 %all_to_all.59 = bf16[128,8,640]{2,0,1:T(8,128)(2,1)} all-to-all(bf16[128,8,640]{2,0,1:T(8,128)(2,1)S(1)} %copy.17), channel_id=1, replica_groups=mesh['section'=64,'dp'=8] {'dp'}, dimensions={1} | all-to-all | bytes 2621440 | tf_op jit(solution)/shard_map/all_to_all | solution.py:63
  38.8 14.7 %all-to-all-start = ((bf16[8,128,384]{2,1,0:T(8,128)(2,1)}), bf16[8,128,384]{2,1,0:T(8,128)(2,1)S(1)}, u32[]{:S(2)}, u32[]{:S(2)}) async-start(bf16[8,128,384]{2,1,0:T(8,128)(2,1)} %broadcast_in_dim.28), calls=%async_computation | async-start | bytes 1572864 | tf_op jit(solution)/shard_map/all_to_all | solution.py:21
  56.1 1.5 copy.22
  57.5 10.1 %all-to-all-done = bf16[8,128,384]{2,1,0:T(8,128)(2,1)S(1)} async-done(((bf16[8,128,384]{2,1,0:T(8,128)(2,1)}), bf16[8,128,384]{2,1,0:T(8,128)(2,1)S(1)}, u32[]{:S(2)}, u32[]{:S(2)}) %all-to-all-start) | async-done | bytes 786464 | tf_op jit(solution)/shard_map/all_to_all | solution.py:21
  67.7 4.9 all-to-all-start.2
  73.9 1.3 collective-permute-start.3
  75.2 1.3 collective-permute-start.4
  76.5 1.4 collective-permute-done
  79.2 20.2 %collective-permute-done.1 = bf16[1024,640]{1,0:T(8,128)(2,1)} collective-permute-done((bf16[1024,640]{1,0:T(8,128)(2,1)}, bf16[1024,640]{1,0:T(8,128)(2,1)}, u32[]{:S(2)}, u32[]{:S(2)}) %collective-permute-start.1) | collective-permute-done | bytes 1310752 | tf_op jit(solution)/shard_map/ppermute | solution.py:35
  101.9 1.7 convert_bitcast_fusion
  103.6 3.2 copy.20
  106.8 55.7 %collective-permute-done.2 = bf16[1024,640]{1,0:T(8,128)(2,1)} collective-permute-done((bf16[1024,640]{1,0:T(8,128)(2,1)}, bf16[1024,640]{1,0:T(8,128)(2,1)}, u32[]{:S(2)}, u32[]{:S(2)}) %collective-permute-start.2) | collective-permute-done | bytes 1310752 | tf_op jit(solution)/shard_map/ppermute | solution.py:35
  162.5 211.0 %collective-permute-done.3 = bf16[1024,640]{1,0:T(8,128)(2,1)} collective-permute-done((bf16[1024,640]{1,0:T(8,128)(2,1)}, bf16[1024,640]{1,0:T(8,128)(2,1)}, u32[]{:S(2)}, u32[]{:S(2)}) %collective-permute-start.3) | collective-permute-done | bytes 1310752 | tf_op jit(solution)/shard_map/ppermute | solution.py:35
  373.5 12.8 %fusion.15 = (f32[]{:T(128)}, f32[]{:T(128)}, f32[]{:T(128)}, f32[]{:T(128)}, f32[]{:T(128)}, /*index=5*/f32[]{:T(128)}, f32[]{:T(128)}, f32[]{:T(128)}, bf16[1024,640]{1,0:T(8,128)(2,1)S(1)}) fusion(bf16[1024,640]{1,0:T(8,128)(2,1)} %collective-permute-done.6, bf16[1024,640]{1,0:T(8,128)(2,1)} %collective-permute-done.5, ...), kind=kOutput, calls=%fused_computation.31 | convolution fusion | flops 530186240 | bytes 15695936 | tf_op jit(solution)/shard_map/dot_general | solution.py:75
  387.4 2.1 fusion.31
  389.5 10.2 %all-to-all-start.4 = ((f32[8,128,384]{2,1,0:T(8,128)}), f32[8,128,384]{2,1,0:T(8,128)}, u32[]{:S(2)}, u32[]{:S(2)}) async-start(f32[8,128,384]{2,1,0:T(8,128)} %fusion.31), calls=%async_computation.4 | async-start | bytes 3145728 | tf_op jit(solution)/shard_map/all_to_all | solution.py:45
  399.7 2.6 broadcast_add_fusion
  402.5 35.2 %all-to-all-done.4 = f32[8,128,384]{2,1,0:T(8,128)} async-done(((f32[8,128,384]{2,1,0:T(8,128)}), f32[8,128,384]{2,1,0:T(8,128)}, u32[]{:S(2)}, u32[]{:S(2)}) %all-to-all-start.4) | async-done | bytes 1572896 | tf_op jit(solution)/shard_map/all_to_all | solution.py:45
  438.3 5.0 all-to-all-start.3
  443.2 1.4 bitcast_convert_fusion
  444.6 5.3 %stack.35 = f32[8]{0:T(128)S(1)} concatenate(f32[1]{0:T(128)} %bitcast.27, f32[1]{0:T(128)} %bitcast.28, f32[1]{0:T(128)} %bitcast.29, f32[1]{0:T(128)} %bitcast.30, f32[1]{0:T(128)} %bitcast.31, f32[1]{0:T(128)} %bitcast.32, f32[1]{0:T(128)} %bitcast.33, f32[1]{0:T(128)} %bitcast.34), dimensions={0} | concatenate | bytes 64 | tf_op jit(solution)/shard_map/stack | solution.py:98
  449.9 2.2 reduce_sum.119
  452.1 1.3 all-to-all-done.3
  454.0 8.3 %all-to-all-start.6 = ((f32[8,1,8]{2,1,0:T(1,128)}), f32[8,1,8]{2,1,0:T(1,128)S(1)}, u32[]{:S(2)}, u32[]{:S(2)}) async-start(f32[8,1,8]{2,1,0:T(1,128)} %broadcast_in_dim.35), calls=%async_computation.6 | async-start | bytes 8192 | tf_op jit(solution)/shard_map/all_to_all | solution.py:21
  462.3 1.3 fusion.38
  463.6 8.7 %all-to-all-done.6 = f32[8,1,8]{2,1,0:T(1,128)S(1)} async-done(((f32[8,1,8]{2,1,0:T(1,128)}), f32[8,1,8]{2,1,0:T(1,128)S(1)}, u32[]{:S(2)}, u32[]{:S(2)}) %all-to-all-start.6) | async-done | bytes 288 | tf_op jit(solution)/shard_map/all_to_all | solution.py:21
  473.3 4.2 all-to-all-start.5
  477.6 3.4 fusion.28
  481.5 10.5 %all-to-all-done.5 = bf16[8,128,384]{2,1,0:T(8,128)(2,1)} async-done(((bf16[8,128,384]{2,1,0:T(8,128)(2,1)}), bf16[8,128,384]{2,1,0:T(8,128)(2,1)}, u32[]{:S(2)}, u32[]{:S(2)}) %all-to-all-start.5) | async-done | bytes 786464 | tf_op jit(solution)/shard_map/all_to_all | solution.py:21
  492.1 3.1 fusion.17
  495.7 2.8 fusion.29
  (36 shorter events, 13.5 us)
Async XLA Ops:
  0.6 372.9 %copy-start = (bf16[1,384,640]{2,1,0:T(8,128)(2,1)S(1)}, bf16[1,384,640]{2,1,0:T(8,128)(2,1)}, u32[]{:S(2)}) copy-start(bf16[1,384,640]{2,1,0:T(8,128)(2,1)} %param.11) | copy-start | bytes 1474564
  2.4 35.4 %copy-start.4 = (bf16[1,128,384]{2,1,0:T(8,128)(2,1)S(1)}, bf16[1,128,384]{2,1,0:T(8,128)(2,1)}, u32[]{:S(2)}) copy-start(bf16[1,128,384]{2,1,0:T(8,128)(2,1)} %param.8) | copy-start | bytes 294916
  37.8 18.3 %copy-start.3 = (bf16[1,128,5120]{2,1,0:T(8,128)(2,1)S(1)}, bf16[1,128,5120]{2,1,0:T(8,128)(2,1)}, u32[]{:S(2)}) copy-start(bf16[1,128,5120]{2,1,0:T(8,128)(2,1)} %param.7) | copy-start | bytes 3932164
  38.8 28.9 %all-to-all-start = ((bf16[8,128,384]{2,1,0:T(8,128)(2,1)}), bf16[8,128,384]{2,1,0:T(8,128)(2,1)S(1)}, u32[]{:S(2)}, u32[]{:S(2)}) async-start(bf16[8,128,384]{2,1,0:T(8,128)(2,1)} %broadcast_in_dim.28), calls=%async_computation | async-start | bytes 1572864 | tf_op jit(solution)/shard_map/all_to_all | solution.py:21
  53.5 24.4 %collective-permute-start = (bf16[1024,640]{1,0:T(8,128)(2,1)}, bf16[1024,640]{1,0:T(8,128)(2,1)}, u32[]{:S(2)}, u32[]{:S(2)}) collective-permute-start(bf16[1024,640]{1,0:T(8,128)(2,1)} %bitcast.89), channel_id=1, source_target_pairs={{64,0},{72,8},{80,16},{88,24},{96,32},{104,40},{112,48},{120,56},{... | collective-permute-start | bytes 3932168 | tf_op jit(solution)/shard_map/ppermute | solution.py:35
  54.8 44.6 %collective-permute-start.1 = (bf16[1024,640]{1,0:T(8,128)(2,1)}, bf16[1024,640]{1,0:T(8,128)(2,1)}, u32[]{:S(2)}, u32[]{:S(2)}) collective-permute-start(bf16[1024,640]{1,0:T(8,128)(2,1)} %bitcast.90), channel_id=1, source_target_pairs={{128,0},{136,8},{144,16},{152,24},{160,32},{168,40},{176,48},{184,... | collective-permute-start | bytes 3932168 | tf_op jit(solution)/shard_map/ppermute | solution.py:35
  57.5 43.2 %copy-start.5 = (f32[1,8]{1,0:T(1,128)S(1)}, f32[1,8]{1,0:T(1,128)}, u32[]{:S(2)}) copy-start(f32[1,8]{1,0:T(1,128)} %param.13) | copy-start | bytes 100
  67.7 34.2 %all-to-all-start.2 = ((bf16[128,8,640]{0,2,1:T(8,128)(2,1)}), bf16[128,8,640]{0,2,1:T(8,128)(2,1)S(1)}, u32[]{:S(2)}, u32[]{:S(2)}) async-start(bf16[128,8,640]{0,2,1:T(8,128)(2,1)} %bitcast.86), calls=%async_computation.2 | async-start | bytes 2621440 | tf_op jit(solution)/shard_map/all_to_all | solution.py:62
  72.6 89.9 %collective-permute-start.2 = (bf16[1024,640]{1,0:T(8,128)(2,1)}, bf16[1024,640]{1,0:T(8,128)(2,1)}, u32[]{:S(2)}, u32[]{:S(2)}) collective-permute-start(bf16[1024,640]{1,0:T(8,128)(2,1)} %bitcast.91), channel_id=1, source_target_pairs={{192,0},{200,8},{208,16},{216,24},{224,32},{232,40},{240,48},{248,... | collective-permute-start | bytes 3932168 | tf_op jit(solution)/shard_map/ppermute | solution.py:35
  73.9 299.6 %collective-permute-start.3 = (bf16[1024,640]{1,0:T(8,128)(2,1)}, bf16[1024,640]{1,0:T(8,128)(2,1)}, u32[]{:S(2)}, u32[]{:S(2)}) collective-permute-start(bf16[1024,640]{1,0:T(8,128)(2,1)} %bitcast.92), channel_id=1, source_target_pairs={{256,0},{264,8},{272,16},{280,24},{288,32},{296,40},{304,48},{312,... | collective-permute-start | bytes 3932168 | tf_op jit(solution)/shard_map/ppermute | solution.py:35
  75.2 298.3 %collective-permute-start.4 = (bf16[1024,640]{1,0:T(8,128)(2,1)}, bf16[1024,640]{1,0:T(8,128)(2,1)}, u32[]{:S(2)}, u32[]{:S(2)}) collective-permute-start(bf16[1024,640]{1,0:T(8,128)(2,1)} %bitcast.93), channel_id=1, source_target_pairs={{320,0},{328,8},{336,16},{344,24},{352,32},{360,40},{368,48},{376,... | collective-permute-start | bytes 3932168 | tf_op jit(solution)/shard_map/ppermute | solution.py:35
  77.9 295.6 %collective-permute-start.5 = (bf16[1024,640]{1,0:T(8,128)(2,1)}, bf16[1024,640]{1,0:T(8,128)(2,1)}, u32[]{:S(2)}, u32[]{:S(2)}) collective-permute-start(bf16[1024,640]{1,0:T(8,128)(2,1)} %bitcast.94), channel_id=1, source_target_pairs={{384,0},{392,8},{400,16},{408,24},{416,32},{424,40},{432,48},{440,... | collective-permute-start | bytes 3932168 | tf_op jit(solution)/shard_map/ppermute | solution.py:35
  99.4 274.1 %collective-permute-start.6 = (bf16[1024,640]{1,0:T(8,128)(2,1)}, bf16[1024,640]{1,0:T(8,128)(2,1)}, u32[]{:S(2)}, u32[]{:S(2)}) collective-permute-start(bf16[1024,640]{1,0:T(8,128)(2,1)} %bitcast.95), channel_id=1, source_target_pairs={{448,0},{456,8},{464,16},{472,24},{480,32},{488,40},{496,48},{504,... | collective-permute-start | bytes 3932168 | tf_op jit(solution)/shard_map/ppermute | solution.py:35
  386.3 1.1 copy-start.2
  389.5 48.1 %all-to-all-start.4 = ((f32[8,128,384]{2,1,0:T(8,128)}), f32[8,128,384]{2,1,0:T(8,128)}, u32[]{:S(2)}, u32[]{:S(2)}) async-start(f32[8,128,384]{2,1,0:T(8,128)} %fusion.31), calls=%async_computation.4 | async-start | bytes 3145728 | tf_op jit(solution)/shard_map/all_to_all | solution.py:45
  438.3 15.1 %all-to-all-start.3 = ((f32[8,1,1024]{2,1,0:T(1,128)}), f32[8,1,1024]{2,1,0:T(1,128)S(1)}, u32[]{:S(2)}, u32[]{:S(2)}) async-start(f32[8,1,1024]{2,1,0:T(1,128)} %broadcast_in_dim.31), calls=%async_computation.3 | async-start | bytes 65536 | tf_op jit(solution)/shard_map/all_to_all | solution.py:21
  444.6 17.7 %copy-start.1 = (f32[1024,384]{1,0:T(8,128)S(1)}, f32[1024,384]{1,0:T(8,128)}, u32[]{:S(2)}) copy-start(f32[1024,384]{1,0:T(8,128)} %get-tuple-element.14) | copy-start | bytes 4718596
  454.0 18.3 %all-to-all-start.6 = ((f32[8,1,8]{2,1,0:T(1,128)}), f32[8,1,8]{2,1,0:T(1,128)S(1)}, u32[]{:S(2)}, u32[]{:S(2)}) async-start(f32[8,1,8]{2,1,0:T(1,128)} %broadcast_in_dim.35), calls=%async_computation.6 | async-start | bytes 8192 | tf_op jit(solution)/shard_map/all_to_all | solution.py:21
  462.3 15.2 %copy-start.6 = (bf16[1,640]{1,0:T(2,128)(2,1)S(1)}, bf16[1,640]{1,0:T(2,128)(2,1)}, u32[]{:S(2)}) copy-start(bf16[1,640]{1,0:T(2,128)(2,1)} %param.12) | copy-start | bytes 3844
  473.3 18.8 %all-to-all-start.5 = ((bf16[8,128,384]{2,1,0:T(8,128)(2,1)}), bf16[8,128,384]{2,1,0:T(8,128)(2,1)}, u32[]{:S(2)}, u32[]{:S(2)}) async-start(bf16[8,128,384]{2,1,0:T(8,128)(2,1)} %broadcast_in_dim.32), calls=%async_computation.5 | async-start | bytes 1572864 | tf_op jit(solution)/shard_map/all_to_all | solution.py:21
where the time goes:
time: 500 us; the launch traced here: 499 us
  waiting for transfers between devices  354 us (71%)
  starting transfers between devices  56.3 us (11%)
  blocking collectives  35.4 us (7%)
  matrix products  24.2 us (5%)
  local copies, waits for them, and re-layouts  17.2 us (3%)
  other arithmetic  10.5 us (2%)
    ppermute x7, waiting for transfers between devices, from_behind(): lax.ppermute(value, axis, [(source, source + steps) for source in range(i...  288 us
    all_to_all x1, blocking collectives, local(): lax.all_to_all(mix_grad[0], 'dp', split_axis=1, concat_axis=0, tiled=True)  35.4 us
    all_to_all x1, waiting for transfers between devices, summed_on_arrival(): lax.all_to_all(pieces, axis, split_axis=0, concat_axis=0, tiled=True)  35.2 us
    all_to_all x4, starting transfers between devices, copy_for_each(): return lax.all_to_all(copies, axis, split_axis=0, concat_axis=0, tiled=True)  32.1 us
    all_to_all x4, waiting for transfers between devices, copy_for_each(): return lax.all_to_all(copies, axis, split_axis=0, concat_axis=0, tiled=True)  30.7 us
    dot_general x1, matrix products, local(): jnp.dot(act_half, up_block, preferred_element_type=jnp.float32)  12.8 us
    all_to_all x1, starting transfers between devices, summed_on_arrival(): lax.all_to_all(pieces, axis, split_axis=0, concat_axis=0, tiled=True)  10.2 us
  transfers between devices with their start and end apart: 13, of which 9 were waited for; matrix products, arithmetic and copies ran while one was open for 5% of the time, Pallas kernels for 0%

commit v1 on v0

v1 whole, which is shorter than its diff:
```python
import jax
import jax.numpy as jnp
from jax import lax
from jax.experimental import pallas as pl
from jax.experimental.pallas import tpu as pltpu
from jax.sharding import Mesh, PartitionSpec as P

MIXES = 8
epsilon = 1e-06
root_coef = 0.7978845608028654
GROUP = ("zl", "yh")


def gelu_pair(values):
    tangent = jnp.tanh(root_coef * (values + 0.044715 * values * values * values))
    result = 0.5 * values * (1.0 + tangent)
    slopes = 0.5 * (1.0 + tangent) + 0.5 * values * (1.0 - tangent * tangent) * root_coef * (
        1.0 + 3.0 * 0.044715 * values * values
    )
    return (result, slopes)


def exchange(pieces, axes):
    return lax.all_to_all(pieces, axes, split_axis=0, concat_axis=0, tiled=True)


def swapped(value, axis):
    return lax.ppermute(value, axis, [(0, 1), (1, 0)])


def shifted(value, axis, steps):
    count = lax.axis_size(axis)
    return lax.ppermute(value, axis, [(i, (i + steps) % count) for i in range(count)])


def mix_body(coef, grads, out):
    halves, sections, rows, cols = grads.shape
    for half in range(halves):
        for at in range(0, cols, 128):
            lanes = slice(at, at + 128)
            tiles = [grads[half, k, :, lanes].astype(jnp.float32) for k in range(sections)]
            for k in range(sections):
                total = coef[k, 0] * tiles[k]
                for m in range(1, sections - k):
                    total = total + coef[k, m] * tiles[k + m]
                out[k, half, :, lanes] = total.astype(jnp.bfloat16)


def mix(weights, grads):
    halves, sections, rows, cols = grads.shape
    block = 640
    return pl.pallas_call(
        mix_body,
        grid=(cols // block,),
        in_specs=[
            pl.BlockSpec(memory_space=pltpu.SMEM),
            pl.BlockSpec((halves, sections, rows, block), lambda j: (0, 0, 0, j)),
        ],
        out_specs=pl.BlockSpec((sections, halves, rows, block), lambda j: (0, 0, 0, j)),
        out_shape=jax.ShapeDtypeStruct((sections, halves, rows, cols), jnp.bfloat16),
        name="mix",
    )(weights, grads)


def gram_body(grads, outs, result):
    halves, sections, rows, cols = grads.shape
    sums = {}
    for half in range(halves):
        for at in range(0, cols, 128):
            lanes = slice(at, at + 128)
            left = [outs[k, half, :, lanes].astype(jnp.float32) for k in range(sections)]
            right = [grads[half, k, :, lanes].astype(jnp.float32) for k in range(sections)]
            for k in range(sections):
                for m in range(sections - k):
                    product = left[k] * right[k + m]
                    folded = product[:8] + product[8:]
                    sums[k, m] = folded if (k, m) not in sums else sums[k, m] + folded

    @pl.when(pl.program_id(0) == 0)
    def _():
        result[...] = jnp.zeros(result.shape, jnp.float32)

    for (k, m), total in sums.items():
        result[k * MIXES + m] += total


def gram(grads, outs):
    halves, sections, rows, cols = grads.shape
    block = 640
    return pl.pallas_call(
        gram_body,
        grid=(cols // block,),
        in_specs=[
            pl.BlockSpec((halves, sections, rows, block), lambda j: (0, 0, 0, j)),
            pl.BlockSpec((sections, halves, rows, block), lambda j: (0, 0, 0, j)),
        ],
        out_specs=pl.BlockSpec((sections * MIXES, 8, 128), lambda j: (0, 0, 0)),
        out_shape=jax.ShapeDtypeStruct((sections * MIXES, 8, 128), jnp.float32),
        name="gram",
    )(grads, outs)


def local(layer_in, latent, mix_grad, down_proj, up_proj, norm_gain, mix_weight):
    layer_in, latent, mix_grad = (layer_in[0], latent[0], mix_grad[0])
    tokens, width = layer_in.shape
    xs, zs = (lax.axis_size("x"), lax.axis_size("zh"))
    sections = lax.axis_size("zl") * lax.axis_size("yh")
    block = width // (xs * zs)
    rows = tokens // sections
    at_x, at_zh, at_zl, at_yh = [lax.axis_index(a) for a in ("x", "zh", "zl", "yh")]
    first = at_zh == 0

    def feature_half(array, half):
        return jnp.concatenate(
            [array[:, (i * zs + half) * block : (i * zs + half + 1) * block] for i in range(xs)], axis=1
        )

    def both_halves(own, other):
        own, other = [t.reshape(sections, rows, *t.shape[1:]) for t in (own, other)]
        pair = jnp.stack([jnp.where(first, own, other), jnp.where(first, other, own)], axis=1)
        return pair.reshape(2 * tokens, *own.shape[2:])

    grads = jnp.stack([feature_half(mix_grad, 0), feature_half(mix_grad, 1)])
    grads = exchange(grads.reshape(zs * sections, rows, xs * block), ("zh", *GROUP))
    grads = grads.reshape(zs, sections, rows, xs * block)

    own_weight = mix_weight[0]
    other_weight = swapped(own_weight, "yh")
    pair = jnp.stack(
        [jnp.where(at_yh == 0, own_weight, other_weight), jnp.where(at_yh == 0, other_weight, own_weight)]
    )
    places = lax.axis_size("zl")
    weights = jnp.zeros((places, *pair.shape), jnp.float32)
    for step in range(places):
        piece = shifted(pair, "zl", step) if step else pair
        here = (jnp.arange(places) == (at_zl - step) % places)[:, None, None]
        weights = jnp.where(here, piece[None], weights)
    weights = weights.reshape(sections, MIXES)

    half_0, half_1 = (feature_half(layer_in, 0), feature_half(layer_in, 1))
    kept = jnp.where(first, half_0, half_1)
    inputs = both_halves(kept, swapped(jnp.where(first, half_1, half_0), "zh"))
    wide = layer_in.astype(jnp.float32)
    own_rms = lax.rsqrt(jnp.sum(wide * wide, axis=1) / width + epsilon)
    inv_rms = both_halves(own_rms, swapped(own_rms, "zh"))
    latents = both_halves(latent, swapped(latent, "zh"))
    activated, slopes = gelu_pair(latents.astype(jnp.float32))
    act_half = activated.astype(jnp.bfloat16)

    up_block = up_proj[0]
    parts = jnp.stack([up_block] + [shifted(up_block, "x", step) for step in range(1, xs)])
    up_half = jnp.concatenate(
        [lax.dynamic_index_in_dim(parts, (at_x - i) % xs, 0, False) for i in range(xs)], axis=1
    )

    branch = jnp.dot(act_half, up_half, preferred_element_type=jnp.float32)
    layer_out = (inputs.astype(jnp.float32) + branch).astype(jnp.bfloat16)

    mixed = mix(weights, grads)
    out_grad = exchange(mixed, GROUP).reshape(2 * tokens, xs * block)

    outs = exchange(layer_out.reshape(sections, zs, rows, xs * block), GROUP)
    products = jnp.sum(gram(grads, outs), axis=(1, 2)).reshape(sections, MIXES)
    spread = jnp.broadcast_to(products[:, None], (sections, xs * zs, MIXES))
    mixing = exchange(spread.reshape(sections * xs * zs, MIXES), (*GROUP, "x", "zh")).sum(axis=0)

    act_partial = jnp.einsum("tc,rc->tr", out_grad, up_half, preferred_element_type=jnp.float32)
    act_other = swapped(act_partial.astype(jnp.bfloat16), "zh").astype(jnp.float32)
    scaled_grad = ((act_partial + act_other) * slopes * inv_rms[:, None]).astype(jnp.bfloat16)

    def by_x(array):
        return jnp.stack([array[:, i * block : (i + 1) * block] for i in range(xs)])

    def to_all_x(array):
        return exchange(jnp.broadcast_to(array, (xs, *array.shape)), "x")

    all_inputs = exchange(by_x(inputs), "x")
    all_grads = exchange(by_x(out_grad), "x")
    all_act = to_all_x(act_half)
    all_latent_grads = to_all_x(scaled_grad)

    up_grad = jnp.einsum(
        "xtr,xtc->rc", all_act, all_grads, preferred_element_type=jnp.float32
    ).astype(jnp.bfloat16)
    gram_grad = jnp.einsum(
        "xtc,xtr->cr", all_inputs, all_latent_grads, preferred_element_type=jnp.float32
    )
    gain = norm_gain[0].astype(jnp.float32)
    down_grad = (gram_grad * gain[:, None]).astype(jnp.bfloat16)
    gain_grad = jnp.sum(gram_grad * down_proj[0].astype(jnp.float32), axis=1)
    return (up_grad[None], down_grad[None], gain_grad[None], mixing[None])


def solution(mesh):
    devices = mesh.devices.reshape(4, 2, 8, 4, 2)
    fine = Mesh(devices, ("zl", "yh", "r", "x", "zh"))
    section, dp = (("zl", "yh", "r"), ("x", "zh"))
    return jax.shard_map(
        local,
        mesh=fine,
        in_specs=(
            P(section, dp, None),
            P(section, dp, None),
            P(section, dp, None),
            P(section, dp, None),
            P(section, None, dp),
            P(section, dp),
            P(section, None),
        ),
        out_specs=(
            P(section, None, dp),
            P(section, dp, None),
            P(section, dp),
            P(section, None),
        ),
        check_vma=False,
    )
```

time: 500 us -> 307 us (0.61)
  the two profiles are of different devices: /device:TPU:24 before, /device:TPU:8 now
where the time goes in v1:
time: 307 us; the launch traced here: 305 us
  waiting for transfers between devices  135 us (44%)
  starting transfers between devices  122 us (40%)
  local copies, waits for them, and re-layouts  17.1 us (6%)
  other arithmetic  12.2 us (4%)
  matrix products  9.58 us (3%)
  Pallas kernels  7.71 us (3%)
    ppermute x5, waiting for transfers between devices, swapped(): return lax.ppermute(value, axis, [(0, 1), (1, 0)])  73.8 us
    all_to_all x8, starting transfers between devices, exchange(): return lax.all_to_all(pieces, axes, split_axis=0, concat_axis=0, tiled=True)  65.2 us
    all_to_all x8, waiting for transfers between devices, exchange(): return lax.all_to_all(pieces, axes, split_axis=0, concat_axis=0, tiled=True)  59.4 us
    ppermute x5, starting transfers between devices, swapped(): return lax.ppermute(value, axis, [(0, 1), (1, 0)])  30.1 us
    ppermute x6, starting transfers between devices, shifted(): lax.ppermute(value, axis, [(i, (i + steps) % count) for i in range(count)])  26.9 us
  transfers between devices with their start and end apart: 19, of which 10 were waited for; matrix products, arithmetic and copies ran while one was open for 10% of the time, Pallas kernels for 3%

profile of v1, /device:TPU:8, one launch (start us, length us, event | category | flops | bytes accessed | tf_op | source)
XLA Modules:
  0.0 305.2 jit_solution(14882011283359457518)
XLA Ops:
  3.5 14.9 %all-to-all-start.1 = ((bf16[16,16,2560]{2,1,0:T(8,128)(2,1)}), bf16[16,16,2560]{2,1,0:T(8,128)(2,1)S(1)}, u32[]{:S(2)}, u32[]{:S(2)}) async-start(bf16[16,16,2560]{2,1,0:T(8,128)(2,1)} %bitcast.122), calls=%async_computation.1 | async-start | bytes 2621440 | tf_op jit(solution)/shard_map/all_to_all | solution.py:24
  18.4 3.4 %collective-permute-start.6 = (bf16[384,640]{1,0:T(8,128)(2,1)}, bf16[384,640]{1,0:T(8,128)(2,1)}, u32[]{:S(2)}, u32[]{:S(2)}) collective-permute-start(bf16[384,640]{1,0:T(8,128)(2,1)} %bitcast.53), channel_id=1, source_target_pairs={{0,2},{2,4},{4,6},{6,0},{1,3},{3,5},{5,7},{7,1},{8,10},{10,12},{12... | collective-permute-start | bytes 1474568 | tf_op jit(solution)/shard_map/ppermute | solution.py:33
  21.8 4.6 %collective-permute-start.7 = (bf16[384,640]{1,0:T(8,128)(2,1)}, bf16[384,640]{1,0:T(8,128)(2,1)}, u32[]{:S(2)}, u32[]{:S(2)}) collective-permute-start(bf16[384,640]{1,0:T(8,128)(2,1)} %bitcast.53), channel_id=1, source_target_pairs={{0,4},{2,6},{4,0},{6,2},{1,5},{3,7},{5,1},{7,3},{8,12},{10,14},{12... | collective-permute-start | bytes 1474568 | tf_op jit(solution)/shard_map/ppermute | solution.py:33
  26.4 3.3 %collective-permute-start.8 = (bf16[384,640]{1,0:T(8,128)(2,1)}, bf16[384,640]{1,0:T(8,128)(2,1)}, u32[]{:S(2)}, u32[]{:S(2)}) collective-permute-start(bf16[384,640]{1,0:T(8,128)(2,1)} %bitcast.53), channel_id=1, source_target_pairs={{0,6},{2,0},{4,2},{6,4},{1,7},{3,1},{5,3},{7,5},{8,14},{10,8},{12,... | collective-permute-start | bytes 1474568 | tf_op jit(solution)/shard_map/ppermute | solution.py:33
  29.8 7.7 %collective-permute-start.1 = (f32[8]{0:T(128)S(1)}, f32[8]{0:T(128)S(1)}, u32[]{:S(2)}, u32[]{:S(2)}) collective-permute-start(f32[8]{0:T(128)S(1)} %bitcast.143), channel_id=1, source_target_pairs={{0,64},{64,0},{1,65},{65,1},{2,66},{66,2},{3,67},{67,3},{4,68},{68... | collective-permute-start | bytes 104 | tf_op jit(solution)/shard_map/ppermute | solution.py:28
  41.7 22.2 %collective-permute-done.1 = f32[8]{0:T(128)S(1)} collective-permute-done((f32[8]{0:T(128)S(1)}, f32[8]{0:T(128)S(1)}, u32[]{:S(2)}, u32[]{:S(2)}) %collective-permute-start.1) | collective-permute-done | bytes 64 | tf_op jit(solution)/shard_map/ppermute | solution.py:28
  63.9 10.4 %collective-permute-start.2 = (f32[2,8]{1,0:T(2,128)S(1)}, f32[2,8]{1,0:T(2,128)S(1)}, u32[]{:S(2)}, u32[]{:S(2)}) collective-permute-start(f32[2,8]{1,0:T(2,128)S(1)} %pad_maximum_fusion.10), channel_id=1, source_target_pairs={{0,384},{128,0},{256,128},{384,256},{1,385},{129,1},{257,129},{385... | collective-permute-start | bytes 200 | tf_op jit(solution)/shard_map/ppermute | solution.py:33
  74.3 1.9 collective-permute-start.3
  76.3 3.2 %collective-permute-start.4 = (f32[2,8]{1,0:T(2,128)S(1)}, f32[2,8]{1,0:T(2,128)S(1)}, u32[]{:S(2)}, u32[]{:S(2)}) collective-permute-start(f32[2,8]{1,0:T(2,128)S(1)} %pad_maximum_fusion.10), channel_id=1, source_target_pairs={{0,128},{128,256},{256,384},{384,0},{1,129},{129,257},{257,385},{3... | collective-permute-start | bytes 200 | tf_op jit(solution)/shard_map/ppermute | solution.py:33
  83.5 6.9 %collective-permute-start = (bf16[128,384]{1,0:T(8,128)(2,1)S(1)}, bf16[128,384]{1,0:T(8,128)(2,1)S(1)}, u32[]{:S(2)}, u32[]{:S(2)}) collective-permute-start(bf16[128,384]{1,0:T(8,128)(2,1)S(1)} %bitcast.135), channel_id=1, source_target_pairs={{0,1},{1,0},{2,3},{3,2},{4,5},{5,4},{6,7},{7,6},{8,9},{9,8},{10,11... | collective-permute-start | bytes 294920 | tf_op jit(solution)/shard_map/ppermute | solution.py:28
  92.3 4.0 %mix.1 = bf16[8,2,16,2560]{3,2,1,0:T(8,128)(2,1)} custom-call(f32[8,8]{1,0:T(8,128)} %select_select_fusion.coef, bf16[2,8,16,2560]{3,2,1,0:T(8,128)(2,1)} %bitcast.117), custom_call_target="tpu_custom_call" | custom-call | tf_op jit(solution)/shard_map/mix/pallas_call | solution.py:52
  96.3 6.4 %all-to-all-start.2 = ((bf16[8,2,16,2560]{3,2,1,0:T(8,128)(2,1)}), bf16[8,2,16,2560]{3,2,1,0:T(8,128)(2,1)S(1)}, u32[]{:S(2)}, u32[]{:S(2)}) async-start(bf16[8,2,16,2560]{3,2,1,0:T(8,128)(2,1)} %mix.1), calls=%async_computation.2 | async-start | bytes 2621440 | tf_op jit(solution)/shard_map/all_to_all | solution.py:24
  103.0 7.3 %collective-permute-start.5 = (bf16[128,2560]{1,0:T(8,128)(2,1)S(1)}, bf16[128,2560]{1,0:T(8,128)(2,1)}, u32[]{:S(2)}, u32[]{:S(2)}) collective-permute-start(bf16[128,2560]{1,0:T(8,128)(2,1)S(1)} %maximum_select_fusion.1), channel_id=1, source_target_pairs={{0,1},{1,0},{2,3},{3,2},{4,5},{5,4},{6,7},{7,6},{8,9},{9,8},{10,11... | collective-permute-start | bytes 1966088 | tf_op jit(solution)/shard_map/ppermute | solution.py:28
  113.7 44.4 %collective-permute-done.5 = bf16[128,2560]{1,0:T(8,128)(2,1)} collective-permute-done((bf16[128,2560]{1,0:T(8,128)(2,1)S(1)}, bf16[128,2560]{1,0:T(8,128)(2,1)}, u32[]{:S(2)}, u32[]{:S(2)}) %collective-permute-start.5) | collective-permute-done | bytes 655392 | tf_op jit(solution)/shard_map/ppermute | solution.py:28
  161.1 4.4 %all-to-all-start.4 = ((bf16[4,256,640]{2,1,0:T(8,128)(2,1)}), bf16[4,256,640]{2,1,0:T(8,128)(2,1)}, u32[]{:S(2)}, u32[]{:S(2)}) async-start(bf16[4,256,640]{2,1,0:T(8,128)(2,1)} %pad_maximum_fusion.5), calls=%async_computation.4 | async-start | bytes 2621440 | tf_op jit(solution)/shard_map/all_to_all | solution.py:24
  165.5 2.2 fusion.24
  167.7 6.2 %collective-permute-start.9 = (bf16[256,384]{1,0:T(8,128)(2,1)S(1)}, bf16[256,384]{1,0:T(8,128)(2,1)S(1)}, u32[]{:S(2)}, u32[]{:S(2)}) collective-permute-start(bf16[256,384]{1,0:T(8,128)(2,1)S(1)} %get-tuple-element.56), channel_id=1, source_target_pairs={{0,1},{1,0},{2,3},{3,2},{4,5},{5,4},{6,7},{7,6},{8,9},{9,8},{10,11... | collective-permute-start | bytes 589832 | tf_op jit(solution)/shard_map/ppermute | solution.py:28
  174.0 7.2 %collective-permute-done.9 = bf16[256,384]{1,0:T(8,128)(2,1)S(1)} collective-permute-done((bf16[256,384]{1,0:T(8,128)(2,1)S(1)}, bf16[256,384]{1,0:T(8,128)(2,1)S(1)}, u32[]{:S(2)}, u32[]{:S(2)}) %collective-permute-start.9) | collective-permute-done | bytes 196640 | tf_op jit(solution)/shard_map/ppermute | solution.py:28
  183.4 4.8 %all-to-all-start.5 = ((bf16[4,256,384]{1,2,0:T(8,128)(2,1)}), bf16[4,256,384]{1,2,0:T(8,128)(2,1)S(1)}, u32[]{:S(2)}, u32[]{:S(2)}) async-start(bf16[4,256,384]{1,2,0:T(8,128)(2,1)} %broadcast_in_dim.130), calls=%async_computation.5 | async-start | bytes 1572864 | tf_op jit(solution)/shard_map/all_to_all | solution.py:24
  189.9 7.7 %all-to-all-done.5 = bf16[4,256,384]{1,2,0:T(8,128)(2,1)S(1)} async-done(((bf16[4,256,384]{1,2,0:T(8,128)(2,1)}), bf16[4,256,384]{1,2,0:T(8,128)(2,1)S(1)}, u32[]{:S(2)}, u32[]{:S(2)}) %all-to-all-start.5) | async-done | bytes 786464 | tf_op jit(solution)/shard_map/all_to_all | solution.py:24
  197.7 2.1 broadcast_in_dim.107
  199.7 3.5 %all-to-all-start = ((bf16[4,256,384]{1,2,0:T(8,128)(2,1)}), bf16[4,256,384]{1,2,0:T(8,128)(2,1)S(1)}, u32[]{:S(2)}, u32[]{:S(2)}) async-start(bf16[4,256,384]{1,2,0:T(8,128)(2,1)} %broadcast_in_dim.107), calls=%async_computation | async-start | bytes 1572864 | tf_op jit(solution)/shard_map/all_to_all | solution.py:24
  203.2 3.5 %fusion = bf16[256,2560]{1,0:T(8,128)(2,1)} fusion(bf16[256,384]{1,0:T(8,128)(2,1)} %get-tuple-element.49, bf16[256,2560]{1,0:T(8,128)(2,1)S(1)} %bitcast.124, bf16[384,640]{1,0:T(8,128)(2,1)} %get-tuple-element.19, bf16[384,640]{1,0:T(8,128)(2,1)} %get-tuple-element.20, bf16[384,640]{1,0:T(8,128)(2,1)} %get-tuple-element.21, ...), kind=kOutput, calls=%fused_computation.1 | convolution fusion | flops 513146880 | bytes 4784128 | tf_op jit(solution)/shard_map/dot_general | solution.py:156
  206.7 6.0 %all-to-all-done = bf16[4,256,384]{1,2,0:T(8,128)(2,1)S(1)} async-done(((bf16[4,256,384]{1,2,0:T(8,128)(2,1)}), bf16[4,256,384]{1,2,0:T(8,128)(2,1)S(1)}, u32[]{:S(2)}, u32[]{:S(2)}) %all-to-all-start) | async-done | bytes 786464 | tf_op jit(solution)/shard_map/all_to_all | solution.py:24
  212.7 15.9 %all-to-all-start.6 = ((bf16[8,2,16,2560]{3,2,1,0:T(8,128)(2,1)}), bf16[8,2,16,2560]{3,2,1,0:T(8,128)(2,1)S(1)}, u32[]{:S(2)}, u32[]{:S(2)}) async-start(bf16[8,2,16,2560]{3,2,1,0:T(8,128)(2,1)} %bitcast.134), calls=%async_computation.6 | async-start | bytes 2621440 | tf_op jit(solution)/shard_map/all_to_all | solution.py:24
  230.0 28.2 %all-to-all-done.6.outs = bf16[8,2,16,2560]{3,2,1,0:T(8,128)(2,1)S(1)} async-done(((bf16[8,2,16,2560]{3,2,1,0:T(8,128)(2,1)}), bf16[8,2,16,2560]{3,2,1,0:T(8,128)(2,1)S(1)}, u32[]{:S(2)}, u32[]{:S(2)}) %all-to-all-start.6) | async-done | bytes 1310752 | tf_op jit(solution)/shard_map/all_to_all | solution.py:24
  259.2 3.5 %all-to-all-start.3 = ((bf16[4,256,640]{2,1,0:T(8,128)(2,1)}), bf16[4,256,640]{2,1,0:T(8,128)(2,1)S(1)}, u32[]{:S(2)}, u32[]{:S(2)}) async-start(bf16[4,256,640]{2,1,0:T(8,128)(2,1)} %pad_maximum_fusion.3), calls=%async_computation.3 | async-start | bytes 2621440 | tf_op jit(solution)/shard_map/all_to_all | solution.py:24
  264.1 2.3 fusion.3
  268.0 3.7 %gram.1 = f32[64,8,128]{2,1,0:T(8,128)} custom-call(bf16[2,8,16,2560]{3,2,1,0:T(8,128)(2,1)} %bitcast.118, bf16[8,2,16,2560]{3,2,1,0:T(8,128)(2,1)} %copy-done.2), custom_call_target="tpu_custom_call" | custom-call | tf_op jit(solution)/shard_map/gram/pallas_call | solution.py:90
  273.3 4.9 %all-to-all-done.3 = bf16[4,256,640]{2,1,0:T(8,128)(2,1)S(1)} async-done(((bf16[4,256,640]{2,1,0:T(8,128)(2,1)}), bf16[4,256,640]{2,1,0:T(8,128)(2,1)S(1)}, u32[]{:S(2)}, u32[]{:S(2)}) %all-to-all-start.3) | async-done | bytes 1310752 | tf_op jit(solution)/shard_map/all_to_all | solution.py:24
  278.7 11.7 %all-to-all-start.7 = ((f32[64,1,8]{2,1,0:T(1,128)}), f32[64,1,8]{2,1,0:T(1,128)S(1)}, u32[]{:S(2)}, u32[]{:S(2)}) async-start(f32[64,1,8]{2,1,0:T(1,128)} %bitcast.65), calls=%async_computation.7 | async-start | bytes 65536 | tf_op jit(solution)/shard_map/all_to_all | solution.py:24
  292.0 12.6 %all-to-all-done.7 = f32[64,1,8]{2,1,0:T(1,128)S(1)} async-done(((f32[64,1,8]{2,1,0:T(1,128)}), f32[64,1,8]{2,1,0:T(1,128)S(1)}, u32[]{:S(2)}, u32[]{:S(2)}) %all-to-all-start.7) | async-done | bytes 2080 | tf_op jit(solution)/shard_map/all_to_all | solution.py:24
  (95 shorter events, 32.8 us)
Async XLA Ops:
  3.5 26.3 %copy-start.10 = (f32[1,8]{1,0:T(1,128)S(1)}, f32[1,8]{1,0:T(1,128)}, u32[]{:S(2)}) copy-start(f32[1,8]{1,0:T(1,128)} %param.13) | copy-start | bytes 100
  3.5 36.4 %copy-start.1 = (bf16[1,128,5120]{2,1,0:T(8,128)(2,1)S(1)}, bf16[1,128,5120]{2,1,0:T(8,128)(2,1)}, u32[]{:S(2)}) copy-start(bf16[1,128,5120]{2,1,0:T(8,128)(2,1)} %param.7) | copy-start | bytes 3932164
  3.5 87.8 %all-to-all-start.1 = ((bf16[16,16,2560]{2,1,0:T(8,128)(2,1)}), bf16[16,16,2560]{2,1,0:T(8,128)(2,1)S(1)}, u32[]{:S(2)}, u32[]{:S(2)}) async-start(bf16[16,16,2560]{2,1,0:T(8,128)(2,1)} %bitcast.122), calls=%async_computation.1 | async-start | bytes 2621440 | tf_op jit(solution)/shard_map/all_to_all | solution.py:24
  18.4 92.2 %collective-permute-start.6 = (bf16[384,640]{1,0:T(8,128)(2,1)}, bf16[384,640]{1,0:T(8,128)(2,1)}, u32[]{:S(2)}, u32[]{:S(2)}) collective-permute-start(bf16[384,640]{1,0:T(8,128)(2,1)} %bitcast.53), channel_id=1, source_target_pairs={{0,2},{2,4},{4,6},{6,0},{1,3},{3,5},{5,7},{7,1},{8,10},{10,12},{12... | collective-permute-start | bytes 1474568 | tf_op jit(solution)/shard_map/ppermute | solution.py:33
  21.8 88.8 %collective-permute-start.7 = (bf16[384,640]{1,0:T(8,128)(2,1)}, bf16[384,640]{1,0:T(8,128)(2,1)}, u32[]{:S(2)}, u32[]{:S(2)}) collective-permute-start(bf16[384,640]{1,0:T(8,128)(2,1)} %bitcast.53), channel_id=1, source_target_pairs={{0,4},{2,6},{4,0},{6,2},{1,5},{3,7},{5,1},{7,3},{8,12},{10,14},{12... | collective-permute-start | bytes 1474568 | tf_op jit(solution)/shard_map/ppermute | solution.py:33
  26.4 84.2 %collective-permute-start.8 = (bf16[384,640]{1,0:T(8,128)(2,1)}, bf16[384,640]{1,0:T(8,128)(2,1)}, u32[]{:S(2)}, u32[]{:S(2)}) collective-permute-start(bf16[384,640]{1,0:T(8,128)(2,1)} %bitcast.53), channel_id=1, source_target_pairs={{0,6},{2,0},{4,2},{6,4},{1,7},{3,1},{5,3},{7,5},{8,14},{10,8},{12,... | collective-permute-start | bytes 1474568 | tf_op jit(solution)/shard_map/ppermute | solution.py:33
  29.8 34.1 %collective-permute-start.1 = (f32[8]{0:T(128)S(1)}, f32[8]{0:T(128)S(1)}, u32[]{:S(2)}, u32[]{:S(2)}) collective-permute-start(f32[8]{0:T(128)S(1)} %bitcast.143), channel_id=1, source_target_pairs={{0,64},{64,0},{1,65},{65,1},{2,66},{66,2},{3,67},{67,3},{4,68},{68... | collective-permute-start | bytes 104 | tf_op jit(solution)/shard_map/ppermute | solution.py:28
  40.8 42.7 %copy-start.8 = (bf16[1,128,384]{2,1,0:T(8,128)(2,1)S(1)}, bf16[1,128,384]{2,1,0:T(8,128)(2,1)}, u32[]{:S(2)}) copy-start(bf16[1,128,384]{2,1,0:T(8,128)(2,1)} %param.8) | copy-start | bytes 294916
  40.8 49.7 %copy-start.11 = (pred[8]{0:T(512)(128)(4,1)S(1)}, pred[8]{0:T(512)(128)(4,1)}, u32[]{:S(2)}) copy-start(pred[8]{0:T(512)(128)(4,1)} %broadcast_in_dim.114) | copy-start | bytes 28
  40.8 49.7 %copy-start.12 = (pred[8]{0:T(512)(128)(4,1)S(1)}, pred[8]{0:T(512)(128)(4,1)}, u32[]{:S(2)}) copy-start(pred[8]{0:T(512)(128)(4,1)} %broadcast_in_dim.119) | copy-start | bytes 28
  40.8 49.7 %copy-start.13 = (pred[8]{0:T(512)(128)(4,1)S(1)}, pred[8]{0:T(512)(128)(4,1)}, u32[]{:S(2)}) copy-start(pred[8]{0:T(512)(128)(4,1)} %broadcast_in_dim.124) | copy-start | bytes 28
  63.9 12.4 %collective-permute-start.2 = (f32[2,8]{1,0:T(2,128)S(1)}, f32[2,8]{1,0:T(2,128)S(1)}, u32[]{:S(2)}, u32[]{:S(2)}) collective-permute-start(f32[2,8]{1,0:T(2,128)S(1)} %pad_maximum_fusion.10), channel_id=1, source_target_pairs={{0,384},{128,0},{256,128},{384,256},{1,385},{129,1},{257,129},{385... | collective-permute-start | bytes 200 | tf_op jit(solution)/shard_map/ppermute | solution.py:33
  74.3 6.4 %collective-permute-start.3 = (f32[2,8]{1,0:T(2,128)S(1)}, f32[2,8]{1,0:T(2,128)S(1)}, u32[]{:S(2)}, u32[]{:S(2)}) collective-permute-start(f32[2,8]{1,0:T(2,128)S(1)} %pad_maximum_fusion.10), channel_id=1, source_target_pairs={{0,256},{128,384},{256,0},{384,128},{1,257},{129,385},{257,1},{385... | collective-permute-start | bytes 200 | tf_op jit(solution)/shard_map/ppermute | solution.py:33
  76.3 7.3 %collective-permute-start.4 = (f32[2,8]{1,0:T(2,128)S(1)}, f32[2,8]{1,0:T(2,128)S(1)}, u32[]{:S(2)}, u32[]{:S(2)}) collective-permute-start(f32[2,8]{1,0:T(2,128)S(1)} %pad_maximum_fusion.10), channel_id=1, source_target_pairs={{0,128},{128,256},{256,384},{384,0},{1,129},{129,257},{257,385},{3... | collective-permute-start | bytes 200 | tf_op jit(solution)/shard_map/ppermute | solution.py:33
  80.7 22.3 %collective-permute-start.10 = (f32[128]{0:T(128)}, f32[128]{0:T(128)S(1)}, u32[]{:S(2)}, u32[]{:S(2)}) collective-permute-start(f32[128]{0:T(128)} %add_rsqrt_fusion), channel_id=1, source_target_pairs={{0,1},{1,0},{2,3},{3,2},{4,5},{5,4},{6,7},{7,6},{8,9},{9,8},{10,11... | collective-permute-start | bytes 1544 | tf_op jit(solution)/shard_map/ppermute | solution.py:28
  83.5 90.4 %collective-permute-start = (bf16[128,384]{1,0:T(8,128)(2,1)S(1)}, bf16[128,384]{1,0:T(8,128)(2,1)S(1)}, u32[]{:S(2)}, u32[]{:S(2)}) collective-permute-start(bf16[128,384]{1,0:T(8,128)(2,1)S(1)} %bitcast.135), channel_id=1, source_target_pairs={{0,1},{1,0},{2,3},{3,2},{4,5},{5,4},{6,7},{7,6},{8,9},{9,8},{10,11... | collective-permute-start | bytes 294920 | tf_op jit(solution)/shard_map/ppermute | solution.py:28
  91.2 1.1 copy-start
  96.3 6.5 %copy-start.3 = (bf16[128,640]{1,0:T(8,128)(2,1)S(1)}, bf16[128,640]{1,0:T(8,128)(2,1)}, u32[]{:S(2)}) copy-start(bf16[128,640]{1,0:T(8,128)(2,1)} %get-tuple-element.31) | copy-start | bytes 491524
  96.3 6.5 %copy-start.4 = (bf16[128,640]{1,0:T(8,128)(2,1)S(1)}, bf16[128,640]{1,0:T(8,128)(2,1)}, u32[]{:S(2)}) copy-start(bf16[128,640]{1,0:T(8,128)(2,1)} %get-tuple-element.32) | copy-start | bytes 491524
  96.3 6.5 %copy-start.5 = (bf16[128,640]{1,0:T(8,128)(2,1)S(1)}, bf16[128,640]{1,0:T(8,128)(2,1)}, u32[]{:S(2)}) copy-start(bf16[128,640]{1,0:T(8,128)(2,1)} %get-tuple-element.33) | copy-start | bytes 491524
  96.3 64.7 %all-to-all-start.2 = ((bf16[8,2,16,2560]{3,2,1,0:T(8,128)(2,1)}), bf16[8,2,16,2560]{3,2,1,0:T(8,128)(2,1)S(1)}, u32[]{:S(2)}, u32[]{:S(2)}) async-start(bf16[8,2,16,2560]{3,2,1,0:T(8,128)(2,1)} %mix.1), calls=%async_computation.2 | async-start | bytes 2621440 | tf_op jit(solution)/shard_map/all_to_all | solution.py:24
  103.0 55.1 %collective-permute-start.5 = (bf16[128,2560]{1,0:T(8,128)(2,1)S(1)}, bf16[128,2560]{1,0:T(8,128)(2,1)}, u32[]{:S(2)}, u32[]{:S(2)}) collective-permute-start(bf16[128,2560]{1,0:T(8,128)(2,1)S(1)} %maximum_select_fusion.1), channel_id=1, source_target_pairs={{0,1},{1,0},{2,3},{3,2},{4,5},{5,4},{6,7},{7,6},{8,9},{9,8},{10,11... | collective-permute-start | bytes 1966088 | tf_op jit(solution)/shard_map/ppermute | solution.py:28
  161.1 4.5 %copy-start.7 = (bf16[384,640]{1,0:T(8,128)(2,1)S(1)}, bf16[384,640]{1,0:T(8,128)(2,1)}, u32[]{:S(2)}) copy-start(bf16[384,640]{1,0:T(8,128)(2,1)} %get-tuple-element.18) | copy-start | bytes 1474564
  161.1 21.4 %all-to-all-start.4 = ((bf16[4,256,640]{2,1,0:T(8,128)(2,1)}), bf16[4,256,640]{2,1,0:T(8,128)(2,1)}, u32[]{:S(2)}, u32[]{:S(2)}) async-start(bf16[4,256,640]{2,1,0:T(8,128)(2,1)} %pad_maximum_fusion.5), calls=%async_computation.4 | async-start | bytes 2621440 | tf_op jit(solution)/shard_map/all_to_all | solution.py:24
  167.7 13.6 %collective-permute-start.9 = (bf16[256,384]{1,0:T(8,128)(2,1)S(1)}, bf16[256,384]{1,0:T(8,128)(2,1)S(1)}, u32[]{:S(2)}, u32[]{:S(2)}) collective-permute-start(bf16[256,384]{1,0:T(8,128)(2,1)S(1)} %get-tuple-element.56), channel_id=1, source_target_pairs={{0,1},{1,0},{2,3},{3,2},{4,5},{5,4},{6,7},{7,6},{8,9},{9,8},{10,11... | collective-permute-start | bytes 589832 | tf_op jit(solution)/shard_map/ppermute | solution.py:28
  183.4 14.3 %all-to-all-start.5 = ((bf16[4,256,384]{1,2,0:T(8,128)(2,1)}), bf16[4,256,384]{1,2,0:T(8,128)(2,1)S(1)}, u32[]{:S(2)}, u32[]{:S(2)}) async-start(bf16[4,256,384]{1,2,0:T(8,128)(2,1)} %broadcast_in_dim.130), calls=%async_computation.5 | async-start | bytes 1572864 | tf_op jit(solution)/shard_map/all_to_all | solution.py:24
  197.7 2.1 copy-start.6
  199.7 13.0 %all-to-all-start = ((bf16[4,256,384]{1,2,0:T(8,128)(2,1)}), bf16[4,256,384]{1,2,0:T(8,128)(2,1)S(1)}, u32[]{:S(2)}, u32[]{:S(2)}) async-start(bf16[4,256,384]{1,2,0:T(8,128)(2,1)} %broadcast_in_dim.107), calls=%async_computation | async-start | bytes 1572864 | tf_op jit(solution)/shard_map/all_to_all | solution.py:24
  212.7 45.4 %all-to-all-start.6 = ((bf16[8,2,16,2560]{3,2,1,0:T(8,128)(2,1)}), bf16[8,2,16,2560]{3,2,1,0:T(8,128)(2,1)S(1)}, u32[]{:S(2)}, u32[]{:S(2)}) async-start(bf16[8,2,16,2560]{3,2,1,0:T(8,128)(2,1)} %bitcast.134), calls=%async_computation.6 | async-start | bytes 2621440 | tf_op jit(solution)/shard_map/all_to_all | solution.py:24
  230.0 34.1 %copy-start.9 = (bf16[1,640]{1,0:T(2,128)(2,1)S(1)}, bf16[1,640]{1,0:T(2,128)(2,1)}, u32[]{:S(2)}) copy-start(bf16[1,640]{1,0:T(2,128)(2,1)} %param.12) | copy-start | bytes 3844
  259.2 18.9 %all-to-all-start.3 = ((bf16[4,256,640]{2,1,0:T(8,128)(2,1)}), bf16[4,256,640]{2,1,0:T(8,128)(2,1)S(1)}, u32[]{:S(2)}, u32[]{:S(2)}) async-start(bf16[4,256,640]{2,1,0:T(8,128)(2,1)} %pad_maximum_fusion.3), calls=%async_computation.3 | async-start | bytes 2621440 | tf_op jit(solution)/shard_map/all_to_all | solution.py:24
  278.7 25.9 %all-to-all-start.7 = ((f32[64,1,8]{2,1,0:T(1,128)}), f32[64,1,8]{2,1,0:T(1,128)S(1)}, u32[]{:S(2)}, u32[]{:S(2)}) async-start(f32[64,1,8]{2,1,0:T(1,128)} %bitcast.65), calls=%async_computation.7 | async-start | bytes 65536 | tf_op jit(solution)/shard_map/all_to_all | solution.py:24
  (1 other events, 1.1 us)

commit v2 on v1

v2 whole, which is shorter than its diff:
```python
import jax
import jax.numpy as jnp
from jax import lax
from jax.experimental import pallas as pl
from jax.experimental.pallas import tpu as pltpu
from jax.sharding import Mesh, PartitionSpec as P

MIXES = 8
LANES = 128
BLOCK = 640
TERMS = 3
epsilon = 1e-06
root_coef = 0.7978845608028654
GROUP = ("zl", "yh")
SMEM = pl.BlockSpec(memory_space=pltpu.SMEM)


def gelu_pair(values):
    tangent = jnp.tanh(root_coef * (values + 0.044715 * values * values * values))
    result = 0.5 * values * (1.0 + tangent)
    slopes = 0.5 * (1.0 + tangent) + 0.5 * values * (1.0 - tangent * tangent) * root_coef * (
        1.0 + 3.0 * 0.044715 * values * values
    )
    return (result, slopes)


def exchange(pieces, axes):
    return lax.all_to_all(pieces, axes, split_axis=0, concat_axis=0, tiled=True)


def swapped(value, axis):
    return lax.ppermute(value, axis, [(0, 1), (1, 0)])


def shifted(value, axis, steps):
    count = lax.axis_size(axis)
    return lax.ppermute(value, axis, [(i, (i + steps) % count) for i in range(count)])


def split_terms(value):
    terms = []
    for _ in range(TERMS):
        term = value.astype(jnp.bfloat16).astype(jnp.float32)
        terms.append(term)
        value = value - term
    return terms


def shape(dims, dtype=jnp.bfloat16):
    return jax.ShapeDtypeStruct(dims, dtype)


def pack_grads_body(weights, grads, out):
    halves, sections, rows, cols = out.shape
    block = BLOCK
    for half in range(halves):
        for i in range((cols - LANES) // block):
            piece = grads[:, (i * halves + half) * block : (i * halves + half + 1) * block]
            out[half, :, :, i * block : (i + 1) * block] = piece.reshape(sections, rows, block)
    lane = lax.broadcasted_iota(jnp.int32, (rows, LANES), 1)
    row = lax.broadcasted_iota(jnp.int32, (rows, LANES), 0)
    value = jnp.zeros((rows, LANES), jnp.float32)
    for m in range(MIXES):
        value = jnp.where(lane == m, weights[0, m], value)
    tail = jnp.zeros((rows, LANES), jnp.float32)
    for i, term in enumerate(split_terms(value)):
        tail = jnp.where(row == i, term, tail)
    tail = tail.astype(jnp.bfloat16)
    for half in range(halves):
        for k in range(sections):
            out[half, k, :, cols - LANES :] = tail


def pack_inputs_body(place, layer_in, latent, kept, sent):
    tokens, cols = kept.shape
    ranks = latent.shape[1]
    half_cols = cols - ranks - LANES
    width = layer_in.shape[1]
    block = BLOCK
    first = place[0] == 0
    squares = jnp.zeros((tokens, LANES), jnp.float32)
    for at in range(0, width, LANES):
        tile = layer_in[:, at : at + LANES].astype(jnp.float32)
        squares = squares + tile * tile
    inv_rms = lax.rsqrt(jnp.sum(squares, axis=1, keepdims=True) / width + epsilon)
    lane = lax.broadcasted_iota(jnp.int32, (tokens, LANES), 1)
    tail = jnp.zeros((tokens, LANES), jnp.float32)
    for i, term in enumerate(split_terms(jnp.broadcast_to(inv_rms, (tokens, LANES)))):
        tail = jnp.where(lane == i, term, tail)
    tail = tail.astype(jnp.bfloat16)
    for i in range(half_cols // block):
        low = layer_in[:, 2 * i * block : (2 * i + 1) * block]
        high = layer_in[:, (2 * i + 1) * block : (2 * i + 2) * block]
        kept[:, i * block : (i + 1) * block] = jnp.where(first, low, high)
        sent[:, i * block : (i + 1) * block] = jnp.where(first, high, low)
    for out in (kept, sent):
        out[:, half_cols : half_cols + ranks] = latent[...]
        out[:, half_cols + ranks :] = tail


def lift_body(place, kept, other, kept_rest, other_rest, up_0, up_1, up_2, up_3, sends, moves, up_half, scale, act):
    sections, _, halves, rows, block = sends.shape
    ranks = up_0.shape[0]
    at = pl.program_id(0)
    first = place[0] == 0

    def in_order(own, far, half):
        return jnp.where(first, own, far) if half == 0 else jnp.where(first, far, own)

    @pl.when(at == 0)
    def _():
        for half in range(halves):
            rest = in_order(kept_rest[...], other_rest[...], half).astype(jnp.float32)
            values, slopes = gelu_pair(rest[:, :, :ranks])
            inv_rms = jnp.sum(rest[:, :, ranks : ranks + LANES], axis=2, keepdims=True)
            act[:, half] = values.astype(jnp.bfloat16)
            scale[:, half] = slopes * inv_rms

    turn = lax.rem(place[1] - at + 4, 4)
    up = jnp.where(turn == 0, up_0[...], jnp.where(turn == 1, up_1[...], jnp.where(turn == 2, up_2[...], up_3[...])))
    up_half[...] = up
    for half in range(halves):
        rows_in = in_order(kept[...], other[...], half)
        moves[0, :, half, :, :block] = rows_in
        moves[0, :, half, :, block:] = act[:, half]
        branch = jnp.dot(
            act[:, half].reshape(sections * rows, ranks), up, preferred_element_type=jnp.float32
        ).reshape(sections, rows, block)
        sends[:, 0, half] = (rows_in.astype(jnp.float32) + branch).astype(jnp.bfloat16)


def mix_body(coef, grads, sends, out):
    halves, sections, rows, cols = grads.shape
    for half in range(halves):
        for at in range(0, cols, LANES):
            lanes = slice(at, at + LANES)
            tiles = [grads[half, k, :, lanes].astype(jnp.float32) for k in range(sections)]
            for k in range(sections):
                total = coef[k, 0] * tiles[k]
                for m in range(1, sections - k):
                    total = total + coef[k, m] * tiles[k + m]
                out[k, 0, half, :, lanes] = total.astype(jnp.bfloat16)


def gram_body(grads, outs, result):
    halves, sections, rows, cols = grads.shape
    sums = {}
    for half in range(halves):
        for at in range(0, cols, LANES):
            lanes = slice(at, at + LANES)
            left = [outs[k, 0, half, :, lanes].astype(jnp.float32) for k in range(sections)]
            right = [grads[half, k, :, lanes].astype(jnp.float32) for k in range(sections)]
            for k in range(sections):
                for m in range(sections - k):
                    product = left[k] * right[k + m]
                    folded = product[:8] + product[8:]
                    sums[k, m] = folded if (k, m) not in sums else sums[k, m] + folded

    @pl.when(pl.program_id(0) == 0)
    def _():
        result[...] = jnp.zeros(result.shape, jnp.float32)

    for (k, m), total in sums.items():
        result[k * MIXES + m] += total


def act_grad_body(grads, up, moves, total, rounded):
    sections, _, halves, rows, block = grads.shape
    at = pl.program_id(0)
    piece = grads[...].reshape(sections * halves * rows, block)
    moves[0] = piece
    part = lax.dot_general(piece, up[...], (((1,), (1,)), ((), ())), preferred_element_type=jnp.float32)

    @pl.when(at == 0)
    def _():
        total[...] = part

    @pl.when(at != 0)
    def _():
        total[...] += part

    @pl.when(at == pl.num_programs(0) - 1)
    def _():
        rounded[...] = total[...].astype(jnp.bfloat16)


def up_grad_body(place, grads, act_0, act_1, act_2, act_3, out):
    total = jnp.zeros(out.shape, jnp.float32)
    for step, act in enumerate((act_0, act_1, act_2, act_3)):
        source = lax.rem(place[1] - step + 4, 4)
        total = total + lax.dot_general(
            act[:, grads.shape[2] :], grads[source], (((0,), (0,)), ((), ())), preferred_element_type=jnp.float32
        )
    out[...] = total.astype(jnp.bfloat16)


def down_grad_body(in_0, in_1, in_2, in_3, lat_0, lat_1, lat_2, lat_3, gain, down, out, gain_out):
    total = jnp.zeros(out.shape, jnp.float32)
    for inputs, latents in ((in_0, lat_0), (in_1, lat_1), (in_2, lat_2), (in_3, lat_3)):
        total = total + lax.dot_general(
            inputs[...], latents[...], (((0,), (0,)), ((), ())), preferred_element_type=jnp.float32
        )
    gain_cols = jnp.transpose(jnp.broadcast_to(gain[...].astype(jnp.float32), (8, gain.shape[1])))
    out[...] = (total * gain_cols[:, :1]).astype(jnp.bfloat16)
    product = total * down[...].astype(jnp.float32)
    ones = jnp.ones((8, product.shape[1]), jnp.float32)
    sums = lax.dot_general(
        ones, product, (((1,), (1,)), ((), ())), precision=lax.Precision.HIGHEST, preferred_element_type=jnp.float32
    )
    gain_out[...] = sums[:1]


def local(layer_in, latent, mix_grad, down_proj, up_proj, norm_gain, mix_weight):
    layer_in, latent, mix_grad = (layer_in[0], latent[0], mix_grad[0])
    tokens, width = layer_in.shape
    ranks = latent.shape[1]
    xs, zs = (lax.axis_size("x"), lax.axis_size("zh"))
    sections = lax.axis_size("zl") * lax.axis_size("yh")
    block = width // (xs * zs)
    half_width = xs * block
    rows = tokens // sections
    place = jnp.stack([lax.axis_index("zh"), lax.axis_index("x")]).astype(jnp.int32)

    packed = pl.pallas_call(
        pack_grads_body,
        in_specs=[SMEM, pl.BlockSpec((tokens, width), lambda: (0, 0))],
        out_specs=pl.BlockSpec((zs, sections, rows, half_width + LANES), lambda: (0, 0, 0, 0)),
        out_shape=shape((zs, sections, rows, half_width + LANES)),
        name="pack_grads",
    )(mix_weight, mix_grad)
    grads = exchange(packed.reshape(zs * sections, rows, half_width + LANES), ("zh", *GROUP))
    grads = grads.reshape(zs, sections, rows, half_width + LANES)

    full = half_width + ranks + LANES
    kept, sent = pl.pallas_call(
        pack_inputs_body,
        in_specs=[SMEM, pl.BlockSpec((tokens, width), lambda: (0, 0)), pl.BlockSpec((tokens, ranks), lambda: (0, 0))],
        out_specs=[pl.BlockSpec((tokens, full), lambda: (0, 0))] * 2,
        out_shape=[shape((tokens, full))] * 2,
        name="pack_inputs",
    )(place, layer_in, latent)
    other = swapped(sent, "zh")

    up_block = up_proj[0]
    ups = [up_block] + [shifted(up_block, "x", step) for step in range(1, xs)]

    kept, other = [t.reshape(sections, rows, full) for t in (kept, other)]
    wide = pl.BlockSpec((sections, rows, block), lambda a: (0, 0, a))
    rest = ranks + LANES
    narrow = pl.BlockSpec((sections, rows, rest), lambda a: (0, 0, half_width // rest))
    whole_up = pl.BlockSpec((ranks, block), lambda a: (0, 0))
    sends, moves, up_half, scale = pl.pallas_call(
        lift_body,
        grid=(xs,),
        in_specs=[SMEM, wide, wide, narrow, narrow] + [whole_up] * xs,
        out_specs=[
            pl.BlockSpec((sections, 1, zs, rows, block), lambda a: (0, 1, 0, 0, a)),
            pl.BlockSpec((1, sections, zs, rows, block + ranks), lambda a: (a, 0, 0, 0, 0)),
            pl.BlockSpec((ranks, block), lambda a: (0, a)),
            pl.BlockSpec((sections, zs, rows, ranks), lambda a: (0, 0, 0, 0)),
        ],
        out_shape=[
            shape((sections, 2, zs, rows, half_width)),
            shape((xs, sections, zs, rows, block + ranks)),
            shape((ranks, half_width)),
            shape((sections, zs, rows, ranks), jnp.float32),
        ],
        scratch_shapes=[pltpu.VMEM((sections, zs, rows, ranks), jnp.bfloat16)],
        name="lift",
    )(place, kept, other, kept, other, *ups)
    scale = scale.reshape(zs * tokens, ranks)

    weights = jnp.sum(grads[0, :, :TERMS, half_width : half_width + MIXES].astype(jnp.float32), axis=1)
    grads_spec = pl.BlockSpec((zs, sections, rows, block), lambda a: (0, 0, 0, a))
    sends = pl.pallas_call(
        mix_body,
        grid=(xs,),
        in_specs=[SMEM, grads_spec, pl.BlockSpec(memory_space=pl.ANY)],
        out_specs=pl.BlockSpec((sections, 1, zs, rows, block), lambda a: (0, 0, 0, 0, a)),
        out_shape=shape(sends.shape),
        input_output_aliases={2: 0},
        name="mix",
    )(weights, grads, sends)
    arrived = exchange(sends, GROUP)

    moves = moves.reshape(xs, zs * tokens, block + ranks)
    at_x = place[1]
    moved = [lax.dynamic_index_in_dim(moves, at_x, 0, False)]
    for step in range(1, xs):
        moved.append(shifted(lax.dynamic_index_in_dim(moves, (at_x + step) % xs, 0, False), "x", step))

    arrived, *moved = lax.optimization_barrier((arrived, *moved))
    by_x, act_partial, act_rounded = pl.pallas_call(
        act_grad_body,
        grid=(xs,),
        in_specs=[
            pl.BlockSpec((sections, 1, zs, rows, block), lambda a: (0, 0, 0, 0, a)),
            pl.BlockSpec((ranks, block), lambda a: (0, a)),
        ],
        out_specs=[
            pl.BlockSpec((1, zs * tokens, block), lambda a: (a, 0, 0)),
            pl.BlockSpec((zs * tokens, ranks), lambda a: (0, 0)),
            pl.BlockSpec((zs * tokens, ranks), lambda a: (0, 0)),
        ],
        out_shape=[
            shape((xs, zs * tokens, block)),
            shape((zs * tokens, ranks), jnp.float32),
            shape((zs * tokens, ranks)),
        ],
        name="act_grad",
    )(arrived, up_half)
    act_other = swapped(act_rounded, "zh").astype(jnp.float32)
    all_grads = exchange(by_x, "x")
    scaled_grad = ((act_partial + act_other) * scale).astype(jnp.bfloat16)
    latent_grads = [scaled_grad] + [shifted(scaled_grad, "x", step) for step in range(1, xs)]

    gram_grads, _ = lax.optimization_barrier((grads, act_rounded))
    products = pl.pallas_call(
        gram_body,
        grid=(xs,),
        in_specs=[grads_spec, pl.BlockSpec((sections, 1, zs, rows, block), lambda a: (0, 1, 0, 0, a))],
        out_specs=pl.BlockSpec((sections * MIXES, 8, LANES), lambda a: (0, 0, 0)),
        out_shape=shape((sections * MIXES, 8, LANES), jnp.float32),
        name="gram",
    )(gram_grads, arrived)
    products = jnp.sum(products, axis=(1, 2)).reshape(sections, MIXES)
    spread = jnp.broadcast_to(products[:, None], (sections, xs * zs, MIXES))
    spread, all_grads = lax.optimization_barrier((spread, all_grads))
    mixing = exchange(spread.reshape(sections * xs * zs, MIXES), (*GROUP, "x", "zh")).sum(axis=0)

    up_grad = pl.pallas_call(
        up_grad_body,
        in_specs=[SMEM, pl.BlockSpec((xs, zs * tokens, block), lambda: (0, 0, 0))]
        + [pl.BlockSpec((zs * tokens, block + ranks), lambda: (0, 0))] * xs,
        out_specs=pl.BlockSpec((ranks, block), lambda: (0, 0)),
        out_shape=shape((ranks, block)),
        name="up_grad",
    )(place, all_grads, *moved)

    down_grad, gain_grad = pl.pallas_call(
        down_grad_body,
        grid=(1,),
        in_specs=[pl.BlockSpec((zs * tokens, block), lambda a: (0, 0))] * xs
        + [pl.BlockSpec((zs * tokens, ranks), lambda a: (0, 0))] * xs
        + [pl.BlockSpec((1, block), lambda a: (0, 0)), pl.BlockSpec((block, ranks), lambda a: (0, 0))],
        out_specs=[pl.BlockSpec((block, ranks), lambda a: (0, 0)), pl.BlockSpec((1, block), lambda a: (0, 0))],
        out_shape=[shape((block, ranks)), shape((1, block), jnp.float32)],
        name="down_grad",
    )(*moved, *latent_grads, norm_gain, down_proj[0])
    return (up_grad[None], down_grad[None], gain_grad, mixing[None])


def solution(mesh):
    devices = mesh.devices.reshape(4, 2, 8, 4, 2)
    fine = Mesh(devices, ("zl", "yh", "r", "x", "zh"))
    section, dp = (("zl", "yh", "r"), ("x", "zh"))
    return jax.shard_map(
        local,
        mesh=fine,
        in_specs=(
            P(section, dp, None),
            P(section, dp, None),
            P(section, dp, None),
            P(section, dp, None),
            P(section, None, dp),
            P(section, dp),
            P(section, None),
        ),
        out_specs=(
            P(section, None, dp),
            P(section, dp, None),
            P(section, dp),
            P(section, None),
        ),
        check_vma=False,
    )
```

time: 307 us -> 250 us (0.81)
  the two profiles are of different devices: /device:TPU:8 before, /device:TPU:16 now
where the time goes in v2:
time: 250 us; the launch traced here: 249 us
  waiting for transfers between devices  106 us (42%)
  starting transfers between devices  98.6 us (39%)
  Pallas kernels  31.9 us (13%)
  local copies, waits for them, and re-layouts  7.79 us (3%)
  other arithmetic  3.44 us (1%)
    all_to_all x4, starting transfers between devices, exchange(): return lax.all_to_all(pieces, axes, split_axis=0, concat_axis=0, tiled=True)  50.8 us
    all_to_all x4, waiting for transfers between devices, exchange(): return lax.all_to_all(pieces, axes, split_axis=0, concat_axis=0, tiled=True)  45.5 us
    ppermute x9, waiting for transfers between devices, shifted(): lax.ppermute(value, axis, [(i, (i + steps) % count) for i in range(count)])  33.9 us
    ppermute x9, starting transfers between devices, shifted(): lax.ppermute(value, axis, [(i, (i + steps) % count) for i in range(count)])  33.7 us
    ppermute x2, waiting for transfers between devices, swapped(): return lax.ppermute(value, axis, [(0, 1), (1, 0)])  26.9 us
    ppermute x2, starting transfers between devices, swapped(): return lax.ppermute(value, axis, [(0, 1), (1, 0)])  14 us
    pallas_call x1, Pallas kernels, local(): pl.pallas_call(lift_body, grid=(xs,), in_specs=[SMEM, wide, wide, narrow,...  6.41 us
  transfers between devices with their start and end apart: 15, of which 10 were waited for; matrix products, arithmetic and copies ran while one was open for 2% of the time, Pallas kernels for 8%

profile of v2, /device:TPU:16, one launch (start us, length us, event | category | flops | bytes accessed | tf_op | source)
XLA Modules:
  0.0 249.0 jit_solution(13573441624239926075)
XLA Ops:
  0.6 2.6 %pack_grads.1 = bf16[2,8,16,2688]{3,2,1,0:T(8,128)(2,1)} custom-call(f32[1,8]{1,0:T(1,128)} %weights.1, bf16[128,5120]{1,0:T(8,128)(2,1)} %bitcast.37), custom_call_target="tpu_custom_call" | custom-call | tf_op jit(solution)/shard_map/pack_grads/pallas_call | solution.py:224
  3.2 13.9 %all-to-all-start = ((bf16[16,16,2688]{2,1,0:T(8,128)(2,1)}), bf16[16,16,2688]{2,1,0:T(8,128)(2,1)S(1)}, u32[]{:S(2)}, u32[]{:S(2)}) async-start(bf16[16,16,2688]{2,1,0:T(8,128)(2,1)} %bitcast.31), calls=%async_computation | async-start | bytes 2752512 | tf_op jit(solution)/shard_map/all_to_all | solution.py:28
  17.7 2.9 %pack_inputs.1 = (bf16[128,3072]{1,0:T(8,128)(2,1)}, bf16[128,3072]{1,0:T(8,128)(2,1)}) custom-call(s32[2]{0:T(128)} %pad_add_fusion.place, bf16[128,5120]{1,0:T(8,128)(2,1)} %bitcast.38, bf16[128,384]{1,0:T(8,128)(2,1)} %bitcast.45), custom_call_target="tpu_custom_call" | custom-call | tf_op jit(solution)/shard_map/pack_inputs/pallas_call | solution.py:235
  20.6 7.7 %collective-permute-start = (bf16[128,3072]{1,0:T(8,128)(2,1)}, bf16[128,3072]{1,0:T(8,128)(2,1)S(1)}, u32[]{:S(2)}, u32[]{:S(2)}) collective-permute-start(bf16[128,3072]{1,0:T(8,128)(2,1)} %get-tuple-element.24), channel_id=1, source_target_pairs={{0,1},{1,0},{2,3},{3,2},{4,5},{5,4},{6,7},{7,6},{8,9},{9,8},{10,11... | collective-permute-start | bytes 2359304 | tf_op jit(solution)/shard_map/ppermute | solution.py:32
  28.4 3.4 %collective-permute-start.1 = (bf16[384,640]{1,0:T(8,128)(2,1)S(1)}, bf16[384,640]{1,0:T(8,128)(2,1)S(1)}, u32[]{:S(2)}, u32[]{:S(2)}) collective-permute-start(bf16[384,640]{1,0:T(8,128)(2,1)S(1)} %bitcast.42), channel_id=1, source_target_pairs={{0,2},{2,4},{4,6},{6,0},{1,3},{3,5},{5,7},{7,1},{8,10},{10,12},{12... | collective-permute-start | bytes 1474568 | tf_op jit(solution)/shard_map/ppermute | solution.py:37
  31.8 4.6 %collective-permute-start.2 = (bf16[384,640]{1,0:T(8,128)(2,1)S(1)}, bf16[384,640]{1,0:T(8,128)(2,1)S(1)}, u32[]{:S(2)}, u32[]{:S(2)}) collective-permute-start(bf16[384,640]{1,0:T(8,128)(2,1)S(1)} %bitcast.43), channel_id=1, source_target_pairs={{0,4},{2,6},{4,0},{6,2},{1,5},{3,7},{5,1},{7,3},{8,12},{10,14},{12... | collective-permute-start | bytes 1474568 | tf_op jit(solution)/shard_map/ppermute | solution.py:37
  36.4 3.3 %collective-permute-start.3 = (bf16[384,640]{1,0:T(8,128)(2,1)S(1)}, bf16[384,640]{1,0:T(8,128)(2,1)S(1)}, u32[]{:S(2)}, u32[]{:S(2)}) collective-permute-start(bf16[384,640]{1,0:T(8,128)(2,1)S(1)} %bitcast.44), channel_id=1, source_target_pairs={{0,6},{2,0},{4,2},{6,4},{1,7},{3,1},{5,3},{7,5},{8,14},{10,8},{12,... | collective-permute-start | bytes 1474568 | tf_op jit(solution)/shard_map/ppermute | solution.py:37
  39.8 4.8 %collective-permute-done.1.up_1 = bf16[384,640]{1,0:T(8,128)(2,1)S(1)} collective-permute-done((bf16[384,640]{1,0:T(8,128)(2,1)S(1)}, bf16[384,640]{1,0:T(8,128)(2,1)S(1)}, u32[]{:S(2)}, u32[]{:S(2)}) %collective-permute-start.1) | collective-permute-done | bytes 491552 | tf_op jit(solution)/shard_map/ppermute | solution.py:37
  44.6 10.5 %collective-permute-done.2.up_2 = bf16[384,640]{1,0:T(8,128)(2,1)S(1)} collective-permute-done((bf16[384,640]{1,0:T(8,128)(2,1)S(1)}, bf16[384,640]{1,0:T(8,128)(2,1)S(1)}, u32[]{:S(2)}, u32[]{:S(2)}) %collective-permute-start.2) | collective-permute-done | bytes 491552 | tf_op jit(solution)/shard_map/ppermute | solution.py:37
  56.7 16.9 %collective-permute-done = bf16[128,3072]{1,0:T(8,128)(2,1)S(1)} collective-permute-done((bf16[128,3072]{1,0:T(8,128)(2,1)}, bf16[128,3072]{1,0:T(8,128)(2,1)S(1)}, u32[]{:S(2)}, u32[]{:S(2)}) %collective-permute-start) | collective-permute-done | bytes 786464 | tf_op jit(solution)/shard_map/ppermute | solution.py:32
  74.5 6.4 %lift.1 = (bf16[8,2,2,16,2560]{4,3,2,1,0:T(8,128)(2,1)}, bf16[4,8,2,16,1024]{4,3,2,1,0:T(8,128)(2,1)}, bf16[384,2560]{1,0:T(8,128)(2,1)}, f32[8,2,16,384]{3,2,1,0:T(8,128)}) custom-call(s32[2]{0:T(128)} %pad_add_fusion.place, bf16[8,16,3072]{2,1,0:T(8,128)(2,1)} %bitcast.32, bf16[8,16,3072]{2,1,0:T(8,128)(2,1)} %bitcast.34, bf16[8,16,3072]{2,1,0:T(8,128)(2,1)} %bitcast.33, ...), custom_call_target="tpu_custom_call" | custom-call | tf_op jit(solution)/shard_map/lift/pallas_call | solution.py:252
  82.0 4.0 %mix.1 = bf16[8,2,2,16,2560]{4,3,2,1,0:T(8,128)(2,1)} custom-call(f32[8,8]{1,0:T(8,128)} %convert_reduce_fusion.coef, bf16[2,8,16,2688]{3,2,1,0:T(8,128)(2,1)} %bitcast.29, bf16[8,2,2,16,2560]{4,3,2,1,0:T(8,128)(2,1)} %get-tuple-element.25.sends), custom_call_target="tpu_custom_call", output_to_operand_aliasing={{}: (2, {})} | custom-call | tf_op jit(solution)/shard_map/mix/pallas_call | solution.py:275
  86.0 26.0 %all-to-all-start.1 = ((bf16[8,2,2,16,2560]{4,3,2,1,0:T(8,128)(2,1)}), bf16[8,2,2,16,2560]{4,3,2,1,0:T(8,128)(2,1)S(1)}, u32[]{:S(2)}, u32[]{:S(2)}) async-start(bf16[8,2,2,16,2560]{4,3,2,1,0:T(8,128)(2,1)} %mix.1), calls=%async_computation.1 | async-start | bytes 5242880 | tf_op jit(solution)/shard_map/all_to_all | solution.py:28
  112.0 2.6 %dynamic-slice_bitcast_fusion = (bf16[256,1024]{1,0:T(8,128)(2,1)S(1)}, bf16[256,1024]{1,0:T(8,128)(2,1)S(1)}, bf16[256,1024]{1,0:T(8,128)(2,1)S(1)}, bf16[256,1024]{1,0:T(8,128)(2,1)}) fusion(bf16[4,256,1024]{2,1,0:T(8,128)(2,1)} %bitcast.36, s32[]{:T(128)S(6)} %select_n.34, s32[]{:T(128)S(6)} %select_n.32, s32[]{:T(128)S(6)} %select_n.30, s32[]{:T(128)S(6)} %select_n.28), kind=kLoop, calls=%fused_computation | loop fusion | bytes 4194320 | tf_op jit(solution)/shard_map/jit(dynamic_index_in_dim)/squeeze | solution.py:290
  114.5 3.4 %collective-permute-start.4 = (bf16[256,1024]{1,0:T(8,128)(2,1)S(1)}, bf16[256,1024]{1,0:T(8,128)(2,1)S(1)}, u32[]{:S(2)}, u32[]{:S(2)}) collective-permute-start(bf16[256,1024]{1,0:T(8,128)(2,1)S(1)} %get-tuple-element.44), channel_id=1, source_target_pairs={{0,2},{2,4},{4,6},{6,0},{1,3},{3,5},{5,7},{7,1},{8,10},{10,12},{12... | collective-permute-start | bytes 1572872 | tf_op jit(solution)/shard_map/ppermute | solution.py:37
  117.9 4.6 %collective-permute-start.5 = (bf16[256,1024]{1,0:T(8,128)(2,1)S(1)}, bf16[256,1024]{1,0:T(8,128)(2,1)S(1)}, u32[]{:S(2)}, u32[]{:S(2)}) collective-permute-start(bf16[256,1024]{1,0:T(8,128)(2,1)S(1)} %get-tuple-element.43), channel_id=1, source_target_pairs={{0,4},{2,6},{4,0},{6,2},{1,5},{3,7},{5,1},{7,3},{8,12},{10,14},{12... | collective-permute-start | bytes 1572872 | tf_op jit(solution)/shard_map/ppermute | solution.py:37
  122.6 3.3 %collective-permute-start.6 = (bf16[256,1024]{1,0:T(8,128)(2,1)S(1)}, bf16[256,1024]{1,0:T(8,128)(2,1)}, u32[]{:S(2)}, u32[]{:S(2)}) collective-permute-start(bf16[256,1024]{1,0:T(8,128)(2,1)S(1)} %get-tuple-element.42), channel_id=1, source_target_pairs={{0,6},{2,0},{4,2},{6,4},{1,7},{3,1},{5,3},{7,5},{8,14},{10,8},{12,... | collective-permute-start | bytes 1572872 | tf_op jit(solution)/shard_map/ppermute | solution.py:37
  125.9 5.5 %collective-permute-done.4.act_1.in_1 = bf16[256,1024]{1,0:T(8,128)(2,1)S(1)} collective-permute-done((bf16[256,1024]{1,0:T(8,128)(2,1)S(1)}, bf16[256,1024]{1,0:T(8,128)(2,1)S(1)}, u32[]{:S(2)}, u32[]{:S(2)}) %collective-permute-start.4) | collective-permute-done | bytes 524320 | tf_op jit(solution)/shard_map/ppermute | solution.py:37
  131.4 10.6 %collective-permute-done.5.act_2.in_2 = bf16[256,1024]{1,0:T(8,128)(2,1)S(1)} collective-permute-done((bf16[256,1024]{1,0:T(8,128)(2,1)S(1)}, bf16[256,1024]{1,0:T(8,128)(2,1)S(1)}, u32[]{:S(2)}, u32[]{:S(2)}) %collective-permute-start.5) | collective-permute-done | bytes 524320 | tf_op jit(solution)/shard_map/ppermute | solution.py:37
  143.7 39.7 %all-to-all-done.1.grads.outs = bf16[8,2,2,16,2560]{4,3,2,1,0:T(8,128)(2,1)S(1)} async-done(((bf16[8,2,2,16,2560]{4,3,2,1,0:T(8,128)(2,1)}), bf16[8,2,2,16,2560]{4,3,2,1,0:T(8,128)(2,1)S(1)}, u32[]{:S(2)}, u32[]{:S(2)}) %all-to-all-start.1) | async-done | bytes 2621472 | tf_op jit(solution)/shard_map/all_to_all | solution.py:28
  184.9 4.8 %act_grad.1 = (bf16[4,256,640]{2,1,0:T(8,128)(2,1)}, f32[256,384]{1,0:T(8,128)}, bf16[256,384]{1,0:T(8,128)(2,1)}) custom-call(bf16[8,2,2,16,2560]{4,3,2,1,0:T(8,128)(2,1)} %copy-done, bf16[384,2560]{1,0:T(8,128)(2,1)} %get-tuple-element.28.up), custom_call_target="tpu_custom_call" | custom-call | tf_op jit(solution)/shard_map/act_grad/pallas_call | solution.py:293
  189.7 4.4 %all-to-all-start.2 = ((bf16[4,256,640]{2,1,0:T(8,128)(2,1)}), bf16[4,256,640]{2,1,0:T(8,128)(2,1)S(1)}, u32[]{:S(2)}, u32[]{:S(2)}) async-start(bf16[4,256,640]{2,1,0:T(8,128)(2,1)} %get-tuple-element.31), calls=%async_computation.2 | async-start | bytes 2621440 | tf_op jit(solution)/shard_map/all_to_all | solution.py:28
  194.1 6.3 %collective-permute-start.7 = (bf16[256,384]{1,0:T(8,128)(2,1)S(1)}, bf16[256,384]{1,0:T(8,128)(2,1)S(1)}, u32[]{:S(2)}, u32[]{:S(2)}) collective-permute-start(bf16[256,384]{1,0:T(8,128)(2,1)S(1)} %copy-done.16), channel_id=1, source_target_pairs={{0,1},{1,0},{2,3},{3,2},{4,5},{5,4},{6,7},{7,6},{8,9},{9,8},{10,11... | collective-permute-start | bytes 589832 | tf_op jit(solution)/shard_map/ppermute | solution.py:32
  200.4 10.1 %collective-permute-done.7 = bf16[256,384]{1,0:T(8,128)(2,1)S(1)} collective-permute-done((bf16[256,384]{1,0:T(8,128)(2,1)S(1)}, bf16[256,384]{1,0:T(8,128)(2,1)S(1)}, u32[]{:S(2)}, u32[]{:S(2)}) %collective-permute-start.7) | collective-permute-done | bytes 196640 | tf_op jit(solution)/shard_map/ppermute | solution.py:32
  210.6 4.9 %collective-permute-start.10 = (bf16[256,384]{1,0:T(8,128)(2,1)S(1)}, bf16[256,384]{1,0:T(8,128)(2,1)S(1)}, u32[]{:S(2)}, u32[]{:S(2)}) collective-permute-start(bf16[256,384]{1,0:T(8,128)(2,1)S(1)} %fusion.lat_0), channel_id=1, source_target_pairs={{0,6},{2,0},{4,2},{6,4},{1,7},{3,1},{5,3},{7,5},{8,14},{10,8},{12,... | collective-permute-start | bytes 589832 | tf_op jit(solution)/shard_map/ppermute | solution.py:37
  215.5 1.9 collective-permute-start.8
  217.4 4.2 %collective-permute-start.9 = (bf16[256,384]{1,0:T(8,128)(2,1)S(1)}, bf16[256,384]{1,0:T(8,128)(2,1)S(1)}, u32[]{:S(2)}, u32[]{:S(2)}) collective-permute-start(bf16[256,384]{1,0:T(8,128)(2,1)S(1)} %fusion.lat_0), channel_id=1, source_target_pairs={{0,4},{2,6},{4,0},{6,2},{1,5},{3,7},{5,1},{7,3},{8,12},{10,14},{12... | collective-permute-start | bytes 589832 | tf_op jit(solution)/shard_map/ppermute | solution.py:37
  221.6 3.7 %gram.1 = f32[64,8,128]{2,1,0:T(8,128)} custom-call(bf16[2,8,16,2688]{3,2,1,0:T(8,128)(2,1)} %bitcast.30, bf16[8,2,2,16,2560]{4,3,2,1,0:T(8,128)(2,1)} %copy-done), custom_call_target="tpu_custom_call" | custom-call | tf_op jit(solution)/shard_map/gram/pallas_call | solution.py:318
  227.6 6.5 %all-to-all-start.3 = ((f32[64,1,8]{2,1,0:T(1,128)}), f32[64,1,8]{2,1,0:T(1,128)S(1)}, u32[]{:S(2)}, u32[]{:S(2)}) async-start(f32[64,1,8]{2,1,0:T(1,128)} %bitcast.19), calls=%async_computation.3 | async-start | bytes 65536 | tf_op jit(solution)/shard_map/all_to_all | solution.py:28
  235.0 4.0 %down_grad.1 = (bf16[640,384]{1,0:T(8,128)(2,1)}, f32[1,640]{1,0:T(1,128)}) custom-call(bf16[256,1024]{1,0:T(8,128)(2,1)} %get-tuple-element.33.act_0.in_0, bf16[256,1024]{1,0:T(8,128)(2,1)} %copy-done.4, bf16[256,1024]{1,0:T(8,128)(2,1)} %copy-done.5, bf16[256,1024]{1,0:T(8,128)(2,1)} %collective-permute-done.6.act_3.in_3, bf16[256,384]{1,0:T(8,128)(2,1)} %copy-done.6, ...), custom_call_target="tpu_custom_call" | custom-call | tf_op jit(solution)/shard_map/down_grad/pallas_call | solution.py:340
  239.0 3.5 %up_grad.1 = bf16[384,640]{1,0:T(8,128)(2,1)} custom-call(s32[2]{0:T(128)} %pad_add_fusion.place, bf16[4,256,640]{2,1,0:T(8,128)(2,1)} %copy-done.2, bf16[256,1024]{1,0:T(8,128)(2,1)} %get-tuple-element.33.act_0.in_0, bf16[256,1024]{1,0:T(8,128)(2,1)} %copy-done.4, bf16[256,1024]{1,0:T(8,128)(2,1)} %copy-done.5, ...), custom_call_target="tpu_custom_call" | custom-call | tf_op jit(solution)/shard_map/up_grad/pallas_call | solution.py:331
  242.5 5.8 %all-to-all-done.3 = f32[64,1,8]{2,1,0:T(1,128)S(1)} async-done(((f32[64,1,8]{2,1,0:T(1,128)}), f32[64,1,8]{2,1,0:T(1,128)S(1)}, u32[]{:S(2)}, u32[]{:S(2)}) %all-to-all-start.3) | async-done | bytes 2080 | tf_op jit(solution)/shard_map/all_to_all | solution.py:28
  (48 shorter events, 11.1 us)
Async XLA Ops:
  3.2 77.7 %all-to-all-start = ((bf16[16,16,2688]{2,1,0:T(8,128)(2,1)}), bf16[16,16,2688]{2,1,0:T(8,128)(2,1)S(1)}, u32[]{:S(2)}, u32[]{:S(2)}) async-start(bf16[16,16,2688]{2,1,0:T(8,128)(2,1)} %bitcast.31), calls=%async_computation | async-start | bytes 2752512 | tf_op jit(solution)/shard_map/all_to_all | solution.py:28
  17.1 11.3 %copy-start.7 = (bf16[1,384,640]{2,1,0:T(8,128)(2,1)S(1)}, bf16[1,384,640]{2,1,0:T(8,128)(2,1)}, u32[]{:S(2)}) copy-start(bf16[1,384,640]{2,1,0:T(8,128)(2,1)} %param.11) | copy-start | bytes 1474564
  20.6 52.9 %collective-permute-start = (bf16[128,3072]{1,0:T(8,128)(2,1)}, bf16[128,3072]{1,0:T(8,128)(2,1)S(1)}, u32[]{:S(2)}, u32[]{:S(2)}) collective-permute-start(bf16[128,3072]{1,0:T(8,128)(2,1)} %get-tuple-element.24), channel_id=1, source_target_pairs={{0,1},{1,0},{2,3},{3,2},{4,5},{5,4},{6,7},{7,6},{8,9},{9,8},{10,11... | collective-permute-start | bytes 2359304 | tf_op jit(solution)/shard_map/ppermute | solution.py:32
  28.4 16.2 %collective-permute-start.1 = (bf16[384,640]{1,0:T(8,128)(2,1)S(1)}, bf16[384,640]{1,0:T(8,128)(2,1)S(1)}, u32[]{:S(2)}, u32[]{:S(2)}) collective-permute-start(bf16[384,640]{1,0:T(8,128)(2,1)S(1)} %bitcast.42), channel_id=1, source_target_pairs={{0,2},{2,4},{4,6},{6,0},{1,3},{3,5},{5,7},{7,1},{8,10},{10,12},{12... | collective-permute-start | bytes 1474568 | tf_op jit(solution)/shard_map/ppermute | solution.py:37
  31.8 23.3 %collective-permute-start.2 = (bf16[384,640]{1,0:T(8,128)(2,1)S(1)}, bf16[384,640]{1,0:T(8,128)(2,1)S(1)}, u32[]{:S(2)}, u32[]{:S(2)}) collective-permute-start(bf16[384,640]{1,0:T(8,128)(2,1)S(1)} %bitcast.43), channel_id=1, source_target_pairs={{0,4},{2,6},{4,0},{6,2},{1,5},{3,7},{5,1},{7,3},{8,12},{10,14},{12... | collective-permute-start | bytes 1474568 | tf_op jit(solution)/shard_map/ppermute | solution.py:37
  36.4 20.2 %collective-permute-start.3 = (bf16[384,640]{1,0:T(8,128)(2,1)S(1)}, bf16[384,640]{1,0:T(8,128)(2,1)S(1)}, u32[]{:S(2)}, u32[]{:S(2)}) collective-permute-start(bf16[384,640]{1,0:T(8,128)(2,1)S(1)} %bitcast.44), channel_id=1, source_target_pairs={{0,6},{2,0},{4,2},{6,4},{1,7},{3,1},{5,3},{7,5},{8,14},{10,8},{12,... | collective-permute-start | bytes 1474568 | tf_op jit(solution)/shard_map/ppermute | solution.py:37
  44.6 29.0 %copy-start.8 = (bf16[384,640]{1,0:T(8,128)(2,1)}, bf16[384,640]{1,0:T(8,128)(2,1)S(1)}, u32[]{:S(2)}) copy-start(bf16[384,640]{1,0:T(8,128)(2,1)S(1)} %collective-permute-done.1.up_1) | copy-start | bytes 1474564
  55.1 18.4 %copy-start.9 = (bf16[384,640]{1,0:T(8,128)(2,1)}, bf16[384,640]{1,0:T(8,128)(2,1)S(1)}, u32[]{:S(2)}) copy-start(bf16[384,640]{1,0:T(8,128)(2,1)S(1)} %collective-permute-done.2.up_2) | copy-start | bytes 1474564
  56.7 16.9 %copy-start.10 = (bf16[384,640]{1,0:T(8,128)(2,1)}, bf16[384,640]{1,0:T(8,128)(2,1)S(1)}, u32[]{:S(2)}) copy-start(bf16[384,640]{1,0:T(8,128)(2,1)S(1)} %collective-permute-done.3.up_3) | copy-start | bytes 1474564
  73.5 0.9 copy-start.3
  80.9 1.1 copy-start.1
  86.0 97.4 %all-to-all-start.1 = ((bf16[8,2,2,16,2560]{4,3,2,1,0:T(8,128)(2,1)}), bf16[8,2,2,16,2560]{4,3,2,1,0:T(8,128)(2,1)S(1)}, u32[]{:S(2)}, u32[]{:S(2)}) async-start(bf16[8,2,2,16,2560]{4,3,2,1,0:T(8,128)(2,1)} %mix.1), calls=%async_computation.1 | async-start | bytes 5242880 | tf_op jit(solution)/shard_map/all_to_all | solution.py:28
  114.5 16.9 %collective-permute-start.4 = (bf16[256,1024]{1,0:T(8,128)(2,1)S(1)}, bf16[256,1024]{1,0:T(8,128)(2,1)S(1)}, u32[]{:S(2)}, u32[]{:S(2)}) collective-permute-start(bf16[256,1024]{1,0:T(8,128)(2,1)S(1)} %get-tuple-element.44), channel_id=1, source_target_pairs={{0,2},{2,4},{4,6},{6,0},{1,3},{3,5},{5,7},{7,1},{8,10},{10,12},{12... | collective-permute-start | bytes 1572872 | tf_op jit(solution)/shard_map/ppermute | solution.py:37
  117.9 24.2 %collective-permute-start.5 = (bf16[256,1024]{1,0:T(8,128)(2,1)S(1)}, bf16[256,1024]{1,0:T(8,128)(2,1)S(1)}, u32[]{:S(2)}, u32[]{:S(2)}) collective-permute-start(bf16[256,1024]{1,0:T(8,128)(2,1)S(1)} %get-tuple-element.43), channel_id=1, source_target_pairs={{0,4},{2,6},{4,0},{6,2},{1,5},{3,7},{5,1},{7,3},{8,12},{10,14},{12... | collective-permute-start | bytes 1572872 | tf_op jit(solution)/shard_map/ppermute | solution.py:37
  122.6 21.2 %collective-permute-start.6 = (bf16[256,1024]{1,0:T(8,128)(2,1)S(1)}, bf16[256,1024]{1,0:T(8,128)(2,1)}, u32[]{:S(2)}, u32[]{:S(2)}) collective-permute-start(bf16[256,1024]{1,0:T(8,128)(2,1)S(1)} %get-tuple-element.42), channel_id=1, source_target_pairs={{0,6},{2,0},{4,2},{6,4},{1,7},{3,1},{5,3},{7,5},{8,14},{10,8},{12,... | collective-permute-start | bytes 1572872 | tf_op jit(solution)/shard_map/ppermute | solution.py:37
  131.4 79.2 %copy-start.4 = (bf16[256,1024]{1,0:T(8,128)(2,1)}, bf16[256,1024]{1,0:T(8,128)(2,1)S(1)}, u32[]{:S(2)}) copy-start(bf16[256,1024]{1,0:T(8,128)(2,1)S(1)} %collective-permute-done.4.act_1.in_1) | copy-start | bytes 1572868
  142.1 0.8 copy-start.5
  183.4 1.5 copy-start
  189.7 4.5 %copy-start.16 = (bf16[256,384]{1,0:T(8,128)(2,1)S(1)}, bf16[256,384]{1,0:T(8,128)(2,1)}, u32[]{:S(2)}) copy-start(bf16[256,384]{1,0:T(8,128)(2,1)} %get-tuple-element.29) | copy-start | bytes 589828
  189.7 20.8 %copy-start.11 = (f32[8,2,16,384]{3,2,1,0:T(8,128)S(1)}, f32[8,2,16,384]{3,2,1,0:T(8,128)}, u32[]{:S(2)}) copy-start(f32[8,2,16,384]{3,2,1,0:T(8,128)} %get-tuple-element.38) | copy-start | bytes 1179652
  189.7 20.8 %copy-start.12 = (f32[256,384]{1,0:T(8,128)S(1)}, f32[256,384]{1,0:T(8,128)}, u32[]{:S(2)}) copy-start(f32[256,384]{1,0:T(8,128)} %get-tuple-element.37) | copy-start | bytes 1179652
  189.7 37.2 %all-to-all-start.2 = ((bf16[4,256,640]{2,1,0:T(8,128)(2,1)}), bf16[4,256,640]{2,1,0:T(8,128)(2,1)S(1)}, u32[]{:S(2)}, u32[]{:S(2)}) async-start(bf16[4,256,640]{2,1,0:T(8,128)(2,1)} %get-tuple-element.31), calls=%async_computation.2 | async-start | bytes 2621440 | tf_op jit(solution)/shard_map/all_to_all | solution.py:28
  194.1 16.4 %collective-permute-start.7 = (bf16[256,384]{1,0:T(8,128)(2,1)S(1)}, bf16[256,384]{1,0:T(8,128)(2,1)S(1)}, u32[]{:S(2)}, u32[]{:S(2)}) collective-permute-start(bf16[256,384]{1,0:T(8,128)(2,1)S(1)} %copy-done.16), channel_id=1, source_target_pairs={{0,1},{1,0},{2,3},{3,2},{4,5},{5,4},{6,7},{7,6},{8,9},{9,8},{10,11... | collective-permute-start | bytes 589832 | tf_op jit(solution)/shard_map/ppermute | solution.py:32
  210.6 14.8 %copy-start.6 = (bf16[256,384]{1,0:T(8,128)(2,1)}, bf16[256,384]{1,0:T(8,128)(2,1)S(1)}, u32[]{:S(2)}) copy-start(bf16[256,384]{1,0:T(8,128)(2,1)S(1)} %fusion.lat_0) | copy-start | bytes 589828
  210.6 23.6 %collective-permute-start.10 = (bf16[256,384]{1,0:T(8,128)(2,1)S(1)}, bf16[256,384]{1,0:T(8,128)(2,1)S(1)}, u32[]{:S(2)}, u32[]{:S(2)}) collective-permute-start(bf16[256,384]{1,0:T(8,128)(2,1)S(1)} %fusion.lat_0), channel_id=1, source_target_pairs={{0,6},{2,0},{4,2},{6,4},{1,7},{3,1},{5,3},{7,5},{8,14},{10,8},{12,... | collective-permute-start | bytes 589832 | tf_op jit(solution)/shard_map/ppermute | solution.py:37
  215.5 18.7 %collective-permute-start.8 = (bf16[256,384]{1,0:T(8,128)(2,1)S(1)}, bf16[256,384]{1,0:T(8,128)(2,1)S(1)}, u32[]{:S(2)}, u32[]{:S(2)}) collective-permute-start(bf16[256,384]{1,0:T(8,128)(2,1)S(1)} %fusion.lat_0), channel_id=1, source_target_pairs={{0,2},{2,4},{4,6},{6,0},{1,3},{3,5},{5,7},{7,1},{8,10},{10,12},{12... | collective-permute-start | bytes 589832 | tf_op jit(solution)/shard_map/ppermute | solution.py:37
  217.4 16.8 %collective-permute-start.9 = (bf16[256,384]{1,0:T(8,128)(2,1)S(1)}, bf16[256,384]{1,0:T(8,128)(2,1)S(1)}, u32[]{:S(2)}, u32[]{:S(2)}) collective-permute-start(bf16[256,384]{1,0:T(8,128)(2,1)S(1)} %fusion.lat_0), channel_id=1, source_target_pairs={{0,4},{2,6},{4,0},{6,2},{1,5},{3,7},{5,1},{7,3},{8,12},{10,14},{12... | collective-permute-start | bytes 589832 | tf_op jit(solution)/shard_map/ppermute | solution.py:37
  226.9 12.1 %copy-start.2 = (bf16[4,256,640]{2,1,0:T(8,128)(2,1)}, bf16[4,256,640]{2,1,0:T(8,128)(2,1)S(1)}, u32[]{:S(2)}) copy-start(bf16[4,256,640]{2,1,0:T(8,128)(2,1)S(1)} %all-to-all-done.2.grads) | copy-start | bytes 3932164
  227.6 20.7 %all-to-all-start.3 = ((f32[64,1,8]{2,1,0:T(1,128)}), f32[64,1,8]{2,1,0:T(1,128)S(1)}, u32[]{:S(2)}, u32[]{:S(2)}) async-start(f32[64,1,8]{2,1,0:T(1,128)} %bitcast.19), calls=%async_computation.3 | async-start | bytes 65536 | tf_op jit(solution)/shard_map/all_to_all | solution.py:28
  234.2 0.7 copy-start.13
  234.2 0.7 copy-start.14
  234.2 0.8 copy-start.15

commit v3 on v2

v3 whole, which is shorter than its diff:
```python
import jax
import jax.numpy as jnp
from jax import lax
from jax.experimental import pallas as pl
from jax.experimental.pallas import tpu as pltpu
from jax.sharding import Mesh, PartitionSpec as P


MIXES = 8
LANES = 128
BLOCK = 640
TERMS = 3
epsilon = 1e-06
root_coef = 0.7978845608028654
GROUP = ("zl", "yh")
SMEM = pl.BlockSpec(memory_space=pltpu.SMEM)


def gelu_pair(values):
    tangent = jnp.tanh(root_coef * (values + 0.044715 * values * values * values))
    result = 0.5 * values * (1.0 + tangent)
    slopes = 0.5 * (1.0 + tangent) + 0.5 * values * (1.0 - tangent * tangent) * root_coef * (
        1.0 + 3.0 * 0.044715 * values * values
    )
    return (result, slopes)


def exchange(pieces, axes):
    return lax.all_to_all(pieces, axes, split_axis=0, concat_axis=0, tiled=True)


def swapped(value, axis):
    return lax.ppermute(value, axis, [(0, 1), (1, 0)])


def shifted(value, axis, steps):
    count = lax.axis_size(axis)
    return lax.ppermute(value, axis, [(i, (i + steps) % count) for i in range(count)])


def split_terms(value):
    terms = []
    for _ in range(TERMS):
        term = value.astype(jnp.bfloat16).astype(jnp.float32)
        terms.append(term)
        value = value - term
    return terms


def shape(dims, dtype=jnp.bfloat16):
    return jax.ShapeDtypeStruct(dims, dtype)


def pack_grads_body(weights, grads, out):
    halves, sections, rows, cols = out.shape
    block = BLOCK
    for half in range(halves):
        for i in range((cols - LANES) // block):
            piece = grads[:, (i * halves + half) * block : (i * halves + half + 1) * block]
            out[half, :, :, i * block : (i + 1) * block] = piece.reshape(sections, rows, block)
    lane = lax.broadcasted_iota(jnp.int32, (rows, LANES), 1)
    row = lax.broadcasted_iota(jnp.int32, (rows, LANES), 0)
    value = jnp.zeros((rows, LANES), jnp.float32)
    for m in range(MIXES):
        value = jnp.where(lane == m, weights[0, m], value)
    tail = jnp.zeros((rows, LANES), jnp.float32)
    for i, term in enumerate(split_terms(value)):
        tail = jnp.where(row == i, term, tail)
    tail = tail.astype(jnp.bfloat16)
    for half in range(halves):
        for k in range(sections):
            out[half, k, :, cols - LANES :] = tail


def pack_inputs_body(place, layer_in, latent, kept, sent):
    tokens, cols = kept.shape
    ranks = latent.shape[1]
    half_cols = cols - ranks - LANES
    width = layer_in.shape[1]
    block = BLOCK
    first = place[0] == 0
    squares = jnp.zeros((tokens, LANES), jnp.float32)
    for at in range(0, width, LANES):
        tile = layer_in[:, at : at + LANES].astype(jnp.float32)
        squares = squares + tile * tile
    inv_rms = lax.rsqrt(jnp.sum(squares, axis=1, keepdims=True) / width + epsilon)
    lane = lax.broadcasted_iota(jnp.int32, (tokens, LANES), 1)
    tail = jnp.zeros((tokens, LANES), jnp.float32)
    for i, term in enumerate(split_terms(jnp.broadcast_to(inv_rms, (tokens, LANES)))):
        tail = jnp.where(lane == i, term, tail)
    tail = tail.astype(jnp.bfloat16)
    for i in range(half_cols // block):
        low = layer_in[:, 2 * i * block : (2 * i + 1) * block]
        high = layer_in[:, (2 * i + 1) * block : (2 * i + 2) * block]
        kept[:, i * block : (i + 1) * block] = jnp.where(first, low, high)
        sent[:, i * block : (i + 1) * block] = jnp.where(first, high, low)
    for out in (kept, sent):
        out[:, half_cols : half_cols + ranks] = latent[...]
        out[:, half_cols + ranks :] = tail


def up_rows_body(place, up_0, up_1, up_2, up_3, out):
    turn = lax.rem(place[1] - pl.program_id(0) + 4, 4)
    near, far = (jnp.where(turn == 0, up_0[...], up_1[...]), jnp.where(turn == 2, up_2[...], up_3[...]))
    out[...] = jnp.where(turn < 2, near, far)


def lift_body(place, kept, other, kept_rest, other_rest, up_half, mixed, sends, moves, scale, act):
    del mixed
    sections, halves, rows, block = sends.shape
    ranks = up_half.shape[0]
    at = pl.program_id(0)
    first = place[0] == 0

    def in_order(own, far, half):
        return jnp.where(first, own, far) if half == 0 else jnp.where(first, far, own)

    @pl.when(at == 0)
    def _():
        for half in range(halves):
            rest = in_order(kept_rest[...], other_rest[...], half).astype(jnp.float32)
            values, slopes = gelu_pair(rest[:, :, :ranks])
            inv_rms = jnp.sum(rest[:, :, ranks : ranks + LANES], axis=2, keepdims=True)
            act[:, half] = values.astype(jnp.bfloat16)
            scale[:, half] = slopes * inv_rms

    up = up_half[...]
    for half in range(halves):
        rows_in = in_order(kept[...], other[...], half)
        moves[0, :, half, :, :block] = rows_in
        moves[0, :, half, :, block:] = act[:, half]
        branch = jnp.dot(
            act[:, half].reshape(sections * rows, ranks), up, preferred_element_type=jnp.float32
        ).reshape(sections, rows, block)
        sends[:, half] = (rows_in.astype(jnp.float32) + branch).astype(jnp.bfloat16)


def mix_body(coef, grads, out):
    halves, sections, _, cols = grads.shape
    for half in range(halves):
        for at in range(0, cols, LANES):
            lanes = slice(at, at + LANES)
            tiles = [grads[half, k, :, lanes].astype(jnp.float32) for k in range(sections)]
            for k in range(sections):
                total = coef[k, 0] * tiles[k]
                for m in range(1, sections - k):
                    total = total + coef[k, m] * tiles[k + m]
                out[k, half, :, lanes] = total.astype(jnp.bfloat16)


def gram_body(grads, outs, result):
    halves, sections, _, cols = grads.shape
    sums = {}
    for half in range(halves):
        for at in range(0, cols, LANES):
            lanes = slice(at, at + LANES)
            left = [outs[k, half, :, lanes].astype(jnp.float32) for k in range(sections)]
            right = [grads[half, k, :, lanes].astype(jnp.float32) for k in range(sections)]
            for k in range(sections):
                for m in range(sections - k):
                    product = left[k] * right[k + m]
                    folded = product[:8] + product[8:]
                    sums[k, m] = folded if (k, m) not in sums else sums[k, m] + folded

    @pl.when(pl.program_id(0) == 0)
    def _():
        result[...] = jnp.zeros(result.shape, jnp.float32)

    for (k, m), total in sums.items():
        result[k * MIXES + m] += total


def share_body(place, grads, partial, other, scale, *outs):
    sections, halves, rows, _ = grads.shape
    count = sections * halves * rows
    latent_grad = ((partial[...] + other[...].astype(jnp.float32)) * scale[...]).astype(jnp.bfloat16)
    for step, out in enumerate(outs):
        at = pl.multiple_of(lax.rem(place[1] + step, len(outs)) * BLOCK, LANES)
        out[:, :BLOCK] = grads[:, :, :, pl.ds(at, BLOCK)].reshape(count, BLOCK)
        out[:, BLOCK:] = latent_grad


def weights_body(*refs):
    half = (len(refs) - 5) // 2
    moved, shared = refs[:half], refs[half : 2 * half]
    gain, down, up_out, down_out, gain_out = refs[2 * half :]
    up_total = jnp.zeros(up_out.shape, jnp.float32)
    down_total = jnp.zeros(down_out.shape, jnp.float32)
    over_tokens = (((0,), (0,)), ((), ()))
    for left, right in zip(moved, shared):
        up_total = up_total + lax.dot_general(
            left[:, BLOCK:], right[:, :BLOCK], over_tokens, preferred_element_type=jnp.float32
        )
        down_total = down_total + lax.dot_general(
            left[:, :BLOCK], right[:, BLOCK:], over_tokens, preferred_element_type=jnp.float32
        )
    up_out[...] = up_total.astype(jnp.bfloat16)
    gain_cols = jnp.transpose(jnp.broadcast_to(gain[...].astype(jnp.float32), (8, gain.shape[1])))
    down_out[...] = (down_total * gain_cols[:, :1]).astype(jnp.bfloat16)
    product = down_total * down[...].astype(jnp.float32)
    ones = jnp.ones((8, product.shape[1]), jnp.float32)
    sums = lax.dot_general(
        ones, product, (((1,), (1,)), ((), ())), precision=lax.Precision.HIGHEST, preferred_element_type=jnp.float32
    )
    gain_out[...] = sums[:1]


def whole(layer_in, latent, mix_grad, down_proj, up_proj, norm_gain, mix_weight):
    layer_in, latent, mix_grad = (layer_in[0], latent[0], mix_grad[0])
    tokens, width = layer_in.shape
    ranks = latent.shape[1]
    xs, zs = (lax.axis_size("x"), lax.axis_size("zh"))
    sections = lax.axis_size("zl") * lax.axis_size("yh")
    block = width // (xs * zs)
    half_width = xs * block
    rows = tokens // sections
    place = jnp.stack([lax.axis_index("zh"), lax.axis_index("x")]).astype(jnp.int32)

    packed = pl.pallas_call(
        pack_grads_body,
        in_specs=[SMEM, pl.BlockSpec((tokens, width), lambda: (0, 0))],
        out_specs=pl.BlockSpec((zs, sections, rows, half_width + LANES), lambda: (0, 0, 0, 0)),
        out_shape=shape((zs, sections, rows, half_width + LANES)),
        name="pack_grads",
    )(mix_weight, mix_grad)
    grads = exchange(packed.reshape(zs * sections, rows, half_width + LANES), ("zh", *GROUP))
    grads = grads.reshape(zs, sections, rows, half_width + LANES)

    full = half_width + ranks + LANES
    kept, sent = pl.pallas_call(
        pack_inputs_body,
        in_specs=[SMEM, pl.BlockSpec((tokens, width), lambda: (0, 0)), pl.BlockSpec((tokens, ranks), lambda: (0, 0))],
        out_specs=[pl.BlockSpec((tokens, full), lambda: (0, 0))] * 2,
        out_shape=[shape((tokens, full))] * 2,
        name="pack_inputs",
    )(place, layer_in, latent)
    other = swapped(sent, "zh")

    up_block = up_proj[0]
    ups = [up_block]
    for step in range(1, xs):
        ups.append(shifted(up_block, "x", step))
    up_half = pl.pallas_call(
        up_rows_body,
        grid=(xs,),
        in_specs=[SMEM] + [pl.BlockSpec((ranks, block), lambda a: (0, 0))] * xs,
        out_specs=pl.BlockSpec((ranks, block), lambda a: (0, a)),
        out_shape=shape((ranks, half_width)),
        name="up_rows",
    )(place, *ups)

    weights = jnp.sum(grads[0, :, :TERMS, half_width : half_width + MIXES].astype(jnp.float32), axis=1)
    grads_spec = pl.BlockSpec((zs, sections, rows, block), lambda a: (0, 0, 0, a))
    chunk_spec = pl.BlockSpec((sections, zs, rows, block), lambda a: (0, 0, 0, a))
    mixed = pl.pallas_call(
        mix_body,
        grid=(xs,),
        in_specs=[SMEM, grads_spec],
        out_specs=chunk_spec,
        out_shape=shape((sections, zs, rows, half_width)),
        name="mix",
    )(weights, grads)
    arrived = exchange(mixed, GROUP)

    kept, other = [t.reshape(sections, rows, full) for t in (kept, other)]
    wide = pl.BlockSpec((sections, rows, block), lambda a: (0, 0, a))
    rest = ranks + LANES
    narrow = pl.BlockSpec((sections, rows, rest), lambda a: (0, 0, half_width // rest))
    layer_out, moves, scale = pl.pallas_call(
        lift_body,
        grid=(xs,),
        in_specs=[SMEM, wide, wide, narrow, narrow]
        + [pl.BlockSpec((ranks, block), lambda a: (0, a)), pl.BlockSpec(memory_space=pl.ANY)],
        out_specs=[
            chunk_spec,
            pl.BlockSpec((1, sections, zs, rows, block + ranks), lambda a: (a, 0, 0, 0, 0)),
            pl.BlockSpec((sections, zs, rows, ranks), lambda a: (0, 0, 0, 0)),
        ],
        out_shape=[
            shape((sections, zs, rows, half_width)),
            shape((xs, sections, zs, rows, block + ranks)),
            shape((sections, zs, rows, ranks), jnp.float32),
        ],
        scratch_shapes=[pltpu.VMEM((sections, zs, rows, ranks), jnp.bfloat16)],
        name="lift",
    )(place, kept, other, kept, other, up_half, mixed)
    scale = scale.reshape(zs * tokens, ranks)

    moves = moves.reshape(xs, zs * tokens, block + ranks)
    at_x = place[1]
    moved = [lax.dynamic_index_in_dim(moves, at_x, 0, False)]
    for step in range(1, xs):
        moved.append(shifted(lax.dynamic_index_in_dim(moves, (at_x + step) % xs, 0, False), "x", step))
    arrived, *moved = lax.optimization_barrier((arrived, *moved))

    layer_out, arrived = lax.optimization_barrier((layer_out, arrived))
    outs = exchange(layer_out, GROUP)

    act_partial = jnp.einsum(
        "tc,rc->tr", arrived.reshape(zs * tokens, half_width), up_half, preferred_element_type=jnp.float32
    )
    act_other = swapped(act_partial.astype(jnp.bfloat16), "zh")
    piece = shape((zs * tokens, block + ranks))
    shares = pl.pallas_call(
        share_body,
        in_specs=[SMEM] + [pl.BlockSpec(memory_space=pltpu.VMEM)] * 4,
        out_specs=[pl.BlockSpec(memory_space=pltpu.VMEM)] * xs,
        out_shape=[piece] * xs,
        name="share",
    )(place, arrived, act_partial, act_other, scale)
    shares = [shares[0]] + [shifted(shares[step], "x", step) for step in range(1, xs)]

    products = pl.pallas_call(
        gram_body,
        grid=(xs,),
        in_specs=[grads_spec, chunk_spec],
        out_specs=pl.BlockSpec((sections * MIXES, 8, LANES), lambda a: (0, 0, 0)),
        out_shape=shape((sections * MIXES, 8, LANES), jnp.float32),
        name="gram",
    )(grads, outs)
    products = jnp.sum(products, axis=(1, 2)).reshape(sections, MIXES)
    spread = jnp.broadcast_to(products[:, None], (sections, xs * zs, MIXES))
    mixing = exchange(spread.reshape(sections * xs * zs, MIXES), (*GROUP, "x", "zh")).sum(axis=0)

    up_grad, down_grad, gain_grad = pl.pallas_call(
        weights_body,
        in_specs=[pl.BlockSpec(memory_space=pltpu.VMEM)] * (2 * xs + 2),
        out_specs=[pl.BlockSpec(memory_space=pltpu.VMEM)] * 3,
        out_shape=[shape((ranks, block)), shape((block, ranks)), shape((1, block), jnp.float32)],
        name="weights",
    )(*moved, *shares, norm_gain, down_proj[0])
    return (up_grad[None], down_grad[None], gain_grad, mixing[None])


def solution(mesh):
    devices = mesh.devices.reshape(4, 2, 8, 4, 2)
    fine = Mesh(devices, ("zl", "yh", "r", "x", "zh"))
    section, dp = (("zl", "yh", "r"), ("x", "zh"))
    return jax.shard_map(
        whole,
        mesh=fine,
        in_specs=(
            P(section, dp, None),
            P(section, dp, None),
            P(section, dp, None),
            P(section, dp, None),
            P(section, None, dp),
            P(section, dp),
            P(section, None),
        ),
        out_specs=(
            P(section, None, dp),
            P(section, dp, None),
            P(section, dp),
            P(section, None),
        ),
        check_vma=False,
    )
```

time: 250 us -> 265 us (1.060)
  blocking collectives: 0 us -> 54 us
  waiting for transfers between devices: 106 us -> 76.1 us
  starting transfers between devices: 98.6 us -> 89.4 us
    all_to_all x0 -> x1, blocking collectives: none -> 54 us  [exchange(): return lax.all_to_all(pieces, axes, split_axis=0, concat_axis=0, tiled=True)]
    all_to_all x4 -> x3, waiting for transfers between devices: 45.5 us -> 7.24 us  [exchange(): return lax.all_to_all(pieces, axes, split_axis=0, concat_axis=0, tiled=True)]
    ppermute x2, waiting for transfers between devices: 26.9 us -> 36.4 us  [swapped(): return lax.ppermute(value, axis, [(0, 1), (1, 0)])]
    all_to_all x4 -> x3, starting transfers between devices: 50.8 us -> 42.7 us  [exchange(): return lax.all_to_all(pieces, axes, split_axis=0, concat_axis=0, tiled=True)]
  transfers between devices with their start and end apart: 15 -> 14, of which waited for: 10 -> 9; matrix products, arithmetic and copies ran while one was open for 2% -> 3% of each run, Pallas kernels for 8% -> 9%
where the time goes in v3:
time: 265 us; the launch traced here: 264 us
  starting transfers between devices  89.4 us (34%)
  waiting for transfers between devices  76.1 us (29%)
  blocking collectives  54 us (20%)
  Pallas kernels  31 us (12%)
  local copies, waits for them, and re-layouts  7.24 us (3%)
  other arithmetic  3.41 us (1%)
    all_to_all x1, blocking collectives, exchange(): return lax.all_to_all(pieces, axes, split_axis=0, concat_axis=0, tiled=True)  54 us
    all_to_all x3, starting transfers between devices, exchange(): return lax.all_to_all(pieces, axes, split_axis=0, concat_axis=0, tiled=True)  42.7 us
    ppermute x2, waiting for transfers between devices, swapped(): return lax.ppermute(value, axis, [(0, 1), (1, 0)])  36.4 us
    ppermute x9, starting transfers between devices, shifted(): lax.ppermute(value, axis, [(i, (i + steps) % count) for i in range(count)])  34.4 us
    ppermute x9, waiting for transfers between devices, shifted(): lax.ppermute(value, axis, [(i, (i + steps) % count) for i in range(count)])  32.4 us
    ppermute x2, starting transfers between devices, swapped(): return lax.ppermute(value, axis, [(0, 1), (1, 0)])  12.3 us
    all_to_all x3, waiting for transfers between devices, exchange(): return lax.all_to_all(pieces, axes, split_axis=0, concat_axis=0, tiled=True)  7.24 us
    pallas_call x1, Pallas kernels, whole(): pl.pallas_call(weights_body, in_specs=[pl.BlockSpec(memory_space=pltpu.VM...  5.82 us
  transfers between devices with their start and end apart: 14, of which 9 were waited for; matrix products, arithmetic and copies ran while one was open for 3% of the time, Pallas kernels for 9%

profile of v3, /device:TPU:16, one launch (start us, length us, event | category | flops | bytes accessed | tf_op | source)
XLA Modules:
  0.0 263.6 jit_solution(10475337346561400689)
XLA Ops:
  0.6 2.5 pack_grads.1
  3.2 54.0 %all_to_all.24 = bf16[16,16,2688]{2,1,0:T(8,128)(2,1)S(1)} all-to-all(bf16[16,16,2688]{2,1,0:T(8,128)(2,1)} %bitcast.32), channel_id=1, replica_groups=mesh['zl'=4,'yh'=2,'r'=8,'x'=4,'zh'=2] {'zh','zl','yh'}, dimensions={0} | all-to-all | bytes 2752512 | tf_op jit(solution)/shard_map/all_to_all | solution.py:29
  58.3 4.0 %mix.1.mixed = bf16[8,2,16,2560]{3,2,1,0:T(8,128)(2,1)} custom-call(f32[8,8]{1,0:T(8,128)} %convert_reduce_fusion.coef, bf16[2,8,16,2688]{3,2,1,0:T(8,128)(2,1)} %bitcast.29), custom_call_target="tpu_custom_call" | custom-call | tf_op jit(solution)/shard_map/mix/pallas_call | solution.py:255
  62.3 3.9 %all-to-all-start.1 = ((bf16[8,2,16,2560]{3,2,1,0:T(8,128)(2,1)}), bf16[8,2,16,2560]{3,2,1,0:T(8,128)(2,1)S(1)}, u32[]{:S(2)}, u32[]{:S(2)}) async-start(bf16[8,2,16,2560]{3,2,1,0:T(8,128)(2,1)} %mix.1.mixed), calls=%async_computation.1 | async-start | bytes 2621440 | tf_op jit(solution)/shard_map/all_to_all | solution.py:29
  66.9 2.9 %pack_inputs.1 = (bf16[128,3072]{1,0:T(8,128)(2,1)}, bf16[128,3072]{1,0:T(8,128)(2,1)}) custom-call(s32[2]{0:T(128)} %pad_add_fusion.place, bf16[128,5120]{1,0:T(8,128)(2,1)} %bitcast.39, bf16[128,384]{1,0:T(8,128)(2,1)} %bitcast.46), custom_call_target="tpu_custom_call" | custom-call | tf_op jit(solution)/shard_map/pack_inputs/pallas_call | solution.py:230
  69.8 4.2 %collective-permute-start = (bf16[128,3072]{1,0:T(8,128)(2,1)}, bf16[128,3072]{1,0:T(8,128)(2,1)S(1)}, u32[]{:S(2)}, u32[]{:S(2)}) collective-permute-start(bf16[128,3072]{1,0:T(8,128)(2,1)} %get-tuple-element.24), channel_id=1, source_target_pairs={{0,1},{1,0},{2,3},{3,2},{4,5},{5,4},{6,7},{7,6},{8,9},{9,8},{10,11... | collective-permute-start | bytes 2359304 | tf_op jit(solution)/shard_map/ppermute | solution.py:33
  73.9 3.4 %collective-permute-start.1 = (bf16[384,640]{1,0:T(8,128)(2,1)S(1)}, bf16[384,640]{1,0:T(8,128)(2,1)S(1)}, u32[]{:S(2)}, u32[]{:S(2)}) collective-permute-start(bf16[384,640]{1,0:T(8,128)(2,1)S(1)} %bitcast.41), channel_id=1, source_target_pairs={{0,2},{2,4},{4,6},{6,0},{1,3},{3,5},{5,7},{7,1},{8,10},{10,12},{12... | collective-permute-start | bytes 1474568 | tf_op jit(solution)/shard_map/ppermute | solution.py:38
  77.3 4.6 %collective-permute-start.2 = (bf16[384,640]{1,0:T(8,128)(2,1)S(1)}, bf16[384,640]{1,0:T(8,128)(2,1)}, u32[]{:S(2)}, u32[]{:S(2)}) collective-permute-start(bf16[384,640]{1,0:T(8,128)(2,1)S(1)} %bitcast.42), channel_id=1, source_target_pairs={{0,4},{2,6},{4,0},{6,2},{1,5},{3,7},{5,1},{7,3},{8,12},{10,14},{12... | collective-permute-start | bytes 1474568 | tf_op jit(solution)/shard_map/ppermute | solution.py:38
  82.0 3.3 %collective-permute-start.3 = (bf16[384,640]{1,0:T(8,128)(2,1)S(1)}, bf16[384,640]{1,0:T(8,128)(2,1)}, u32[]{:S(2)}, u32[]{:S(2)}) collective-permute-start(bf16[384,640]{1,0:T(8,128)(2,1)S(1)} %bitcast.43), channel_id=1, source_target_pairs={{0,6},{2,0},{4,2},{6,4},{1,7},{3,1},{5,3},{7,5},{8,14},{10,8},{12,... | collective-permute-start | bytes 1474568 | tf_op jit(solution)/shard_map/ppermute | solution.py:38
  85.4 4.8 %collective-permute-done.1.up_1 = bf16[384,640]{1,0:T(8,128)(2,1)S(1)} collective-permute-done((bf16[384,640]{1,0:T(8,128)(2,1)S(1)}, bf16[384,640]{1,0:T(8,128)(2,1)S(1)}, u32[]{:S(2)}, u32[]{:S(2)}) %collective-permute-start.1) | collective-permute-done | bytes 491552 | tf_op jit(solution)/shard_map/ppermute | solution.py:38
  90.1 9.3 %collective-permute-done.2.up_2 = bf16[384,640]{1,0:T(8,128)(2,1)} collective-permute-done((bf16[384,640]{1,0:T(8,128)(2,1)S(1)}, bf16[384,640]{1,0:T(8,128)(2,1)}, u32[]{:S(2)}, u32[]{:S(2)}) %collective-permute-start.2) | collective-permute-done | bytes 491552 | tf_op jit(solution)/shard_map/ppermute | solution.py:38
  101.0 3.5 %up_rows.1.up_half = bf16[384,2560]{1,0:T(8,128)(2,1)} custom-call(s32[2]{0:T(128)} %pad_add_fusion.place, bf16[384,640]{1,0:T(8,128)(2,1)} %bitcast.40, bf16[384,640]{1,0:T(8,128)(2,1)} %copy-done.10, bf16[384,640]{1,0:T(8,128)(2,1)} %collective-permute-done.2.up_2, bf16[384,640]{1,0:T(8,128)(2,1)} %collective-permute-done.3.up_3), custom_call_target="tpu_custom_call" | custom-call | tf_op jit(solution)/shard_map/up_rows/pallas_call | solution.py:243
  104.5 21.4 %collective-permute-done = bf16[128,3072]{1,0:T(8,128)(2,1)S(1)} collective-permute-done((bf16[128,3072]{1,0:T(8,128)(2,1)}, bf16[128,3072]{1,0:T(8,128)(2,1)S(1)}, u32[]{:S(2)}, u32[]{:S(2)}) %collective-permute-start) | collective-permute-done | bytes 786464 | tf_op jit(solution)/shard_map/ppermute | solution.py:33
  126.7 5.4 %lift.1 = (bf16[8,2,16,2560]{3,2,1,0:T(8,128)(2,1)}, bf16[4,8,2,16,1024]{4,3,2,1,0:T(8,128)(2,1)}, f32[8,2,16,384]{3,2,1,0:T(8,128)}) custom-call(s32[2]{0:T(128)} %pad_add_fusion.place, bf16[8,16,3072]{2,1,0:T(8,128)(2,1)} %bitcast.33, bf16[8,16,3072]{2,1,0:T(8,128)(2,1)} %bitcast.35, bf16[8,16,3072]{2,1,0:T(8,128)(2,1)} %bitcast.34, ...), custom_call_target="tpu_custom_call" | custom-call | tf_op jit(solution)/shard_map/lift/pallas_call | solution.py:269
  132.1 2.6 dynamic-slice_bitcast_fusion
  134.7 3.5 %collective-permute-start.4 = (bf16[256,1024]{1,0:T(8,128)(2,1)S(1)}, bf16[256,1024]{1,0:T(8,128)(2,1)S(1)}, u32[]{:S(2)}, u32[]{:S(2)}) collective-permute-start(bf16[256,1024]{1,0:T(8,128)(2,1)S(1)} %get-tuple-element.44), channel_id=1, source_target_pairs={{0,2},{2,4},{4,6},{6,0},{1,3},{3,5},{5,7},{7,1},{8,10},{10,12},{12... | collective-permute-start | bytes 1572872 | tf_op jit(solution)/shard_map/ppermute | solution.py:38
  138.2 4.6 %collective-permute-start.5 = (bf16[256,1024]{1,0:T(8,128)(2,1)S(1)}, bf16[256,1024]{1,0:T(8,128)(2,1)S(1)}, u32[]{:S(2)}, u32[]{:S(2)}) collective-permute-start(bf16[256,1024]{1,0:T(8,128)(2,1)S(1)} %get-tuple-element.43), channel_id=1, source_target_pairs={{0,4},{2,6},{4,0},{6,2},{1,5},{3,7},{5,1},{7,3},{8,12},{10,14},{12... | collective-permute-start | bytes 1572872 | tf_op jit(solution)/shard_map/ppermute | solution.py:38
  142.9 3.4 %collective-permute-start.6 = (bf16[256,1024]{1,0:T(8,128)(2,1)S(1)}, bf16[256,1024]{1,0:T(8,128)(2,1)}, u32[]{:S(2)}, u32[]{:S(2)}) collective-permute-start(bf16[256,1024]{1,0:T(8,128)(2,1)S(1)} %get-tuple-element.42), channel_id=1, source_target_pairs={{0,6},{2,0},{4,2},{6,4},{1,7},{3,1},{5,3},{7,5},{8,14},{10,8},{12,... | collective-permute-start | bytes 1572872 | tf_op jit(solution)/shard_map/ppermute | solution.py:38
  146.3 5.6 %collective-permute-done.4.refs_1_ = bf16[256,1024]{1,0:T(8,128)(2,1)S(1)} collective-permute-done((bf16[256,1024]{1,0:T(8,128)(2,1)S(1)}, bf16[256,1024]{1,0:T(8,128)(2,1)S(1)}, u32[]{:S(2)}, u32[]{:S(2)}) %collective-permute-start.4) | collective-permute-done | bytes 524320 | tf_op jit(solution)/shard_map/ppermute | solution.py:38
  151.8 10.4 %collective-permute-done.5.refs_2_ = bf16[256,1024]{1,0:T(8,128)(2,1)S(1)} collective-permute-done((bf16[256,1024]{1,0:T(8,128)(2,1)S(1)}, bf16[256,1024]{1,0:T(8,128)(2,1)S(1)}, u32[]{:S(2)}, u32[]{:S(2)}) %collective-permute-start.5) | collective-permute-done | bytes 524320 | tf_op jit(solution)/shard_map/ppermute | solution.py:38
  163.9 12.0 %all-to-all-start.2 = ((bf16[8,2,16,2560]{3,2,1,0:T(8,128)(2,1)}), bf16[8,2,16,2560]{3,2,1,0:T(8,128)(2,1)}, u32[]{:S(2)}, u32[]{:S(2)}) async-start(bf16[8,2,16,2560]{3,2,1,0:T(8,128)(2,1)} %get-tuple-element.41), calls=%async_computation.2 | async-start | bytes 2621440 | tf_op jit(solution)/shard_map/all_to_all | solution.py:29
  175.9 1.6 fusion
  177.5 8.2 %collective-permute-start.7 = (bf16[256,384]{1,0:T(8,128)(2,1)S(1)}, bf16[256,384]{1,0:T(8,128)(2,1)S(1)}, u32[]{:S(2)}, u32[]{:S(2)}) collective-permute-start(bf16[256,384]{1,0:T(8,128)(2,1)S(1)} %get-tuple-element.46), channel_id=1, source_target_pairs={{0,1},{1,0},{2,3},{3,2},{4,5},{5,4},{6,7},{7,6},{8,9},{9,8},{10,11... | collective-permute-start | bytes 589832 | tf_op jit(solution)/shard_map/ppermute | solution.py:33
  185.7 15.1 %collective-permute-done.7.other = bf16[256,384]{1,0:T(8,128)(2,1)S(1)} collective-permute-done((bf16[256,384]{1,0:T(8,128)(2,1)S(1)}, bf16[256,384]{1,0:T(8,128)(2,1)S(1)}, u32[]{:S(2)}, u32[]{:S(2)}) %collective-permute-start.7) | collective-permute-done | bytes 196640 | tf_op jit(solution)/shard_map/ppermute | solution.py:33
  201.4 3.1 %share.1 = (bf16[256,1024]{1,0:T(8,128)(2,1)}, bf16[256,1024]{1,0:T(8,128)(2,1)}, bf16[256,1024]{1,0:T(8,128)(2,1)}, bf16[256,1024]{1,0:T(8,128)(2,1)}) custom-call(s32[2]{0:T(128)} %pad_add_fusion.place, bf16[8,2,16,2560]{3,2,1,0:T(8,128)(2,1)} %copy-done.2, f32[256,384]{1,0:T(8,128)} %get-tuple-element.47.partial, bf16[256,384]{1,0:T(8,128)(2,1)} %copy-done.11, ...), custom_call_target="tpu_custom_call" | custom-call | tf_op jit(solution)/shard_map/share/pallas_call | solution.py:304
  204.5 5.8 %collective-permute-start.10 = (bf16[256,1024]{1,0:T(8,128)(2,1)}, bf16[256,1024]{1,0:T(8,128)(2,1)S(1)}, u32[]{:S(2)}, u32[]{:S(2)}) collective-permute-start(bf16[256,1024]{1,0:T(8,128)(2,1)} %get-tuple-element.37), channel_id=1, source_target_pairs={{0,6},{2,0},{4,2},{6,4},{1,7},{3,1},{5,3},{7,5},{8,14},{10,8},{12,... | collective-permute-start | bytes 1572872 | tf_op jit(solution)/shard_map/ppermute | solution.py:38
  210.3 1.9 collective-permute-start.8
  212.3 3.7 %collective-permute-start.9 = (bf16[256,1024]{1,0:T(8,128)(2,1)}, bf16[256,1024]{1,0:T(8,128)(2,1)S(1)}, u32[]{:S(2)}, u32[]{:S(2)}) collective-permute-start(bf16[256,1024]{1,0:T(8,128)(2,1)} %get-tuple-element.36), channel_id=1, source_target_pairs={{0,4},{2,6},{4,0},{6,2},{1,5},{3,7},{5,1},{7,3},{8,12},{10,14},{12... | collective-permute-start | bytes 1572872 | tf_op jit(solution)/shard_map/ppermute | solution.py:38
  216.0 3.7 %gram.1 = f32[64,8,128]{2,1,0:T(8,128)} custom-call(bf16[2,8,16,2688]{3,2,1,0:T(8,128)(2,1)} %bitcast.30, bf16[8,2,16,2560]{3,2,1,0:T(8,128)(2,1)} %all-to-all-done.2.outs), custom_call_target="tpu_custom_call" | custom-call | tf_op jit(solution)/shard_map/gram/pallas_call | solution.py:313
  221.9 26.8 %all-to-all-start.3 = ((f32[64,1,8]{2,1,0:T(1,128)}), f32[64,1,8]{2,1,0:T(1,128)S(1)}, u32[]{:S(2)}, u32[]{:S(2)}) async-start(f32[64,1,8]{2,1,0:T(1,128)} %bitcast.20), calls=%async_computation.3 | async-start | bytes 65536 | tf_op jit(solution)/shard_map/all_to_all | solution.py:29
  249.9 5.8 %weights.3 = (bf16[384,640]{1,0:T(8,128)(2,1)}, bf16[640,384]{1,0:T(8,128)(2,1)}, f32[1,640]{1,0:T(1,128)}) custom-call(bf16[256,1024]{1,0:T(8,128)(2,1)} %get-tuple-element.26.refs_0_, bf16[256,1024]{1,0:T(8,128)(2,1)} %copy-done.4, bf16[256,1024]{1,0:T(8,128)(2,1)} %copy-done.5, bf16[256,1024]{1,0:T(8,128)(2,1)} %collective-permute-done.6.refs_3_, ...), custom_call_target="tpu_custom_call" | custom-call | tf_op jit(solution)/shard_map/weights/pallas_call | solution.py:325
  255.8 7.2 %all-to-all-done.3 = f32[64,1,8]{2,1,0:T(1,128)S(1)} async-done(((f32[64,1,8]{2,1,0:T(1,128)}), f32[64,1,8]{2,1,0:T(1,128)S(1)}, u32[]{:S(2)}, u32[]{:S(2)}) %all-to-all-start.3) | async-done | bytes 2080 | tf_op jit(solution)/shard_map/all_to_all | solution.py:29
  (37 shorter events, 10.5 us)
Async XLA Ops:
  57.2 1.1 copy-start.1
  62.3 11.6 %copy-start.9 = (bf16[1,384,640]{2,1,0:T(8,128)(2,1)S(1)}, bf16[1,384,640]{2,1,0:T(8,128)(2,1)}, u32[]{:S(2)}) copy-start(bf16[1,384,640]{2,1,0:T(8,128)(2,1)} %param.11) | copy-start | bytes 1474564
  62.3 101.6 %all-to-all-start.1 = ((bf16[8,2,16,2560]{3,2,1,0:T(8,128)(2,1)}), bf16[8,2,16,2560]{3,2,1,0:T(8,128)(2,1)S(1)}, u32[]{:S(2)}, u32[]{:S(2)}) async-start(bf16[8,2,16,2560]{3,2,1,0:T(8,128)(2,1)} %mix.1.mixed), calls=%async_computation.1 | async-start | bytes 2621440 | tf_op jit(solution)/shard_map/all_to_all | solution.py:29
  69.8 56.1 %collective-permute-start = (bf16[128,3072]{1,0:T(8,128)(2,1)}, bf16[128,3072]{1,0:T(8,128)(2,1)S(1)}, u32[]{:S(2)}, u32[]{:S(2)}) collective-permute-start(bf16[128,3072]{1,0:T(8,128)(2,1)} %get-tuple-element.24), channel_id=1, source_target_pairs={{0,1},{1,0},{2,3},{3,2},{4,5},{5,4},{6,7},{7,6},{8,9},{9,8},{10,11... | collective-permute-start | bytes 2359304 | tf_op jit(solution)/shard_map/ppermute | solution.py:33
  73.9 16.2 %collective-permute-start.1 = (bf16[384,640]{1,0:T(8,128)(2,1)S(1)}, bf16[384,640]{1,0:T(8,128)(2,1)S(1)}, u32[]{:S(2)}, u32[]{:S(2)}) collective-permute-start(bf16[384,640]{1,0:T(8,128)(2,1)S(1)} %bitcast.41), channel_id=1, source_target_pairs={{0,2},{2,4},{4,6},{6,0},{1,3},{3,5},{5,7},{7,1},{8,10},{10,12},{12... | collective-permute-start | bytes 1474568 | tf_op jit(solution)/shard_map/ppermute | solution.py:38
  77.3 22.1 %collective-permute-start.2 = (bf16[384,640]{1,0:T(8,128)(2,1)S(1)}, bf16[384,640]{1,0:T(8,128)(2,1)}, u32[]{:S(2)}, u32[]{:S(2)}) collective-permute-start(bf16[384,640]{1,0:T(8,128)(2,1)S(1)} %bitcast.42), channel_id=1, source_target_pairs={{0,4},{2,6},{4,0},{6,2},{1,5},{3,7},{5,1},{7,3},{8,12},{10,14},{12... | collective-permute-start | bytes 1474568 | tf_op jit(solution)/shard_map/ppermute | solution.py:38
  82.0 19.0 %collective-permute-start.3 = (bf16[384,640]{1,0:T(8,128)(2,1)S(1)}, bf16[384,640]{1,0:T(8,128)(2,1)}, u32[]{:S(2)}, u32[]{:S(2)}) collective-permute-start(bf16[384,640]{1,0:T(8,128)(2,1)S(1)} %bitcast.43), channel_id=1, source_target_pairs={{0,6},{2,0},{4,2},{6,4},{1,7},{3,1},{5,3},{7,5},{8,14},{10,8},{12,... | collective-permute-start | bytes 1474568 | tf_op jit(solution)/shard_map/ppermute | solution.py:38
  90.1 10.8 %copy-start.10 = (bf16[384,640]{1,0:T(8,128)(2,1)}, bf16[384,640]{1,0:T(8,128)(2,1)S(1)}, u32[]{:S(2)}) copy-start(bf16[384,640]{1,0:T(8,128)(2,1)S(1)} %collective-permute-done.1.up_1) | copy-start | bytes 1474564
  125.8 0.9 copy-start.3
  134.7 41.2 %copy-start = (bf16[384,2560]{1,0:T(8,128)(2,1)S(1)}, bf16[384,2560]{1,0:T(8,128)(2,1)}, u32[]{:S(2)}) copy-start(bf16[384,2560]{1,0:T(8,128)(2,1)} %up_rows.1.up_half) | copy-start | bytes 5898244
  134.7 17.1 %collective-permute-start.4 = (bf16[256,1024]{1,0:T(8,128)(2,1)S(1)}, bf16[256,1024]{1,0:T(8,128)(2,1)S(1)}, u32[]{:S(2)}, u32[]{:S(2)}) collective-permute-start(bf16[256,1024]{1,0:T(8,128)(2,1)S(1)} %get-tuple-element.44), channel_id=1, source_target_pairs={{0,2},{2,4},{4,6},{6,0},{1,3},{3,5},{5,7},{7,1},{8,10},{10,12},{12... | collective-permute-start | bytes 1572872 | tf_op jit(solution)/shard_map/ppermute | solution.py:38
  138.2 23.9 %collective-permute-start.5 = (bf16[256,1024]{1,0:T(8,128)(2,1)S(1)}, bf16[256,1024]{1,0:T(8,128)(2,1)S(1)}, u32[]{:S(2)}, u32[]{:S(2)}) collective-permute-start(bf16[256,1024]{1,0:T(8,128)(2,1)S(1)} %get-tuple-element.43), channel_id=1, source_target_pairs={{0,4},{2,6},{4,0},{6,2},{1,5},{3,7},{5,1},{7,3},{8,12},{10,14},{12... | collective-permute-start | bytes 1572872 | tf_op jit(solution)/shard_map/ppermute | solution.py:38
  142.9 21.0 %collective-permute-start.6 = (bf16[256,1024]{1,0:T(8,128)(2,1)S(1)}, bf16[256,1024]{1,0:T(8,128)(2,1)}, u32[]{:S(2)}, u32[]{:S(2)}) collective-permute-start(bf16[256,1024]{1,0:T(8,128)(2,1)S(1)} %get-tuple-element.42), channel_id=1, source_target_pairs={{0,6},{2,0},{4,2},{6,4},{1,7},{3,1},{5,3},{7,5},{8,14},{10,8},{12,... | collective-permute-start | bytes 1572872 | tf_op jit(solution)/shard_map/ppermute | solution.py:38
  151.8 10.4 %copy-start.4 = (bf16[256,1024]{1,0:T(8,128)(2,1)}, bf16[256,1024]{1,0:T(8,128)(2,1)S(1)}, u32[]{:S(2)}) copy-start(bf16[256,1024]{1,0:T(8,128)(2,1)S(1)} %collective-permute-done.4.refs_1_) | copy-start | bytes 1572868
  162.2 0.8 copy-start.5
  163.9 13.6 %copy-start.2 = (bf16[8,2,16,2560]{3,2,1,0:T(8,128)(2,1)}, bf16[8,2,16,2560]{3,2,1,0:T(8,128)(2,1)S(1)}, u32[]{:S(2)}) copy-start(bf16[8,2,16,2560]{3,2,1,0:T(8,128)(2,1)S(1)} %all-to-all-done.1.grads) | copy-start | bytes 3932164
  163.9 52.1 %all-to-all-start.2 = ((bf16[8,2,16,2560]{3,2,1,0:T(8,128)(2,1)}), bf16[8,2,16,2560]{3,2,1,0:T(8,128)(2,1)}, u32[]{:S(2)}, u32[]{:S(2)}) async-start(bf16[8,2,16,2560]{3,2,1,0:T(8,128)(2,1)} %get-tuple-element.41), calls=%async_computation.2 | async-start | bytes 2621440 | tf_op jit(solution)/shard_map/all_to_all | solution.py:29
  177.5 23.2 %collective-permute-start.7 = (bf16[256,384]{1,0:T(8,128)(2,1)S(1)}, bf16[256,384]{1,0:T(8,128)(2,1)S(1)}, u32[]{:S(2)}, u32[]{:S(2)}) collective-permute-start(bf16[256,384]{1,0:T(8,128)(2,1)S(1)} %get-tuple-element.46), channel_id=1, source_target_pairs={{0,1},{1,0},{2,3},{3,2},{4,5},{5,4},{6,7},{7,6},{8,9},{9,8},{10,11... | collective-permute-start | bytes 589832 | tf_op jit(solution)/shard_map/ppermute | solution.py:33
  200.7 0.7 copy-start.11
  204.5 44.3 %collective-permute-start.10 = (bf16[256,1024]{1,0:T(8,128)(2,1)}, bf16[256,1024]{1,0:T(8,128)(2,1)S(1)}, u32[]{:S(2)}, u32[]{:S(2)}) collective-permute-start(bf16[256,1024]{1,0:T(8,128)(2,1)} %get-tuple-element.37), channel_id=1, source_target_pairs={{0,6},{2,0},{4,2},{6,4},{1,7},{3,1},{5,3},{7,5},{8,14},{10,8},{12,... | collective-permute-start | bytes 1572872 | tf_op jit(solution)/shard_map/ppermute | solution.py:38
  210.3 38.5 %collective-permute-start.8 = (bf16[256,1024]{1,0:T(8,128)(2,1)}, bf16[256,1024]{1,0:T(8,128)(2,1)S(1)}, u32[]{:S(2)}, u32[]{:S(2)}) collective-permute-start(bf16[256,1024]{1,0:T(8,128)(2,1)} %get-tuple-element.35), channel_id=1, source_target_pairs={{0,2},{2,4},{4,6},{6,0},{1,3},{3,5},{5,7},{7,1},{8,10},{10,12},{12... | collective-permute-start | bytes 1572872 | tf_op jit(solution)/shard_map/ppermute | solution.py:38
  212.3 36.6 %collective-permute-start.9 = (bf16[256,1024]{1,0:T(8,128)(2,1)}, bf16[256,1024]{1,0:T(8,128)(2,1)S(1)}, u32[]{:S(2)}, u32[]{:S(2)}) collective-permute-start(bf16[256,1024]{1,0:T(8,128)(2,1)} %get-tuple-element.36), channel_id=1, source_target_pairs={{0,4},{2,6},{4,0},{6,2},{1,5},{3,7},{5,1},{7,3},{8,12},{10,14},{12... | collective-permute-start | bytes 1572872 | tf_op jit(solution)/shard_map/ppermute | solution.py:38
  221.9 41.0 %all-to-all-start.3 = ((f32[64,1,8]{2,1,0:T(1,128)}), f32[64,1,8]{2,1,0:T(1,128)S(1)}, u32[]{:S(2)}, u32[]{:S(2)}) async-start(f32[64,1,8]{2,1,0:T(1,128)} %bitcast.20), calls=%async_computation.3 | async-start | bytes 65536 | tf_op jit(solution)/shard_map/all_to_all | solution.py:29
  248.8 0.8 copy-start.6
  248.8 1.0 copy-start.7
  248.8 1.1 copy-start.8

commit v4 on v3

--- a/solution.py
+++ b/solution.py
@@ -148,7 +148,7 @@
                 out[k, half, :, lanes] = total.astype(jnp.bfloat16)
 
 
-def gram_body(grads, outs, result):
+def gram_body(grads, outs, result, kept):
     halves, sections, _, cols = grads.shape
     sums = {}
     for half in range(halves):
@@ -162,12 +162,27 @@
                     folded = product[:8] + product[8:]
                     sums[k, m] = folded if (k, m) not in sums else sums[k, m] + folded
 
+    last = pl.num_programs(0) - 1
+
     @pl.when(pl.program_id(0) == 0)
     def _():
-        result[...] = jnp.zeros(result.shape, jnp.float32)
-
-    for (k, m), total in sums.items():
-        result[k * MIXES + m] += total
+        for (k, m), total in sums.items():
+            kept[k * MIXES + m] = total
+
+    @pl.when(pl.program_id(0) != 0)
+    def _():
+        for (k, m), total in sums.items():
+            kept[k * MIXES + m] += total
+
+    @pl.when(pl.program_id(0) == last)
+    def _():
+        lane = lax.broadcasted_iota(jnp.int32, (1, LANES), 1)
+        share = result.shape[0] // sections
+        for k in range(sections):
+            row = jnp.zeros((1, LANES), jnp.float32)
+            for m in range(sections - k):
+                row = jnp.where(lane == m, jnp.sum(kept[k * MIXES + m], keepdims=True), row)
+            result[k * share : (k + 1) * share] = jnp.broadcast_to(row, (share, LANES))
 
 
 def share_body(place, grads, partial, other, scale, *outs):
@@ -291,7 +306,6 @@
     moved = [lax.dynamic_index_in_dim(moves, at_x, 0, False)]
     for step in range(1, xs):
         moved.append(shifted(lax.dynamic_index_in_dim(moves, (at_x + step) % xs, 0, False), "x", step))
-    arrived, *moved = lax.optimization_barrier((arrived, *moved))
 
     layer_out, arrived = lax.optimization_barrier((layer_out, arrived))
     outs = exchange(layer_out, GROUP)
@@ -310,17 +324,17 @@
     )(place, arrived, act_partial, act_other, scale)
     shares = [shares[0]] + [shifted(shares[step], "x", step) for step in range(1, xs)]
 
+    everyone = sections * xs * zs
     products = pl.pallas_call(
         gram_body,
         grid=(xs,),
         in_specs=[grads_spec, chunk_spec],
-        out_specs=pl.BlockSpec((sections * MIXES, 8, LANES), lambda a: (0, 0, 0)),
-        out_shape=shape((sections * MIXES, 8, LANES), jnp.float32),
+        out_specs=pl.BlockSpec((everyone, LANES), lambda a: (0, 0)),
+        out_shape=shape((everyone, LANES), jnp.float32),
+        scratch_shapes=[pltpu.VMEM((sections * MIXES, 8, LANES), jnp.float32)],
         name="gram",
     )(grads, outs)
-    products = jnp.sum(products, axis=(1, 2)).reshape(sections, MIXES)
-    spread = jnp.broadcast_to(products[:, None], (sections, xs * zs, MIXES))
-    mixing = exchange(spread.reshape(sections * xs * zs, MIXES), (*GROUP, "x", "zh")).sum(axis=0)
+    mixing = exchange(products, (*GROUP, "x", "zh")).sum(axis=0)[:MIXES]
 
     up_grad, down_grad, gain_grad = pl.pallas_call(
         weights_body,

time: 265 us -> 231 us (0.87)
  the two profiles are of different devices: /device:TPU:16 before, /device:TPU:8 now
where the time goes in v4:
time: 231 us; the launch traced here: 230 us
  starting transfers between devices  67.6 us (29%)
  waiting for transfers between devices  61.7 us (27%)
  blocking collectives  57.1 us (25%)
  Pallas kernels  31.2 us (14%)
  local copies, waits for them, and re-layouts  8.36 us (4%)
    all_to_all x1, blocking collectives, exchange(): return lax.all_to_all(pieces, axes, split_axis=0, concat_axis=0, tiled=True)  57.1 us
    ppermute x2, waiting for transfers between devices, swapped(): return lax.ppermute(value, axis, [(0, 1), (1, 0)])  38.7 us
    ppermute x9, starting transfers between devices, shifted(): lax.ppermute(value, axis, [(i, (i + steps) % count) for i in range(count)])  33.4 us
    all_to_all x3, starting transfers between devices, exchange(): return lax.all_to_all(pieces, axes, split_axis=0, concat_axis=0, tiled=True)  24.8 us
    ppermute x9, waiting for transfers between devices, shifted(): lax.ppermute(value, axis, [(i, (i + steps) % count) for i in range(count)])  15.7 us
    ppermute x2, starting transfers between devices, swapped(): return lax.ppermute(value, axis, [(0, 1), (1, 0)])  9.34 us
    all_to_all x3, waiting for transfers between devices, exchange(): return lax.all_to_all(pieces, axes, split_axis=0, concat_axis=0, tiled=True)  7.36 us
    pallas_call x1, Pallas kernels, whole(): pl.pallas_call(weights_body, in_specs=[pl.BlockSpec(memory_space=pltpu.VM...  5.82 us
  transfers between devices with their start and end apart: 14, of which 6 were waited for; matrix products, arithmetic and copies ran while one was open for 2% of the time, Pallas kernels for 11%

profile of v4, /device:TPU:8, one launch (start us, length us, event | category | flops | bytes accessed | tf_op | source)
XLA Modules:
  0.0 229.7 jit_solution(1476695832474947589)
XLA Ops:
  0.6 2.5 %pack_grads.1 = bf16[2,8,16,2688]{3,2,1,0:T(8,128)(2,1)} custom-call(f32[1,8]{1,0:T(1,128)} %weights.2, bf16[128,5120]{1,0:T(8,128)(2,1)} %bitcast.41), custom_call_target="tpu_custom_call" | custom-call | tf_op jit(solution)/shard_map/pack_grads/pallas_call | solution.py:234
  3.2 57.1 %all_to_all.24 = bf16[16,16,2688]{2,1,0:T(8,128)(2,1)S(1)} all-to-all(bf16[16,16,2688]{2,1,0:T(8,128)(2,1)} %bitcast.35), channel_id=1, replica_groups=mesh['zl'=4,'yh'=2,'r'=8,'x'=4,'zh'=2] {'zh','zl','yh'}, dimensions={0} | all-to-all | bytes 2752512 | tf_op jit(solution)/shard_map/all_to_all | solution.py:29
  61.4 4.0 %mix.1.mixed = bf16[8,2,16,2560]{3,2,1,0:T(8,128)(2,1)} custom-call(f32[8,8]{1,0:T(8,128)} %convert_reduce_fusion.coef, bf16[2,8,16,2688]{3,2,1,0:T(8,128)(2,1)} %bitcast.32), custom_call_target="tpu_custom_call" | custom-call | tf_op jit(solution)/shard_map/mix/pallas_call | solution.py:270
  65.4 4.3 %all-to-all-start.1 = ((bf16[8,2,16,2560]{3,2,1,0:T(8,128)(2,1)}), bf16[8,2,16,2560]{3,2,1,0:T(8,128)(2,1)S(1)}, u32[]{:S(2)}, u32[]{:S(2)}) async-start(bf16[8,2,16,2560]{3,2,1,0:T(8,128)(2,1)} %mix.1.mixed), calls=%async_computation.1 | async-start | bytes 2621440 | tf_op jit(solution)/shard_map/all_to_all | solution.py:29
  70.2 3.0 %pack_inputs.1 = (bf16[128,3072]{1,0:T(8,128)(2,1)}, bf16[128,3072]{1,0:T(8,128)(2,1)}) custom-call(s32[2]{0:T(128)} %pad_add_fusion.place, bf16[128,5120]{1,0:T(8,128)(2,1)} %bitcast.42, bf16[128,384]{1,0:T(8,128)(2,1)} %bitcast.50), custom_call_target="tpu_custom_call" | custom-call | tf_op jit(solution)/shard_map/pack_inputs/pallas_call | solution.py:245
  73.2 5.2 %collective-permute-start = (bf16[128,3072]{1,0:T(8,128)(2,1)}, bf16[128,3072]{1,0:T(8,128)(2,1)S(1)}, u32[]{:S(2)}, u32[]{:S(2)}) collective-permute-start(bf16[128,3072]{1,0:T(8,128)(2,1)} %get-tuple-element.19), channel_id=1, source_target_pairs={{0,1},{1,0},{2,3},{3,2},{4,5},{5,4},{6,7},{7,6},{8,9},{9,8},{10,11... | collective-permute-start | bytes 2359304 | tf_op jit(solution)/shard_map/ppermute | solution.py:33
  78.4 3.4 %collective-permute-start.1 = (bf16[384,640]{1,0:T(8,128)(2,1)S(1)}, bf16[384,640]{1,0:T(8,128)(2,1)S(1)}, u32[]{:S(2)}, u32[]{:S(2)}) collective-permute-start(bf16[384,640]{1,0:T(8,128)(2,1)S(1)} %bitcast.44), channel_id=1, source_target_pairs={{0,2},{2,4},{4,6},{6,0},{1,3},{3,5},{5,7},{7,1},{8,10},{10,12},{12... | collective-permute-start | bytes 1474568 | tf_op jit(solution)/shard_map/ppermute | solution.py:38
  81.8 4.6 %collective-permute-start.2 = (bf16[384,640]{1,0:T(8,128)(2,1)S(1)}, bf16[384,640]{1,0:T(8,128)(2,1)S(1)}, u32[]{:S(2)}, u32[]{:S(2)}) collective-permute-start(bf16[384,640]{1,0:T(8,128)(2,1)S(1)} %bitcast.45), channel_id=1, source_target_pairs={{0,4},{2,6},{4,0},{6,2},{1,5},{3,7},{5,1},{7,3},{8,12},{10,14},{12... | collective-permute-start | bytes 1474568 | tf_op jit(solution)/shard_map/ppermute | solution.py:38
  86.5 3.3 %collective-permute-start.3 = (bf16[384,640]{1,0:T(8,128)(2,1)S(1)}, bf16[384,640]{1,0:T(8,128)(2,1)}, u32[]{:S(2)}, u32[]{:S(2)}) collective-permute-start(bf16[384,640]{1,0:T(8,128)(2,1)S(1)} %bitcast.46), channel_id=1, source_target_pairs={{0,6},{2,0},{4,2},{6,4},{1,7},{3,1},{5,3},{7,5},{8,14},{10,8},{12,... | collective-permute-start | bytes 1474568 | tf_op jit(solution)/shard_map/ppermute | solution.py:38
  89.8 4.8 %collective-permute-done.1.up_1 = bf16[384,640]{1,0:T(8,128)(2,1)S(1)} collective-permute-done((bf16[384,640]{1,0:T(8,128)(2,1)S(1)}, bf16[384,640]{1,0:T(8,128)(2,1)S(1)}, u32[]{:S(2)}, u32[]{:S(2)}) %collective-permute-start.1) | collective-permute-done | bytes 491552 | tf_op jit(solution)/shard_map/ppermute | solution.py:38
  94.6 10.0 %collective-permute-done.2.up_2 = bf16[384,640]{1,0:T(8,128)(2,1)S(1)} collective-permute-done((bf16[384,640]{1,0:T(8,128)(2,1)S(1)}, bf16[384,640]{1,0:T(8,128)(2,1)S(1)}, u32[]{:S(2)}, u32[]{:S(2)}) %collective-permute-start.2) | collective-permute-done | bytes 491552 | tf_op jit(solution)/shard_map/ppermute | solution.py:38
  105.4 0.9 collective-permute-done.3.up_3
  106.3 3.6 %up_rows.1.up_half = bf16[384,2560]{1,0:T(8,128)(2,1)} custom-call(s32[2]{0:T(128)} %pad_add_fusion.place, bf16[384,640]{1,0:T(8,128)(2,1)} %bitcast.43, bf16[384,640]{1,0:T(8,128)(2,1)} %copy-done.9, bf16[384,640]{1,0:T(8,128)(2,1)} %copy-done.10, bf16[384,640]{1,0:T(8,128)(2,1)} %collective-permute-done.3.up_3), custom_call_target="tpu_custom_call" | custom-call | tf_op jit(solution)/shard_map/up_rows/pallas_call | solution.py:258
  109.8 21.2 %collective-permute-done = bf16[128,3072]{1,0:T(8,128)(2,1)S(1)} collective-permute-done((bf16[128,3072]{1,0:T(8,128)(2,1)}, bf16[128,3072]{1,0:T(8,128)(2,1)S(1)}, u32[]{:S(2)}, u32[]{:S(2)}) %collective-permute-start) | collective-permute-done | bytes 786464 | tf_op jit(solution)/shard_map/ppermute | solution.py:33
  131.9 5.4 %lift.1 = (bf16[8,2,16,2560]{3,2,1,0:T(8,128)(2,1)}, bf16[4,8,2,16,1024]{4,3,2,1,0:T(8,128)(2,1)}, f32[8,2,16,384]{3,2,1,0:T(8,128)}) custom-call(s32[2]{0:T(128)} %pad_add_fusion.place, bf16[8,16,3072]{2,1,0:T(8,128)(2,1)} %bitcast.36, bf16[8,16,3072]{2,1,0:T(8,128)(2,1)} %bitcast.38, bf16[8,16,3072]{2,1,0:T(8,128)(2,1)} %bitcast.37, ...), custom_call_target="tpu_custom_call" | custom-call | tf_op jit(solution)/shard_map/lift/pallas_call | solution.py:284
  137.4 10.3 %all-to-all-start.2 = ((bf16[8,2,16,2560]{3,2,1,0:T(8,128)(2,1)}), bf16[8,2,16,2560]{3,2,1,0:T(8,128)(2,1)S(1)}, u32[]{:S(2)}, u32[]{:S(2)}) async-start(bf16[8,2,16,2560]{3,2,1,0:T(8,128)(2,1)} %get-tuple-element.31), calls=%async_computation.2 | async-start | bytes 2621440 | tf_op jit(solution)/shard_map/all_to_all | solution.py:29
  147.7 3.0 %dynamic-slice_bitcast_fusion = (bf16[256,1024]{1,0:T(8,128)(2,1)}, bf16[256,1024]{1,0:T(8,128)(2,1)}, bf16[256,1024]{1,0:T(8,128)(2,1)}, bf16[256,1024]{1,0:T(8,128)(2,1)}) fusion(bf16[4,256,1024]{2,1,0:T(8,128)(2,1)} %bitcast.40, s32[]{:T(128)S(6)} %select_n.34, s32[]{:T(128)S(6)} %select_n.32, s32[]{:T(128)S(6)} %select_n.30, s32[]{:T(128)S(6)} %select_n.28), kind=kLoop, calls=%fused_computation | loop fusion | bytes 4194320 | tf_op jit(solution)/shard_map/jit(dynamic_index_in_dim)/squeeze | solution.py:308
  150.8 3.4 %collective-permute-start.4 = (bf16[256,1024]{1,0:T(8,128)(2,1)}, bf16[256,1024]{1,0:T(8,128)(2,1)S(1)}, u32[]{:S(2)}, u32[]{:S(2)}) collective-permute-start(bf16[256,1024]{1,0:T(8,128)(2,1)} %get-tuple-element.34), channel_id=1, source_target_pairs={{0,2},{2,4},{4,6},{6,0},{1,3},{3,5},{5,7},{7,1},{8,10},{10,12},{12... | collective-permute-start | bytes 1572872 | tf_op jit(solution)/shard_map/ppermute | solution.py:38
  154.2 1.6 fusion
  155.8 4.1 %collective-permute-start.7 = (bf16[256,384]{1,0:T(8,128)(2,1)S(1)}, bf16[256,384]{1,0:T(8,128)(2,1)S(1)}, u32[]{:S(2)}, u32[]{:S(2)}) collective-permute-start(bf16[256,384]{1,0:T(8,128)(2,1)S(1)} %get-tuple-element.36), channel_id=1, source_target_pairs={{0,1},{1,0},{2,3},{3,2},{4,5},{5,4},{6,7},{7,6},{8,9},{9,8},{10,11... | collective-permute-start | bytes 589832 | tf_op jit(solution)/shard_map/ppermute | solution.py:33
  159.9 4.6 %collective-permute-start.5 = (bf16[256,1024]{1,0:T(8,128)(2,1)}, bf16[256,1024]{1,0:T(8,128)(2,1)S(1)}, u32[]{:S(2)}, u32[]{:S(2)}) collective-permute-start(bf16[256,1024]{1,0:T(8,128)(2,1)} %get-tuple-element.33), channel_id=1, source_target_pairs={{0,4},{2,6},{4,0},{6,2},{1,5},{3,7},{5,1},{7,3},{8,12},{10,14},{12... | collective-permute-start | bytes 1572872 | tf_op jit(solution)/shard_map/ppermute | solution.py:38
  164.5 3.3 %collective-permute-start.6 = (bf16[256,1024]{1,0:T(8,128)(2,1)}, bf16[256,1024]{1,0:T(8,128)(2,1)S(1)}, u32[]{:S(2)}, u32[]{:S(2)}) collective-permute-start(bf16[256,1024]{1,0:T(8,128)(2,1)} %get-tuple-element.32), channel_id=1, source_target_pairs={{0,6},{2,0},{4,2},{6,4},{1,7},{3,1},{5,3},{7,5},{8,14},{10,8},{12,... | collective-permute-start | bytes 1572872 | tf_op jit(solution)/shard_map/ppermute | solution.py:38
  167.9 17.5 %collective-permute-done.7.other = bf16[256,384]{1,0:T(8,128)(2,1)S(1)} collective-permute-done((bf16[256,384]{1,0:T(8,128)(2,1)S(1)}, bf16[256,384]{1,0:T(8,128)(2,1)S(1)}, u32[]{:S(2)}, u32[]{:S(2)}) %collective-permute-start.7) | collective-permute-done | bytes 196640 | tf_op jit(solution)/shard_map/ppermute | solution.py:33
  186.1 3.1 %share.1 = (bf16[256,1024]{1,0:T(8,128)(2,1)}, bf16[256,1024]{1,0:T(8,128)(2,1)}, bf16[256,1024]{1,0:T(8,128)(2,1)}, bf16[256,1024]{1,0:T(8,128)(2,1)}) custom-call(s32[2]{0:T(128)} %pad_add_fusion.place, bf16[8,2,16,2560]{3,2,1,0:T(8,128)(2,1)} %copy-done.2, f32[256,384]{1,0:T(8,128)} %get-tuple-element.37.partial, bf16[256,384]{1,0:T(8,128)(2,1)} %copy-done.11, ...), custom_call_target="tpu_custom_call" | custom-call | tf_op jit(solution)/shard_map/share/pallas_call | solution.py:318
  189.2 4.3 %collective-permute-start.10 = (bf16[256,1024]{1,0:T(8,128)(2,1)}, bf16[256,1024]{1,0:T(8,128)(2,1)}, u32[]{:S(2)}, u32[]{:S(2)}) collective-permute-start(bf16[256,1024]{1,0:T(8,128)(2,1)} %get-tuple-element.27), channel_id=1, source_target_pairs={{0,6},{2,0},{4,2},{6,4},{1,7},{3,1},{5,3},{7,5},{8,14},{10,8},{12,... | collective-permute-start | bytes 1572872 | tf_op jit(solution)/shard_map/ppermute | solution.py:38
  193.5 1.9 collective-permute-start.8
  195.5 4.4 %collective-permute-start.9 = (bf16[256,1024]{1,0:T(8,128)(2,1)}, bf16[256,1024]{1,0:T(8,128)(2,1)}, u32[]{:S(2)}, u32[]{:S(2)}) collective-permute-start(bf16[256,1024]{1,0:T(8,128)(2,1)} %get-tuple-element.26), channel_id=1, source_target_pairs={{0,4},{2,6},{4,0},{6,2},{1,5},{3,7},{5,1},{7,3},{8,12},{10,14},{12... | collective-permute-start | bytes 1572872 | tf_op jit(solution)/shard_map/ppermute | solution.py:38
  199.9 1.1 copy-done.3
  201.0 3.8 %gram.1 = f32[64,128]{1,0:T(8,128)} custom-call(bf16[2,8,16,2688]{3,2,1,0:T(8,128)(2,1)} %bitcast.33, bf16[8,2,16,2560]{3,2,1,0:T(8,128)(2,1)} %copy-done.3), custom_call_target="tpu_custom_call" | custom-call | tf_op jit(solution)/shard_map/gram/pallas_call | solution.py:328
  204.7 10.2 %all-to-all-start.3 = ((f32[64,1,128]{2,1,0:T(1,128)}), f32[64,1,128]{2,1,0:T(1,128)S(1)}, u32[]{:S(2)}, u32[]{:S(2)}) async-start(f32[64,1,128]{2,1,0:T(1,128)} %bitcast.49), calls=%async_computation.3 | async-start | bytes 65536 | tf_op jit(solution)/shard_map/all_to_all | solution.py:29
  216.0 5.8 %weights.3 = (bf16[384,640]{1,0:T(8,128)(2,1)}, bf16[640,384]{1,0:T(8,128)(2,1)}, f32[1,640]{1,0:T(1,128)}) custom-call(bf16[256,1024]{1,0:T(8,128)(2,1)} %get-tuple-element.35.refs_0_, bf16[256,1024]{1,0:T(8,128)(2,1)} %copy-done.5, bf16[256,1024]{1,0:T(8,128)(2,1)} %copy-done.6, bf16[256,1024]{1,0:T(8,128)(2,1)} %copy-done.7, ...), custom_call_target="tpu_custom_call" | custom-call | tf_op jit(solution)/shard_map/weights/pallas_call | solution.py:339
  221.8 7.4 %all-to-all-done.3 = f32[64,1,128]{2,1,0:T(1,128)S(1)} async-done(((f32[64,1,128]{2,1,0:T(1,128)}), f32[64,1,128]{2,1,0:T(1,128)S(1)}, u32[]{:S(2)}, u32[]{:S(2)}) %all-to-all-start.3) | async-done | bytes 32800 | tf_op jit(solution)/shard_map/all_to_all | solution.py:29
  (35 shorter events, 5.6 us)
Async XLA Ops:
  60.3 1.1 copy-start.1
  65.4 13.0 %copy-start.8 = (bf16[1,384,640]{2,1,0:T(8,128)(2,1)S(1)}, bf16[1,384,640]{2,1,0:T(8,128)(2,1)}, u32[]{:S(2)}) copy-start(bf16[1,384,640]{2,1,0:T(8,128)(2,1)} %param.11) | copy-start | bytes 1474564
  65.4 72.0 %all-to-all-start.1 = ((bf16[8,2,16,2560]{3,2,1,0:T(8,128)(2,1)}), bf16[8,2,16,2560]{3,2,1,0:T(8,128)(2,1)S(1)}, u32[]{:S(2)}, u32[]{:S(2)}) async-start(bf16[8,2,16,2560]{3,2,1,0:T(8,128)(2,1)} %mix.1.mixed), calls=%async_computation.1 | async-start | bytes 2621440 | tf_op jit(solution)/shard_map/all_to_all | solution.py:29
  73.2 57.9 %collective-permute-start = (bf16[128,3072]{1,0:T(8,128)(2,1)}, bf16[128,3072]{1,0:T(8,128)(2,1)S(1)}, u32[]{:S(2)}, u32[]{:S(2)}) collective-permute-start(bf16[128,3072]{1,0:T(8,128)(2,1)} %get-tuple-element.19), channel_id=1, source_target_pairs={{0,1},{1,0},{2,3},{3,2},{4,5},{5,4},{6,7},{7,6},{8,9},{9,8},{10,11... | collective-permute-start | bytes 2359304 | tf_op jit(solution)/shard_map/ppermute | solution.py:33
  78.4 16.2 %collective-permute-start.1 = (bf16[384,640]{1,0:T(8,128)(2,1)S(1)}, bf16[384,640]{1,0:T(8,128)(2,1)S(1)}, u32[]{:S(2)}, u32[]{:S(2)}) collective-permute-start(bf16[384,640]{1,0:T(8,128)(2,1)S(1)} %bitcast.44), channel_id=1, source_target_pairs={{0,2},{2,4},{4,6},{6,0},{1,3},{3,5},{5,7},{7,1},{8,10},{10,12},{12... | collective-permute-start | bytes 1474568 | tf_op jit(solution)/shard_map/ppermute | solution.py:38
  81.8 22.8 %collective-permute-start.2 = (bf16[384,640]{1,0:T(8,128)(2,1)S(1)}, bf16[384,640]{1,0:T(8,128)(2,1)S(1)}, u32[]{:S(2)}, u32[]{:S(2)}) collective-permute-start(bf16[384,640]{1,0:T(8,128)(2,1)S(1)} %bitcast.45), channel_id=1, source_target_pairs={{0,4},{2,6},{4,0},{6,2},{1,5},{3,7},{5,1},{7,3},{8,12},{10,14},{12... | collective-permute-start | bytes 1474568 | tf_op jit(solution)/shard_map/ppermute | solution.py:38
  86.5 19.8 %collective-permute-start.3 = (bf16[384,640]{1,0:T(8,128)(2,1)S(1)}, bf16[384,640]{1,0:T(8,128)(2,1)}, u32[]{:S(2)}, u32[]{:S(2)}) collective-permute-start(bf16[384,640]{1,0:T(8,128)(2,1)S(1)} %bitcast.46), channel_id=1, source_target_pairs={{0,6},{2,0},{4,2},{6,4},{1,7},{3,1},{5,3},{7,5},{8,14},{10,8},{12,... | collective-permute-start | bytes 1474568 | tf_op jit(solution)/shard_map/ppermute | solution.py:38
  94.6 11.6 %copy-start.9 = (bf16[384,640]{1,0:T(8,128)(2,1)}, bf16[384,640]{1,0:T(8,128)(2,1)S(1)}, u32[]{:S(2)}) copy-start(bf16[384,640]{1,0:T(8,128)(2,1)S(1)} %collective-permute-done.1.up_1) | copy-start | bytes 1474564
  104.6 0.8 copy-start.10
  131.0 0.9 copy-start.4
  137.4 16.8 %copy-start.2 = (bf16[8,2,16,2560]{3,2,1,0:T(8,128)(2,1)}, bf16[8,2,16,2560]{3,2,1,0:T(8,128)(2,1)S(1)}, u32[]{:S(2)}) copy-start(bf16[8,2,16,2560]{3,2,1,0:T(8,128)(2,1)S(1)} %all-to-all-done.1.grads) | copy-start | bytes 3932164
  137.4 62.5 %all-to-all-start.2 = ((bf16[8,2,16,2560]{3,2,1,0:T(8,128)(2,1)}), bf16[8,2,16,2560]{3,2,1,0:T(8,128)(2,1)S(1)}, u32[]{:S(2)}, u32[]{:S(2)}) async-start(bf16[8,2,16,2560]{3,2,1,0:T(8,128)(2,1)} %get-tuple-element.31), calls=%async_computation.2 | async-start | bytes 2621440 | tf_op jit(solution)/shard_map/all_to_all | solution.py:29
  147.7 6.4 %copy-start = (bf16[384,2560]{1,0:T(8,128)(2,1)S(1)}, bf16[384,2560]{1,0:T(8,128)(2,1)}, u32[]{:S(2)}) copy-start(bf16[384,2560]{1,0:T(8,128)(2,1)} %up_rows.1.up_half) | copy-start | bytes 5898244
  150.8 44.7 %collective-permute-start.4 = (bf16[256,1024]{1,0:T(8,128)(2,1)}, bf16[256,1024]{1,0:T(8,128)(2,1)S(1)}, u32[]{:S(2)}, u32[]{:S(2)}) collective-permute-start(bf16[256,1024]{1,0:T(8,128)(2,1)} %get-tuple-element.34), channel_id=1, source_target_pairs={{0,2},{2,4},{4,6},{6,0},{1,3},{3,5},{5,7},{7,1},{8,10},{10,12},{12... | collective-permute-start | bytes 1572872 | tf_op jit(solution)/shard_map/ppermute | solution.py:38
  155.8 29.6 %collective-permute-start.7 = (bf16[256,384]{1,0:T(8,128)(2,1)S(1)}, bf16[256,384]{1,0:T(8,128)(2,1)S(1)}, u32[]{:S(2)}, u32[]{:S(2)}) collective-permute-start(bf16[256,384]{1,0:T(8,128)(2,1)S(1)} %get-tuple-element.36), channel_id=1, source_target_pairs={{0,1},{1,0},{2,3},{3,2},{4,5},{5,4},{6,7},{7,6},{8,9},{9,8},{10,11... | collective-permute-start | bytes 589832 | tf_op jit(solution)/shard_map/ppermute | solution.py:33
  159.9 55.1 %collective-permute-start.5 = (bf16[256,1024]{1,0:T(8,128)(2,1)}, bf16[256,1024]{1,0:T(8,128)(2,1)S(1)}, u32[]{:S(2)}, u32[]{:S(2)}) collective-permute-start(bf16[256,1024]{1,0:T(8,128)(2,1)} %get-tuple-element.33), channel_id=1, source_target_pairs={{0,4},{2,6},{4,0},{6,2},{1,5},{3,7},{5,1},{7,3},{8,12},{10,14},{12... | collective-permute-start | bytes 1572872 | tf_op jit(solution)/shard_map/ppermute | solution.py:38
  164.5 50.5 %collective-permute-start.6 = (bf16[256,1024]{1,0:T(8,128)(2,1)}, bf16[256,1024]{1,0:T(8,128)(2,1)S(1)}, u32[]{:S(2)}, u32[]{:S(2)}) collective-permute-start(bf16[256,1024]{1,0:T(8,128)(2,1)} %get-tuple-element.32), channel_id=1, source_target_pairs={{0,6},{2,0},{4,2},{6,4},{1,7},{3,1},{5,3},{7,5},{8,14},{10,8},{12,... | collective-permute-start | bytes 1572872 | tf_op jit(solution)/shard_map/ppermute | solution.py:38
  185.4 0.7 copy-start.11
  189.2 25.9 %collective-permute-start.10 = (bf16[256,1024]{1,0:T(8,128)(2,1)}, bf16[256,1024]{1,0:T(8,128)(2,1)}, u32[]{:S(2)}, u32[]{:S(2)}) collective-permute-start(bf16[256,1024]{1,0:T(8,128)(2,1)} %get-tuple-element.27), channel_id=1, source_target_pairs={{0,6},{2,0},{4,2},{6,4},{1,7},{3,1},{5,3},{7,5},{8,14},{10,8},{12,... | collective-permute-start | bytes 1572872 | tf_op jit(solution)/shard_map/ppermute | solution.py:38
  193.5 21.5 %collective-permute-start.8 = (bf16[256,1024]{1,0:T(8,128)(2,1)}, bf16[256,1024]{1,0:T(8,128)(2,1)}, u32[]{:S(2)}, u32[]{:S(2)}) collective-permute-start(bf16[256,1024]{1,0:T(8,128)(2,1)} %get-tuple-element.25), channel_id=1, source_target_pairs={{0,2},{2,4},{4,6},{6,0},{1,3},{3,5},{5,7},{7,1},{8,10},{10,12},{12... | collective-permute-start | bytes 1572872 | tf_op jit(solution)/shard_map/ppermute | solution.py:38
  195.4 19.6 %copy-start.5 = (bf16[256,1024]{1,0:T(8,128)(2,1)}, bf16[256,1024]{1,0:T(8,128)(2,1)S(1)}, u32[]{:S(2)}) copy-start(bf16[256,1024]{1,0:T(8,128)(2,1)S(1)} %collective-permute-done.4.refs_1_) | copy-start | bytes 1572868
  195.5 19.6 %collective-permute-start.9 = (bf16[256,1024]{1,0:T(8,128)(2,1)}, bf16[256,1024]{1,0:T(8,128)(2,1)}, u32[]{:S(2)}, u32[]{:S(2)}) collective-permute-start(bf16[256,1024]{1,0:T(8,128)(2,1)} %get-tuple-element.26), channel_id=1, source_target_pairs={{0,4},{2,6},{4,0},{6,2},{1,5},{3,7},{5,1},{7,3},{8,12},{10,14},{12... | collective-permute-start | bytes 1572872 | tf_op jit(solution)/shard_map/ppermute | solution.py:38
  199.9 1.1 copy-start.3
  204.7 24.4 %all-to-all-start.3 = ((f32[64,1,128]{2,1,0:T(1,128)}), f32[64,1,128]{2,1,0:T(1,128)S(1)}, u32[]{:S(2)}, u32[]{:S(2)}) async-start(f32[64,1,128]{2,1,0:T(1,128)} %bitcast.49), calls=%async_computation.3 | async-start | bytes 65536 | tf_op jit(solution)/shard_map/all_to_all | solution.py:29
  215.0 0.8 copy-start.6
  215.0 1.0 copy-start.7

commit v5 on v4

--- a/solution.py
+++ b/solution.py
@@ -72,10 +72,9 @@
             out[half, k, :, cols - LANES :] = tail
 
 
-def pack_inputs_body(place, layer_in, latent, kept, sent):
-    tokens, cols = kept.shape
+def pack_inputs_body(place, layer_in, latent, kept, sent, rest):
+    tokens, half_cols = kept.shape
     ranks = latent.shape[1]
-    half_cols = cols - ranks - LANES
     width = layer_in.shape[1]
     block = BLOCK
     first = place[0] == 0
@@ -88,15 +87,13 @@
     tail = jnp.zeros((tokens, LANES), jnp.float32)
     for i, term in enumerate(split_terms(jnp.broadcast_to(inv_rms, (tokens, LANES)))):
         tail = jnp.where(lane == i, term, tail)
-    tail = tail.astype(jnp.bfloat16)
     for i in range(half_cols // block):
         low = layer_in[:, 2 * i * block : (2 * i + 1) * block]
         high = layer_in[:, (2 * i + 1) * block : (2 * i + 2) * block]
         kept[:, i * block : (i + 1) * block] = jnp.where(first, low, high)
         sent[:, i * block : (i + 1) * block] = jnp.where(first, high, low)
-    for out in (kept, sent):
-        out[:, half_cols : half_cols + ranks] = latent[...]
-        out[:, half_cols + ranks :] = tail
+    rest[:, :ranks] = latent[...]
+    rest[:, ranks:] = tail.astype(jnp.bfloat16)
 
 
 def up_rows_body(place, up_0, up_1, up_2, up_3, out):
@@ -149,40 +146,45 @@
 
 
 def gram_body(grads, outs, result, kept):
-    halves, sections, _, cols = grads.shape
-    sums = {}
-    for half in range(halves):
-        for at in range(0, cols, LANES):
-            lanes = slice(at, at + LANES)
-            left = [outs[k, half, :, lanes].astype(jnp.float32) for k in range(sections)]
-            right = [grads[half, k, :, lanes].astype(jnp.float32) for k in range(sections)]
-            for k in range(sections):
-                for m in range(sections - k):
-                    product = left[k] * right[k + m]
-                    folded = product[:8] + product[8:]
-                    sums[k, m] = folded if (k, m) not in sums else sums[k, m] + folded
-
-    last = pl.num_programs(0) - 1
+    halves, sections, rows, cols = grads.shape
+    total = jnp.zeros(kept.shape, jnp.float32)
+    for half in range(halves):
+        total = total + lax.dot_general(
+            outs[:, half].reshape(sections * rows, cols),
+            grads[half].reshape(sections * rows, cols),
+            (((1,), (1,)), ((), ())),
+            preferred_element_type=jnp.float32,
+        )
 
     @pl.when(pl.program_id(0) == 0)
     def _():
-        for (k, m), total in sums.items():
-            kept[k * MIXES + m] = total
+        kept[...] = total
 
     @pl.when(pl.program_id(0) != 0)
     def _():
-        for (k, m), total in sums.items():
-            kept[k * MIXES + m] += total
-
-    @pl.when(pl.program_id(0) == last)
+        kept[...] += total
+
+    @pl.when(pl.program_id(0) == pl.num_programs(0) - 1)
     def _():
-        lane = lax.broadcasted_iota(jnp.int32, (1, LANES), 1)
+        row = lax.broadcasted_iota(jnp.int32, kept.shape, 0)
+        lane = lax.broadcasted_iota(jnp.int32, kept.shape, 1)
+        same = jnp.where(lax.rem(row, rows) == lax.rem(lane, rows), kept[...], 0.0)
         share = result.shape[0] // sections
+        spread = []
         for k in range(sections):
-            row = jnp.zeros((1, LANES), jnp.float32)
-            for m in range(sections - k):
-                row = jnp.where(lane == m, jnp.sum(kept[k * MIXES + m], keepdims=True), row)
-            result[k * share : (k + 1) * share] = jnp.broadcast_to(row, (share, LANES))
+            sums = jnp.sum(same[k * rows : (k + 1) * rows], axis=0, keepdims=True)
+            sums = jnp.broadcast_to(sums, (share, LANES))
+            if k:
+                sums = pltpu.roll(sums, LANES - k * rows, 1)
+                sums = jnp.where(lane[:share] < LANES - k * rows, sums, 0.0)
+            spread.append(sums)
+        gather = jnp.where(lax.div(row, rows) == lane, 1.0, 0.0)
+        result[...] = jnp.dot(
+            jnp.concatenate(spread, axis=0),
+            gather,
+            precision=lax.Precision.HIGHEST,
+            preferred_element_type=jnp.float32,
+        )
 
 
 def share_body(place, grads, partial, other, scale, *outs):
@@ -233,22 +235,25 @@
 
     packed = pl.pallas_call(
         pack_grads_body,
-        in_specs=[SMEM, pl.BlockSpec((tokens, width), lambda: (0, 0))],
-        out_specs=pl.BlockSpec((zs, sections, rows, half_width + LANES), lambda: (0, 0, 0, 0)),
+        grid=(4,),
+        in_specs=[SMEM, pl.BlockSpec((tokens // 4, width), lambda i: (i, 0))],
+        out_specs=pl.BlockSpec((zs, sections // 4, rows, half_width + LANES), lambda i: (0, i, 0, 0)),
         out_shape=shape((zs, sections, rows, half_width + LANES)),
         name="pack_grads",
     )(mix_weight, mix_grad)
     grads = exchange(packed.reshape(zs * sections, rows, half_width + LANES), ("zh", *GROUP))
     grads = grads.reshape(zs, sections, rows, half_width + LANES)
 
-    full = half_width + ranks + LANES
-    kept, sent = pl.pallas_call(
+    rest = ranks + LANES
+    kept, sent, kept_rest = pl.pallas_call(
         pack_inputs_body,
         in_specs=[SMEM, pl.BlockSpec((tokens, width), lambda: (0, 0)), pl.BlockSpec((tokens, ranks), lambda: (0, 0))],
-        out_specs=[pl.BlockSpec((tokens, full), lambda: (0, 0))] * 2,
-        out_shape=[shape((tokens, full))] * 2,
+        out_specs=[pl.BlockSpec((tokens, half_width), lambda: (0, 0))] * 2
+        + [pl.BlockSpec((tokens, rest), lambda: (0, 0))],
+        out_shape=[shape((tokens, half_width))] * 2 + [shape((tokens, rest))],
         name="pack_inputs",
     )(place, layer_in, latent)
+    other_rest = swapped(kept_rest, "zh")
     other = swapped(sent, "zh")
 
     up_block = up_proj[0]
@@ -277,10 +282,11 @@
     )(weights, grads)
     arrived = exchange(mixed, GROUP)
 
-    kept, other = [t.reshape(sections, rows, full) for t in (kept, other)]
+    kept, other, kept_rest, other_rest = [
+        t.reshape(sections, rows, t.shape[1]) for t in (kept, other, kept_rest, other_rest)
+    ]
     wide = pl.BlockSpec((sections, rows, block), lambda a: (0, 0, a))
-    rest = ranks + LANES
-    narrow = pl.BlockSpec((sections, rows, rest), lambda a: (0, 0, half_width // rest))
+    narrow = pl.BlockSpec((sections, rows, rest), lambda a: (0, 0, 0))
     layer_out, moves, scale = pl.pallas_call(
         lift_body,
         grid=(xs,),
@@ -298,7 +304,7 @@
         ],
         scratch_shapes=[pltpu.VMEM((sections, zs, rows, ranks), jnp.bfloat16)],
         name="lift",
-    )(place, kept, other, kept, other, up_half, mixed)
+    )(place, kept, other, kept_rest, other_rest, up_half, mixed)
     scale = scale.reshape(zs * tokens, ranks)
 
     moves = moves.reshape(xs, zs * tokens, block + ranks)
@@ -322,7 +328,9 @@
         out_shape=[piece] * xs,
         name="share",
     )(place, arrived, act_partial, act_other, scale)
-    shares = [shares[0]] + [shifted(shares[step], "x", step) for step in range(1, xs)]
+    shares = list(shares)
+    for step in range(1, xs):
+        shares[step] = shifted(shares[step], "x", step)
 
     everyone = sections * xs * zs
     products = pl.pallas_call(
@@ -331,7 +339,7 @@
         in_specs=[grads_spec, chunk_spec],
         out_specs=pl.BlockSpec((everyone, LANES), lambda a: (0, 0)),
         out_shape=shape((everyone, LANES), jnp.float32),
-        scratch_shapes=[pltpu.VMEM((sections * MIXES, 8, LANES), jnp.float32)],
+        scratch_shapes=[pltpu.VMEM((sections * rows, LANES), jnp.float32)],
         name="gram",
     )(grads, outs)
     mixing = exchange(products, (*GROUP, "x", "zh")).sum(axis=0)[:MIXES]

time: 231 us -> 232 us (level)
  starting transfers between devices: 67.6 us -> 72.5 us
  waiting for transfers between devices: 61.7 us -> 57.4 us
    ppermute x2 -> x3, starting transfers between devices: 9.34 us -> 13.9 us  [swapped(): return lax.ppermute(value, axis, [(0, 1), (1, 0)])]
    ppermute x9, waiting for transfers between devices: 15.7 us -> 11.1 us  [shifted(): lax.ppermute(value, axis, [(i, (i + steps) % count) for i in range(count)])]
    ppermute x2 -> x3, waiting for transfers between devices: 38.7 us -> 38.8 us  [swapped(): return lax.ppermute(value, axis, [(0, 1), (1, 0)])]
    unnamed x24 -> x26, local copies, waits for them, and re-layouts: 4.8 us -> 4.81 us
  transfers between devices with their start and end apart: 14 -> 15, of which waited for: 6 -> 6; matrix products, arithmetic and copies ran while one was open for 2% -> 2% of each run, Pallas kernels for 11% -> 11%
where the time goes in v5:
time: 232 us; the launch traced here: 231 us
  starting transfers between devices  72.5 us (31%)
  waiting for transfers between devices  57.4 us (25%)
  blocking collectives  57.1 us (25%)
  Pallas kernels  32.2 us (14%)
  local copies, waits for them, and re-layouts  8.4 us (4%)
    all_to_all x1, blocking collectives, exchange(): return lax.all_to_all(pieces, axes, split_axis=0, concat_axis=0, tiled=True)  57.1 us
    ppermute x3, waiting for transfers between devices, swapped(): return lax.ppermute(value, axis, [(0, 1), (1, 0)])  38.8 us
    ppermute x9, starting transfers between devices, shifted(): lax.ppermute(value, axis, [(i, (i + steps) % count) for i in range(count)])  33.4 us
    all_to_all x3, starting transfers between devices, exchange(): return lax.all_to_all(pieces, axes, split_axis=0, concat_axis=0, tiled=True)  25.3 us
    ppermute x3, starting transfers between devices, swapped(): return lax.ppermute(value, axis, [(0, 1), (1, 0)])  13.9 us
    ppermute x9, waiting for transfers between devices, shifted(): lax.ppermute(value, axis, [(i, (i + steps) % count) for i in range(count)])  11.1 us
    all_to_all x3, waiting for transfers between devices, exchange(): return lax.all_to_all(pieces, axes, split_axis=0, concat_axis=0, tiled=True)  7.38 us
    pallas_call x1, Pallas kernels, whole(): pl.pallas_call(weights_body, in_specs=[pl.BlockSpec(memory_space=pltpu.VM...  5.82 us
  transfers between devices with their start and end apart: 15, of which 6 were waited for; matrix products, arithmetic and copies ran while one was open for 2% of the time, Pallas kernels for 11%

profile of v5, /device:TPU:8, one launch (start us, length us, event | category | flops | bytes accessed | tf_op | source)
XLA Modules:
  0.0 231.4 jit_solution(17414266615727232220)
XLA Ops:
  0.6 3.5 %pack_grads.1 = bf16[2,8,16,2688]{3,2,1,0:T(8,128)(2,1)} custom-call(f32[1,8]{1,0:T(1,128)} %weights.2, bf16[128,5120]{1,0:T(8,128)(2,1)} %bitcast.39), custom_call_target="tpu_custom_call" | custom-call | tf_op jit(solution)/shard_map/pack_grads/pallas_call | solution.py:236
  4.2 57.1 %all_to_all.24 = bf16[16,16,2688]{2,1,0:T(8,128)(2,1)S(1)} all-to-all(bf16[16,16,2688]{2,1,0:T(8,128)(2,1)} %bitcast.37), channel_id=1, replica_groups=mesh['zl'=4,'yh'=2,'r'=8,'x'=4,'zh'=2] {'zh','zl','yh'}, dimensions={0} | all-to-all | bytes 2752512 | tf_op jit(solution)/shard_map/all_to_all | solution.py:29
  62.4 4.0 %mix.1.mixed = bf16[8,2,16,2560]{3,2,1,0:T(8,128)(2,1)} custom-call(f32[8,8]{1,0:T(8,128)} %convert_reduce_fusion.coef, bf16[2,8,16,2688]{3,2,1,0:T(8,128)(2,1)} %bitcast.34), custom_call_target="tpu_custom_call" | custom-call | tf_op jit(solution)/shard_map/mix/pallas_call | solution.py:275
  66.4 4.3 %all-to-all-start.1 = ((bf16[8,2,16,2560]{3,2,1,0:T(8,128)(2,1)}), bf16[8,2,16,2560]{3,2,1,0:T(8,128)(2,1)S(1)}, u32[]{:S(2)}, u32[]{:S(2)}) async-start(bf16[8,2,16,2560]{3,2,1,0:T(8,128)(2,1)} %mix.1.mixed), calls=%async_computation.1 | async-start | bytes 2621440 | tf_op jit(solution)/shard_map/all_to_all | solution.py:29
  71.2 2.9 %pack_inputs.1 = (bf16[128,2560]{1,0:T(8,128)(2,1)}, bf16[128,2560]{1,0:T(8,128)(2,1)}, bf16[128,512]{1,0:T(8,128)(2,1)}) custom-call(s32[2]{0:T(128)} %pad_add_fusion.place, bf16[128,5120]{1,0:T(8,128)(2,1)} %bitcast.40, bf16[128,384]{1,0:T(8,128)(2,1)} %bitcast.52), custom_call_target="tpu_custom_call" | custom-call | tf_op jit(solution)/shard_map/pack_inputs/pallas_call | solution.py:248
  74.1 5.2 %collective-permute-start = (bf16[128,2560]{1,0:T(8,128)(2,1)}, bf16[128,2560]{1,0:T(8,128)(2,1)S(1)}, u32[]{:S(2)}, u32[]{:S(2)}) collective-permute-start(bf16[128,2560]{1,0:T(8,128)(2,1)} %get-tuple-element.20), channel_id=1, source_target_pairs={{0,1},{1,0},{2,3},{3,2},{4,5},{5,4},{6,7},{7,6},{8,9},{9,8},{10,11... | collective-permute-start | bytes 1966088 | tf_op jit(solution)/shard_map/ppermute | solution.py:33
  79.3 3.4 %collective-permute-start.2 = (bf16[384,640]{1,0:T(8,128)(2,1)S(1)}, bf16[384,640]{1,0:T(8,128)(2,1)S(1)}, u32[]{:S(2)}, u32[]{:S(2)}) collective-permute-start(bf16[384,640]{1,0:T(8,128)(2,1)S(1)} %bitcast.44), channel_id=1, source_target_pairs={{0,2},{2,4},{4,6},{6,0},{1,3},{3,5},{5,7},{7,1},{8,10},{10,12},{12... | collective-permute-start | bytes 1474568 | tf_op jit(solution)/shard_map/ppermute | solution.py:38
  82.7 4.6 %collective-permute-start.3 = (bf16[384,640]{1,0:T(8,128)(2,1)S(1)}, bf16[384,640]{1,0:T(8,128)(2,1)S(1)}, u32[]{:S(2)}, u32[]{:S(2)}) collective-permute-start(bf16[384,640]{1,0:T(8,128)(2,1)S(1)} %bitcast.45), channel_id=1, source_target_pairs={{0,4},{2,6},{4,0},{6,2},{1,5},{3,7},{5,1},{7,3},{8,12},{10,14},{12... | collective-permute-start | bytes 1474568 | tf_op jit(solution)/shard_map/ppermute | solution.py:38
  87.4 3.3 %collective-permute-start.4 = (bf16[384,640]{1,0:T(8,128)(2,1)S(1)}, bf16[384,640]{1,0:T(8,128)(2,1)}, u32[]{:S(2)}, u32[]{:S(2)}) collective-permute-start(bf16[384,640]{1,0:T(8,128)(2,1)S(1)} %bitcast.46), channel_id=1, source_target_pairs={{0,6},{2,0},{4,2},{6,4},{1,7},{3,1},{5,3},{7,5},{8,14},{10,8},{12,... | collective-permute-start | bytes 1474568 | tf_op jit(solution)/shard_map/ppermute | solution.py:38
  90.7 4.5 %collective-permute-start.1 = (bf16[128,512]{1,0:T(8,128)(2,1)}, bf16[128,512]{1,0:T(8,128)(2,1)S(1)}, u32[]{:S(2)}, u32[]{:S(2)}) collective-permute-start(bf16[128,512]{1,0:T(8,128)(2,1)} %get-tuple-element.21), channel_id=1, source_target_pairs={{0,1},{1,0},{2,3},{3,2},{4,5},{5,4},{6,7},{7,6},{8,9},{9,8},{10,11... | collective-permute-start | bytes 393224 | tf_op jit(solution)/shard_map/ppermute | solution.py:33
  95.5 10.0 %collective-permute-done.3.up_2 = bf16[384,640]{1,0:T(8,128)(2,1)S(1)} collective-permute-done((bf16[384,640]{1,0:T(8,128)(2,1)S(1)}, bf16[384,640]{1,0:T(8,128)(2,1)S(1)}, u32[]{:S(2)}, u32[]{:S(2)}) %collective-permute-start.3) | collective-permute-done | bytes 491552 | tf_op jit(solution)/shard_map/ppermute | solution.py:38
  106.3 0.9 collective-permute-done.4.up_3
  107.2 3.5 %up_rows.1.up_half = bf16[384,2560]{1,0:T(8,128)(2,1)} custom-call(s32[2]{0:T(128)} %pad_add_fusion.place, bf16[384,640]{1,0:T(8,128)(2,1)} %bitcast.43, bf16[384,640]{1,0:T(8,128)(2,1)} %copy-done.9, bf16[384,640]{1,0:T(8,128)(2,1)} %copy-done.10, bf16[384,640]{1,0:T(8,128)(2,1)} %collective-permute-done.4.up_3), custom_call_target="tpu_custom_call" | custom-call | tf_op jit(solution)/shard_map/up_rows/pallas_call | solution.py:263
  110.7 21.3 %collective-permute-done.1 = bf16[128,512]{1,0:T(8,128)(2,1)S(1)} collective-permute-done((bf16[128,512]{1,0:T(8,128)(2,1)}, bf16[128,512]{1,0:T(8,128)(2,1)S(1)}, u32[]{:S(2)}, u32[]{:S(2)}) %collective-permute-start.1) | collective-permute-done | bytes 131104 | tf_op jit(solution)/shard_map/ppermute | solution.py:33
  132.9 5.5 %lift.1 = (bf16[8,2,16,2560]{3,2,1,0:T(8,128)(2,1)}, bf16[4,8,2,16,1024]{4,3,2,1,0:T(8,128)(2,1)}, f32[8,2,16,384]{3,2,1,0:T(8,128)}) custom-call(s32[2]{0:T(128)} %pad_add_fusion.place, bf16[8,16,2560]{2,1,0:T(8,128)(2,1)} %bitcast.41, bf16[8,16,2560]{2,1,0:T(8,128)(2,1)} %bitcast.42, bf16[8,16,512]{2,1,0:T(8,128)(2,1)} %bitcast.50, ...), custom_call_target="tpu_custom_call" | custom-call | tf_op jit(solution)/shard_map/lift/pallas_call | solution.py:290
  138.5 10.3 %all-to-all-start.2 = ((bf16[8,2,16,2560]{3,2,1,0:T(8,128)(2,1)}), bf16[8,2,16,2560]{3,2,1,0:T(8,128)(2,1)S(1)}, u32[]{:S(2)}, u32[]{:S(2)}) async-start(bf16[8,2,16,2560]{3,2,1,0:T(8,128)(2,1)} %get-tuple-element.33), calls=%async_computation.2 | async-start | bytes 2621440 | tf_op jit(solution)/shard_map/all_to_all | solution.py:29
  148.8 3.1 %dynamic-slice_bitcast_fusion = (bf16[256,1024]{1,0:T(8,128)(2,1)}, bf16[256,1024]{1,0:T(8,128)(2,1)}, bf16[256,1024]{1,0:T(8,128)(2,1)}, bf16[256,1024]{1,0:T(8,128)(2,1)}) fusion(bf16[4,256,1024]{2,1,0:T(8,128)(2,1)} %bitcast.38, s32[]{:T(128)S(6)} %select_n.34, s32[]{:T(128)S(6)} %select_n.32, s32[]{:T(128)S(6)} %select_n.30, s32[]{:T(128)S(6)} %select_n.28), kind=kLoop, calls=%fused_computation | loop fusion | bytes 4194320 | tf_op jit(solution)/shard_map/jit(dynamic_index_in_dim)/squeeze | solution.py:314
  151.9 3.4 %collective-permute-start.5 = (bf16[256,1024]{1,0:T(8,128)(2,1)}, bf16[256,1024]{1,0:T(8,128)(2,1)S(1)}, u32[]{:S(2)}, u32[]{:S(2)}) collective-permute-start(bf16[256,1024]{1,0:T(8,128)(2,1)} %get-tuple-element.36), channel_id=1, source_target_pairs={{0,2},{2,4},{4,6},{6,0},{1,3},{3,5},{5,7},{7,1},{8,10},{10,12},{12... | collective-permute-start | bytes 1572872 | tf_op jit(solution)/shard_map/ppermute | solution.py:38
  155.3 1.6 fusion
  156.9 4.1 %collective-permute-start.8 = (bf16[256,384]{1,0:T(8,128)(2,1)S(1)}, bf16[256,384]{1,0:T(8,128)(2,1)S(1)}, u32[]{:S(2)}, u32[]{:S(2)}) collective-permute-start(bf16[256,384]{1,0:T(8,128)(2,1)S(1)} %get-tuple-element.38), channel_id=1, source_target_pairs={{0,1},{1,0},{2,3},{3,2},{4,5},{5,4},{6,7},{7,6},{8,9},{9,8},{10,11... | collective-permute-start | bytes 589832 | tf_op jit(solution)/shard_map/ppermute | solution.py:33
  161.0 4.6 %collective-permute-start.6 = (bf16[256,1024]{1,0:T(8,128)(2,1)}, bf16[256,1024]{1,0:T(8,128)(2,1)S(1)}, u32[]{:S(2)}, u32[]{:S(2)}) collective-permute-start(bf16[256,1024]{1,0:T(8,128)(2,1)} %get-tuple-element.35), channel_id=1, source_target_pairs={{0,4},{2,6},{4,0},{6,2},{1,5},{3,7},{5,1},{7,3},{8,12},{10,14},{12... | collective-permute-start | bytes 1572872 | tf_op jit(solution)/shard_map/ppermute | solution.py:38
  165.7 3.3 %collective-permute-start.7 = (bf16[256,1024]{1,0:T(8,128)(2,1)}, bf16[256,1024]{1,0:T(8,128)(2,1)S(1)}, u32[]{:S(2)}, u32[]{:S(2)}) collective-permute-start(bf16[256,1024]{1,0:T(8,128)(2,1)} %get-tuple-element.34), channel_id=1, source_target_pairs={{0,6},{2,0},{4,2},{6,4},{1,7},{3,1},{5,3},{7,5},{8,14},{10,8},{12,... | collective-permute-start | bytes 1572872 | tf_op jit(solution)/shard_map/ppermute | solution.py:38
  169.0 17.5 %collective-permute-done.8.other = bf16[256,384]{1,0:T(8,128)(2,1)S(1)} collective-permute-done((bf16[256,384]{1,0:T(8,128)(2,1)S(1)}, bf16[256,384]{1,0:T(8,128)(2,1)S(1)}, u32[]{:S(2)}, u32[]{:S(2)}) %collective-permute-start.8) | collective-permute-done | bytes 196640 | tf_op jit(solution)/shard_map/ppermute | solution.py:33
  187.2 3.1 %share.1 = (bf16[256,1024]{1,0:T(8,128)(2,1)}, bf16[256,1024]{1,0:T(8,128)(2,1)}, bf16[256,1024]{1,0:T(8,128)(2,1)}, bf16[256,1024]{1,0:T(8,128)(2,1)}) custom-call(s32[2]{0:T(128)} %pad_add_fusion.place, bf16[8,2,16,2560]{3,2,1,0:T(8,128)(2,1)} %copy-done.2, f32[256,384]{1,0:T(8,128)} %get-tuple-element.39.partial, bf16[256,384]{1,0:T(8,128)(2,1)} %copy-done.11, ...), custom_call_target="tpu_custom_call" | custom-call | tf_op jit(solution)/shard_map/share/pallas_call | solution.py:324
  190.2 4.8 %collective-permute-start.10 = (bf16[256,1024]{1,0:T(8,128)(2,1)}, bf16[256,1024]{1,0:T(8,128)(2,1)}, u32[]{:S(2)}, u32[]{:S(2)}) collective-permute-start(bf16[256,1024]{1,0:T(8,128)(2,1)} %get-tuple-element.28), channel_id=1, source_target_pairs={{0,4},{2,6},{4,0},{6,2},{1,5},{3,7},{5,1},{7,3},{8,12},{10,14},{12... | collective-permute-start | bytes 1572872 | tf_op jit(solution)/shard_map/ppermute | solution.py:38
  195.1 3.2 %collective-permute-start.11 = (bf16[256,1024]{1,0:T(8,128)(2,1)}, bf16[256,1024]{1,0:T(8,128)(2,1)}, u32[]{:S(2)}, u32[]{:S(2)}) collective-permute-start(bf16[256,1024]{1,0:T(8,128)(2,1)} %get-tuple-element.29), channel_id=1, source_target_pairs={{0,6},{2,0},{4,2},{6,4},{1,7},{3,1},{5,3},{7,5},{8,14},{10,8},{12,... | collective-permute-start | bytes 1572872 | tf_op jit(solution)/shard_map/ppermute | solution.py:38
  198.3 2.7 %collective-permute-start.9 = (bf16[256,1024]{1,0:T(8,128)(2,1)}, bf16[256,1024]{1,0:T(8,128)(2,1)}, u32[]{:S(2)}, u32[]{:S(2)}) collective-permute-start(bf16[256,1024]{1,0:T(8,128)(2,1)} %get-tuple-element.27), channel_id=1, source_target_pairs={{0,2},{2,4},{4,6},{6,0},{1,3},{3,5},{5,7},{7,1},{8,10},{10,12},{12... | collective-permute-start | bytes 1572872 | tf_op jit(solution)/shard_map/ppermute | solution.py:38
  201.0 1.1 copy-done.3
  202.0 3.9 %gram.1 = f32[64,128]{1,0:T(8,128)} custom-call(bf16[2,8,16,2688]{3,2,1,0:T(8,128)(2,1)} %bitcast.35, bf16[8,2,16,2560]{3,2,1,0:T(8,128)(2,1)} %copy-done.3), custom_call_target="tpu_custom_call" | custom-call | tf_op jit(solution)/shard_map/gram/pallas_call | solution.py:336
  205.9 10.7 %all-to-all-start.3 = ((f32[64,1,128]{2,1,0:T(1,128)}), f32[64,1,128]{2,1,0:T(1,128)S(1)}, u32[]{:S(2)}, u32[]{:S(2)}) async-start(f32[64,1,128]{2,1,0:T(1,128)} %bitcast.49), calls=%async_computation.3 | async-start | bytes 65536 | tf_op jit(solution)/shard_map/all_to_all | solution.py:29
  217.6 5.8 %weights.3 = (bf16[384,640]{1,0:T(8,128)(2,1)}, bf16[640,384]{1,0:T(8,128)(2,1)}, f32[1,640]{1,0:T(1,128)}) custom-call(bf16[256,1024]{1,0:T(8,128)(2,1)} %get-tuple-element.37.refs_0_, bf16[256,1024]{1,0:T(8,128)(2,1)} %copy-done.5, bf16[256,1024]{1,0:T(8,128)(2,1)} %copy-done.6, bf16[256,1024]{1,0:T(8,128)(2,1)} %copy-done.7, ...), custom_call_target="tpu_custom_call" | custom-call | tf_op jit(solution)/shard_map/weights/pallas_call | solution.py:347
  223.4 7.4 %all-to-all-done.3 = f32[64,1,128]{2,1,0:T(1,128)S(1)} async-done(((f32[64,1,128]{2,1,0:T(1,128)}), f32[64,1,128]{2,1,0:T(1,128)S(1)}, u32[]{:S(2)}, u32[]{:S(2)}) %all-to-all-start.3) | async-done | bytes 32800 | tf_op jit(solution)/shard_map/all_to_all | solution.py:29
  (39 shorter events, 5.9 us)
Async XLA Ops:
  61.3 1.1 copy-start.1
  66.4 12.9 %copy-start.8 = (bf16[1,384,640]{2,1,0:T(8,128)(2,1)S(1)}, bf16[1,384,640]{2,1,0:T(8,128)(2,1)}, u32[]{:S(2)}) copy-start(bf16[1,384,640]{2,1,0:T(8,128)(2,1)} %param.11) | copy-start | bytes 1474564
  66.4 72.1 %all-to-all-start.1 = ((bf16[8,2,16,2560]{3,2,1,0:T(8,128)(2,1)}), bf16[8,2,16,2560]{3,2,1,0:T(8,128)(2,1)S(1)}, u32[]{:S(2)}, u32[]{:S(2)}) async-start(bf16[8,2,16,2560]{3,2,1,0:T(8,128)(2,1)} %mix.1.mixed), calls=%async_computation.1 | async-start | bytes 2621440 | tf_op jit(solution)/shard_map/all_to_all | solution.py:29
  74.1 58.0 %collective-permute-start = (bf16[128,2560]{1,0:T(8,128)(2,1)}, bf16[128,2560]{1,0:T(8,128)(2,1)S(1)}, u32[]{:S(2)}, u32[]{:S(2)}) collective-permute-start(bf16[128,2560]{1,0:T(8,128)(2,1)} %get-tuple-element.20), channel_id=1, source_target_pairs={{0,1},{1,0},{2,3},{3,2},{4,5},{5,4},{6,7},{7,6},{8,9},{9,8},{10,11... | collective-permute-start | bytes 1966088 | tf_op jit(solution)/shard_map/ppermute | solution.py:33
  79.3 16.2 %collective-permute-start.2 = (bf16[384,640]{1,0:T(8,128)(2,1)S(1)}, bf16[384,640]{1,0:T(8,128)(2,1)S(1)}, u32[]{:S(2)}, u32[]{:S(2)}) collective-permute-start(bf16[384,640]{1,0:T(8,128)(2,1)S(1)} %bitcast.44), channel_id=1, source_target_pairs={{0,2},{2,4},{4,6},{6,0},{1,3},{3,5},{5,7},{7,1},{8,10},{10,12},{12... | collective-permute-start | bytes 1474568 | tf_op jit(solution)/shard_map/ppermute | solution.py:38
  82.7 22.8 %collective-permute-start.3 = (bf16[384,640]{1,0:T(8,128)(2,1)S(1)}, bf16[384,640]{1,0:T(8,128)(2,1)S(1)}, u32[]{:S(2)}, u32[]{:S(2)}) collective-permute-start(bf16[384,640]{1,0:T(8,128)(2,1)S(1)} %bitcast.45), channel_id=1, source_target_pairs={{0,4},{2,6},{4,0},{6,2},{1,5},{3,7},{5,1},{7,3},{8,12},{10,14},{12... | collective-permute-start | bytes 1474568 | tf_op jit(solution)/shard_map/ppermute | solution.py:38
  87.4 19.8 %collective-permute-start.4 = (bf16[384,640]{1,0:T(8,128)(2,1)S(1)}, bf16[384,640]{1,0:T(8,128)(2,1)}, u32[]{:S(2)}, u32[]{:S(2)}) collective-permute-start(bf16[384,640]{1,0:T(8,128)(2,1)S(1)} %bitcast.46), channel_id=1, source_target_pairs={{0,6},{2,0},{4,2},{6,4},{1,7},{3,1},{5,3},{7,5},{8,14},{10,8},{12,... | collective-permute-start | bytes 1474568 | tf_op jit(solution)/shard_map/ppermute | solution.py:38
  90.7 41.3 %collective-permute-start.1 = (bf16[128,512]{1,0:T(8,128)(2,1)}, bf16[128,512]{1,0:T(8,128)(2,1)S(1)}, u32[]{:S(2)}, u32[]{:S(2)}) collective-permute-start(bf16[128,512]{1,0:T(8,128)(2,1)} %get-tuple-element.21), channel_id=1, source_target_pairs={{0,1},{1,0},{2,3},{3,2},{4,5},{5,4},{6,7},{7,6},{8,9},{9,8},{10,11... | collective-permute-start | bytes 393224 | tf_op jit(solution)/shard_map/ppermute | solution.py:33
  95.5 11.6 %copy-start.9 = (bf16[384,640]{1,0:T(8,128)(2,1)}, bf16[384,640]{1,0:T(8,128)(2,1)S(1)}, u32[]{:S(2)}) copy-start(bf16[384,640]{1,0:T(8,128)(2,1)S(1)} %collective-permute-done.2.up_1) | copy-start | bytes 1474564
  105.5 0.8 copy-start.10
  132.0 0.7 copy-start.12
  132.0 0.9 copy-start.4
  138.4 16.8 %copy-start.2 = (bf16[8,2,16,2560]{3,2,1,0:T(8,128)(2,1)}, bf16[8,2,16,2560]{3,2,1,0:T(8,128)(2,1)S(1)}, u32[]{:S(2)}) copy-start(bf16[8,2,16,2560]{3,2,1,0:T(8,128)(2,1)S(1)} %all-to-all-done.1.grads) | copy-start | bytes 3932164
  138.5 62.5 %all-to-all-start.2 = ((bf16[8,2,16,2560]{3,2,1,0:T(8,128)(2,1)}), bf16[8,2,16,2560]{3,2,1,0:T(8,128)(2,1)S(1)}, u32[]{:S(2)}, u32[]{:S(2)}) async-start(bf16[8,2,16,2560]{3,2,1,0:T(8,128)(2,1)} %get-tuple-element.33), calls=%async_computation.2 | async-start | bytes 2621440 | tf_op jit(solution)/shard_map/all_to_all | solution.py:29
  148.8 6.5 %copy-start = (bf16[384,2560]{1,0:T(8,128)(2,1)S(1)}, bf16[384,2560]{1,0:T(8,128)(2,1)}, u32[]{:S(2)}) copy-start(bf16[384,2560]{1,0:T(8,128)(2,1)} %up_rows.1.up_half) | copy-start | bytes 5898244
  151.9 46.4 %collective-permute-start.5 = (bf16[256,1024]{1,0:T(8,128)(2,1)}, bf16[256,1024]{1,0:T(8,128)(2,1)S(1)}, u32[]{:S(2)}, u32[]{:S(2)}) collective-permute-start(bf16[256,1024]{1,0:T(8,128)(2,1)} %get-tuple-element.36), channel_id=1, source_target_pairs={{0,2},{2,4},{4,6},{6,0},{1,3},{3,5},{5,7},{7,1},{8,10},{10,12},{12... | collective-permute-start | bytes 1572872 | tf_op jit(solution)/shard_map/ppermute | solution.py:38
  156.9 29.6 %collective-permute-start.8 = (bf16[256,384]{1,0:T(8,128)(2,1)S(1)}, bf16[256,384]{1,0:T(8,128)(2,1)S(1)}, u32[]{:S(2)}, u32[]{:S(2)}) collective-permute-start(bf16[256,384]{1,0:T(8,128)(2,1)S(1)} %get-tuple-element.38), channel_id=1, source_target_pairs={{0,1},{1,0},{2,3},{3,2},{4,5},{5,4},{6,7},{7,6},{8,9},{9,8},{10,11... | collective-permute-start | bytes 589832 | tf_op jit(solution)/shard_map/ppermute | solution.py:33
  161.0 55.6 %collective-permute-start.6 = (bf16[256,1024]{1,0:T(8,128)(2,1)}, bf16[256,1024]{1,0:T(8,128)(2,1)S(1)}, u32[]{:S(2)}, u32[]{:S(2)}) collective-permute-start(bf16[256,1024]{1,0:T(8,128)(2,1)} %get-tuple-element.35), channel_id=1, source_target_pairs={{0,4},{2,6},{4,0},{6,2},{1,5},{3,7},{5,1},{7,3},{8,12},{10,14},{12... | collective-permute-start | bytes 1572872 | tf_op jit(solution)/shard_map/ppermute | solution.py:38
  165.7 51.0 %collective-permute-start.7 = (bf16[256,1024]{1,0:T(8,128)(2,1)}, bf16[256,1024]{1,0:T(8,128)(2,1)S(1)}, u32[]{:S(2)}, u32[]{:S(2)}) collective-permute-start(bf16[256,1024]{1,0:T(8,128)(2,1)} %get-tuple-element.34), channel_id=1, source_target_pairs={{0,6},{2,0},{4,2},{6,4},{1,7},{3,1},{5,3},{7,5},{8,14},{10,8},{12,... | collective-permute-start | bytes 1572872 | tf_op jit(solution)/shard_map/ppermute | solution.py:38
  186.5 0.7 copy-start.11
  190.2 26.4 %collective-permute-start.10 = (bf16[256,1024]{1,0:T(8,128)(2,1)}, bf16[256,1024]{1,0:T(8,128)(2,1)}, u32[]{:S(2)}, u32[]{:S(2)}) collective-permute-start(bf16[256,1024]{1,0:T(8,128)(2,1)} %get-tuple-element.28), channel_id=1, source_target_pairs={{0,4},{2,6},{4,0},{6,2},{1,5},{3,7},{5,1},{7,3},{8,12},{10,14},{12... | collective-permute-start | bytes 1572872 | tf_op jit(solution)/shard_map/ppermute | solution.py:38
  195.1 21.6 %collective-permute-start.11 = (bf16[256,1024]{1,0:T(8,128)(2,1)}, bf16[256,1024]{1,0:T(8,128)(2,1)}, u32[]{:S(2)}, u32[]{:S(2)}) collective-permute-start(bf16[256,1024]{1,0:T(8,128)(2,1)} %get-tuple-element.29), channel_id=1, source_target_pairs={{0,6},{2,0},{4,2},{6,4},{1,7},{3,1},{5,3},{7,5},{8,14},{10,8},{12,... | collective-permute-start | bytes 1572872 | tf_op jit(solution)/shard_map/ppermute | solution.py:38
  198.3 18.4 %copy-start.5 = (bf16[256,1024]{1,0:T(8,128)(2,1)}, bf16[256,1024]{1,0:T(8,128)(2,1)S(1)}, u32[]{:S(2)}) copy-start(bf16[256,1024]{1,0:T(8,128)(2,1)S(1)} %collective-permute-done.5.refs_1_) | copy-start | bytes 1572868
  198.3 18.4 %collective-permute-start.9 = (bf16[256,1024]{1,0:T(8,128)(2,1)}, bf16[256,1024]{1,0:T(8,128)(2,1)}, u32[]{:S(2)}, u32[]{:S(2)}) collective-permute-start(bf16[256,1024]{1,0:T(8,128)(2,1)} %get-tuple-element.27), channel_id=1, source_target_pairs={{0,2},{2,4},{4,6},{6,0},{1,3},{3,5},{5,7},{7,1},{8,10},{10,12},{12... | collective-permute-start | bytes 1572872 | tf_op jit(solution)/shard_map/ppermute | solution.py:38
  200.9 1.1 copy-start.3
  205.9 24.9 %all-to-all-start.3 = ((f32[64,1,128]{2,1,0:T(1,128)}), f32[64,1,128]{2,1,0:T(1,128)S(1)}, u32[]{:S(2)}, u32[]{:S(2)}) async-start(f32[64,1,128]{2,1,0:T(1,128)} %bitcast.49), calls=%async_computation.3 | async-start | bytes 65536 | tf_op jit(solution)/shard_map/all_to_all | solution.py:29
  216.6 0.8 copy-start.6
  216.6 1.0 copy-start.7

commit v6 on v5

v6 whole, which is shorter than its diff:
```python
import jax
import jax.numpy as jnp
from jax import lax
from jax.experimental import pallas as pl
from jax.experimental.pallas import tpu as pltpu
from jax.sharding import Mesh, PartitionSpec as P


MIXES = 8
LANES = 128
BLOCK = 640
TERMS = 3
epsilon = 1e-06
root_coef = 0.7978845608028654
GROUP = ("zl", "yh")
SMEM = pl.BlockSpec(memory_space=pltpu.SMEM)
VMEM = pl.BlockSpec(memory_space=pltpu.VMEM)


def gelu_pair(values):
    tangent = jnp.tanh(root_coef * (values + 0.044715 * values * values * values))
    result = 0.5 * values * (1.0 + tangent)
    slopes = 0.5 * (1.0 + tangent) + 0.5 * values * (1.0 - tangent * tangent) * root_coef * (
        1.0 + 3.0 * 0.044715 * values * values
    )
    return (result, slopes)


def exchange(pieces, axes):
    return lax.all_to_all(pieces, axes, split_axis=0, concat_axis=0, tiled=True)


def swapped(value, axis):
    return lax.ppermute(value, axis, [(0, 1), (1, 0)])


def shifted(value, axis, steps):
    count = lax.axis_size(axis)
    return lax.ppermute(value, axis, [(i, (i + steps) % count) for i in range(count)])


def split_terms(value):
    terms = []
    for _ in range(TERMS):
        term = value.astype(jnp.bfloat16).astype(jnp.float32)
        terms.append(term)
        value = value - term
    return terms


def shape(dims, dtype=jnp.bfloat16):
    return jax.ShapeDtypeStruct(dims, dtype)


def pack_grads_body(weights, grads, out):
    halves, sections, rows, cols = out.shape
    block = BLOCK
    for half in range(halves):
        for i in range((cols - LANES) // block):
            piece = grads[:, (i * halves + half) * block : (i * halves + half + 1) * block]
            out[half, :, :, i * block : (i + 1) * block] = piece.reshape(sections, rows, block)
    lane = lax.broadcasted_iota(jnp.int32, (rows, LANES), 1)
    row = lax.broadcasted_iota(jnp.int32, (rows, LANES), 0)
    value = jnp.zeros((rows, LANES), jnp.float32)
    for m in range(MIXES):
        value = jnp.where(lane == m, weights[0, m], value)
    tail = jnp.zeros((rows, LANES), jnp.float32)
    for i, term in enumerate(split_terms(value)):
        tail = jnp.where(row == i, term, tail)
    tail = tail.astype(jnp.bfloat16)
    for half in range(halves):
        for k in range(sections):
            out[half, k, :, cols - LANES :] = tail


def pack_inputs_body(place, layer_in, latent, kept, sent, rest):
    tokens, half_cols = kept.shape
    ranks = latent.shape[1]
    width = layer_in.shape[1]
    block = BLOCK
    first = place[0] == 0
    squares = jnp.zeros((tokens, LANES), jnp.float32)
    for at in range(0, width, LANES):
        tile = layer_in[:, at : at + LANES].astype(jnp.float32)
        squares = squares + tile * tile
    inv_rms = lax.rsqrt(jnp.sum(squares, axis=1, keepdims=True) / width + epsilon)
    lane = lax.broadcasted_iota(jnp.int32, (tokens, LANES), 1)
    tail = jnp.zeros((tokens, LANES), jnp.float32)
    for i, term in enumerate(split_terms(jnp.broadcast_to(inv_rms, (tokens, LANES)))):
        tail = jnp.where(lane == i, term, tail)
    for i in range(half_cols // block):
        low = layer_in[:, 2 * i * block : (2 * i + 1) * block]
        high = layer_in[:, (2 * i + 1) * block : (2 * i + 2) * block]
        kept[:, i * block : (i + 1) * block] = jnp.where(first, low, high)
        sent[:, i * block : (i + 1) * block] = jnp.where(first, high, low)
    rest[:, :ranks] = latent[...]
    rest[:, ranks:] = tail.astype(jnp.bfloat16)


def activate_body(place, kept, other, up, act, scale, out):
    sections, halves, rows, ranks = act.shape
    first = place[0] == 0
    for half in range(halves):
        near, far = (kept[...], other[...]) if half == 0 else (other[...], kept[...])
        rest = jnp.where(first, near, far).astype(jnp.float32)
        values, slopes = gelu_pair(rest[:, :, :ranks])
        inv_rms = jnp.sum(rest[:, :, ranks:], axis=2, keepdims=True)
        act[:, half] = values.astype(jnp.bfloat16)
        scale[:, half] = slopes * inv_rms
    out[:, :BLOCK] = up[...]
    whole_act = act[...].reshape(sections * halves * rows, ranks).astype(jnp.float32)
    out[:, BLOCK:] = jnp.transpose(whole_act).astype(jnp.bfloat16)


def up_rows_body(place, up_0, up_1, up_2, up_3, out):
    for i in range(4):
        turn = lax.rem(place[1] - i + 4, 4)
        pieces = [up[:, :BLOCK] for up in (up_0, up_1, up_2, up_3)]
        near, far = (jnp.where(turn == 0, pieces[0], pieces[1]), jnp.where(turn == 2, pieces[2], pieces[3]))
        out[:, i * BLOCK : (i + 1) * BLOCK] = jnp.where(turn < 2, near, far)


def lift_body(place, kept, other, act, up_half, mixed, sends, inputs):
    del mixed
    sections, halves, rows, width = sends.shape
    ranks = up_half.shape[0]
    first = place[0] == 0
    for at in range(0, width, BLOCK):
        lanes = slice(at, at + BLOCK)
        for half in range(halves):
            near, far = (kept, other) if half == 0 else (other, kept)
            rows_in = jnp.where(first, near[:, :, lanes], far[:, :, lanes])
            inputs[:, half, :, lanes] = rows_in
            branch = jnp.dot(
                act[:, half].reshape(sections * rows, ranks), up_half[:, lanes], preferred_element_type=jnp.float32
            ).reshape(sections, rows, BLOCK)
            sends[:, half, :, lanes] = (rows_in.astype(jnp.float32) + branch).astype(jnp.bfloat16)


def mix_body(coef, grads, out):
    sections, halves, _, cols = out.shape
    for half in range(halves):
        for at in range(0, cols, LANES):
            lanes = slice(at, at + LANES)
            tiles = [grads[half, k, :, lanes].astype(jnp.float32) for k in range(sections)]
            for k in range(sections):
                total = coef[k, 0] * tiles[k]
                for m in range(1, sections - k):
                    total = total + coef[k, m] * tiles[k + m]
                out[k, half, :, lanes] = total.astype(jnp.bfloat16)


def gram_body(grads, outs, result):
    sections, halves, rows, cols = outs.shape
    total = jnp.zeros((sections * rows, LANES), jnp.float32)
    for half in range(halves):
        total = total + lax.dot_general(
            outs[:, half].reshape(sections * rows, cols),
            grads[half, :, :, :cols].reshape(sections * rows, cols),
            (((1,), (1,)), ((), ())),
            preferred_element_type=jnp.float32,
        )
    row = lax.broadcasted_iota(jnp.int32, total.shape, 0)
    lane = lax.broadcasted_iota(jnp.int32, total.shape, 1)
    same = jnp.where(lax.rem(row, rows) == lax.rem(lane, rows), total, 0.0)
    share = result.shape[0] // sections
    spread = []
    for k in range(sections):
        sums = jnp.sum(same[k * rows : (k + 1) * rows], axis=0, keepdims=True)
        sums = jnp.broadcast_to(sums, (share, LANES))
        if k:
            sums = pltpu.roll(sums, LANES - k * rows, 1)
            sums = jnp.where(lane[:share] < LANES - k * rows, sums, 0.0)
        spread.append(sums)
    gather = jnp.where(lax.div(row, rows) == lane, 1.0, 0.0)
    result[...] = jnp.dot(
        jnp.concatenate(spread, axis=0), gather, precision=lax.Precision.HIGHEST, preferred_element_type=jnp.float32
    )


def share_body(place, inputs, grads, partial, other, scale, *outs):
    sections, halves, rows, _ = grads.shape
    count = sections * halves * rows
    latent_grad = ((partial[...] + other[...].astype(jnp.float32)) * scale[...]).astype(jnp.bfloat16)
    for step, out in enumerate(outs):
        at = pl.multiple_of(lax.rem(place[1] + step, len(outs)) * BLOCK, LANES)
        out[:, :BLOCK] = inputs[:, :, :, pl.ds(at, BLOCK)].reshape(count, BLOCK)
        out[:, BLOCK : 2 * BLOCK] = grads[:, :, :, pl.ds(at, BLOCK)].reshape(count, BLOCK)
        out[:, 2 * BLOCK :] = latent_grad


def weights_body(*refs):
    half = (len(refs) - 5) // 2
    acts, shared = refs[:half], refs[half : 2 * half]
    gain, down, up_out, down_out, gain_out = refs[2 * half :]
    up_total = jnp.zeros(up_out.shape, jnp.float32)
    down_total = jnp.zeros(down_out.shape, jnp.float32)
    for act, piece in zip(acts, shared):
        up_total = up_total + jnp.dot(
            act[:, BLOCK:], piece[:, BLOCK : 2 * BLOCK], preferred_element_type=jnp.float32
        )
        down_total = down_total + lax.dot_general(
            piece[:, :BLOCK], piece[:, 2 * BLOCK :], (((0,), (0,)), ((), ())), preferred_element_type=jnp.float32
        )
    up_out[...] = up_total.astype(jnp.bfloat16)
    gain_cols = jnp.transpose(jnp.broadcast_to(gain[...].astype(jnp.float32), (8, gain.shape[1])))
    down_out[...] = (down_total * gain_cols[:, :1]).astype(jnp.bfloat16)
    product = down_total * down[...].astype(jnp.float32)
    ones = jnp.ones((8, product.shape[1]), jnp.float32)
    sums = lax.dot_general(
        ones, product, (((1,), (1,)), ((), ())), precision=lax.Precision.HIGHEST, preferred_element_type=jnp.float32
    )
    gain_out[...] = sums[:1]


def whole(layer_in, latent, mix_grad, down_proj, up_proj, norm_gain, mix_weight):
    layer_in, latent, mix_grad = (layer_in[0], latent[0], mix_grad[0])
    tokens, width = layer_in.shape
    ranks = latent.shape[1]
    xs, zs = (lax.axis_size("x"), lax.axis_size("zh"))
    sections = lax.axis_size("zl") * lax.axis_size("yh")
    block = width // (xs * zs)
    half_width = xs * block
    rows = tokens // sections
    place = jnp.stack([lax.axis_index("zh"), lax.axis_index("x")]).astype(jnp.int32)

    packed = pl.pallas_call(
        pack_grads_body,
        in_specs=[SMEM, pl.BlockSpec((tokens, width), lambda: (0, 0))],
        out_specs=pl.BlockSpec((zs, sections, rows, half_width + LANES), lambda: (0, 0, 0, 0)),
        out_shape=shape((zs, sections, rows, half_width + LANES)),
        name="pack_grads",
    )(mix_weight, mix_grad)
    grads = exchange(packed.reshape(zs * sections, rows, half_width + LANES), ("zh", *GROUP))
    grads = grads.reshape(zs, sections, rows, half_width + LANES)

    rest = ranks + LANES
    kept, sent, kept_rest = pl.pallas_call(
        pack_inputs_body,
        in_specs=[SMEM, pl.BlockSpec((tokens, width), lambda: (0, 0)), pl.BlockSpec((tokens, ranks), lambda: (0, 0))],
        out_specs=[pl.BlockSpec((tokens, half_width), lambda: (0, 0))] * 2
        + [pl.BlockSpec((tokens, rest), lambda: (0, 0))],
        out_shape=[shape((tokens, half_width))] * 2 + [shape((tokens, rest))],
        name="pack_inputs",
    )(place, layer_in, latent)
    other_rest = swapped(kept_rest, "zh")
    other = swapped(sent, "zh")

    kept, other, kept_rest, other_rest = [
        t.reshape(sections, rows, t.shape[1]) for t in (kept, other, kept_rest, other_rest)
    ]
    act, scale, up_part = pl.pallas_call(
        activate_body,
        in_specs=[SMEM] + [VMEM] * 3,
        out_specs=[VMEM] * 3,
        out_shape=[
            shape((sections, zs, rows, ranks)),
            shape((sections, zs, rows, ranks), jnp.float32),
            shape((ranks, block + zs * tokens)),
        ],
        name="activate",
    )(place, kept_rest, other_rest, up_proj[0])
    scale = scale.reshape(zs * tokens, ranks)

    ups = [up_part]
    for step in range(1, xs):
        ups.append(shifted(up_part, "x", step))
    up_half = pl.pallas_call(
        up_rows_body,
        in_specs=[SMEM] + [VMEM] * xs,
        out_specs=VMEM,
        out_shape=shape((ranks, half_width)),
        name="up_rows",
    )(place, *ups)

    weights = jnp.sum(grads[0, :, :TERMS, half_width : half_width + MIXES].astype(jnp.float32), axis=1)
    chunk = shape((sections, zs, rows, half_width))
    mixed = pl.pallas_call(mix_body, in_specs=[SMEM, VMEM], out_specs=VMEM, out_shape=chunk, name="mix")(weights, grads)
    arrived = exchange(mixed, GROUP)

    layer_out, inputs = pl.pallas_call(
        lift_body,
        in_specs=[SMEM] + [VMEM] * 4 + [pl.BlockSpec(memory_space=pl.ANY)],
        out_specs=[VMEM] * 2,
        out_shape=[chunk] * 2,
        name="lift",
    )(place, kept, other, act, up_half, mixed)

    layer_out, arrived = lax.optimization_barrier((layer_out, arrived))
    outs = exchange(layer_out, GROUP)

    act_partial = jnp.einsum(
        "tc,rc->tr", arrived.reshape(zs * tokens, half_width), up_half, preferred_element_type=jnp.float32
    )
    act_other = swapped(act_partial.astype(jnp.bfloat16), "zh")
    shares = pl.pallas_call(
        share_body,
        in_specs=[SMEM] + [VMEM] * 5,
        out_specs=[VMEM] * xs,
        out_shape=[shape((zs * tokens, 2 * block + ranks))] * xs,
        name="share",
    )(place, inputs, arrived, act_partial, act_other, scale)
    shares = list(shares)
    for step in range(1, xs):
        shares[step] = shifted(shares[step], "x", step)

    everyone = sections * xs * zs
    products = pl.pallas_call(
        gram_body,
        in_specs=[VMEM] * 2,
        out_specs=VMEM,
        out_shape=shape((everyone, LANES), jnp.float32),
        name="gram",
    )(grads, outs)
    mixing = exchange(products, (*GROUP, "x", "zh")).sum(axis=0)[:MIXES]

    up_grad, down_grad, gain_grad = pl.pallas_call(
        weights_body,
        in_specs=[VMEM] * (2 * xs + 2),
        out_specs=[VMEM] * 3,
        out_shape=[shape((ranks, block)), shape((block, ranks)), shape((1, block), jnp.float32)],
        name="weights",
    )(*ups, *shares, norm_gain, down_proj[0])
    return (up_grad[None], down_grad[None], gain_grad, mixing[None])


def solution(mesh):
    devices = mesh.devices.reshape(4, 2, 8, 4, 2)
    fine = Mesh(devices, ("zl", "yh", "r", "x", "zh"))
    section, dp = (("zl", "yh", "r"), ("x", "zh"))
    return jax.shard_map(
        whole,
        mesh=fine,
        in_specs=(
            P(section, dp, None),
            P(section, dp, None),
            P(section, dp, None),
            P(section, dp, None),
            P(section, None, dp),
            P(section, dp),
            P(section, None),
        ),
        out_specs=(
            P(section, None, dp),
            P(section, dp, None),
            P(section, dp),
            P(section, None),
        ),
        check_vma=False,
    )
```

time: 232 us -> 257 us (1.11)
  the two profiles are of different devices: /device:TPU:8 before, /device:TPU:11 now
where the time goes in v6:
time: 257 us; the launch traced here: 256 us
  waiting for transfers between devices  87.6 us (34%)
  starting transfers between devices  71.7 us (28%)
  blocking collectives  56.4 us (22%)
  Pallas kernels  32.8 us (13%)
  local copies, waits for them, and re-layouts  4.16 us (2%)
    all_to_all x1, blocking collectives, exchange(): return lax.all_to_all(pieces, axes, split_axis=0, concat_axis=0, tiled=True)  56.4 us
    ppermute x6, waiting for transfers between devices, shifted(): lax.ppermute(value, axis, [(i, (i + steps) % count) for i in range(count)])  47.6 us
    ppermute x3, waiting for transfers between devices, swapped(): return lax.ppermute(value, axis, [(0, 1), (1, 0)])  40 us
    all_to_all x3, starting transfers between devices, exchange(): return lax.all_to_all(pieces, axes, split_axis=0, concat_axis=0, tiled=True)  39.9 us
    ppermute x6, starting transfers between devices, shifted(): lax.ppermute(value, axis, [(i, (i + steps) % count) for i in range(count)])  18.2 us
    ppermute x3, starting transfers between devices, swapped(): return lax.ppermute(value, axis, [(0, 1), (1, 0)])  13.5 us
    pallas_call x1, Pallas kernels, whole(): pl.pallas_call(weights_body, in_specs=[VMEM] * (2 * xs + 2), out_specs=[V...  6.37 us
  transfers between devices with their start and end apart: 12, of which 7 were waited for; matrix products, arithmetic and copies ran while one was open for 1% of the time, Pallas kernels for 10%

profile of v6, /device:TPU:11, one launch (start us, length us, event | category | flops | bytes accessed | tf_op | source)
XLA Modules:
  0.0 256.3 jit_solution(17302799495617283032)
XLA Ops:
  0.6 2.5 pack_grads.1
  3.2 56.4 %all_to_all.24 = bf16[16,16,2688]{2,1,0:T(8,128)(2,1)S(1)} all-to-all(bf16[16,16,2688]{2,1,0:T(8,128)(2,1)} %bitcast.28), channel_id=1, replica_groups=mesh['zl'=4,'yh'=2,'r'=8,'x'=4,'zh'=2] {'zh','zl','yh'}, dimensions={0} | all-to-all | bytes 2752512 | tf_op jit(solution)/shard_map/all_to_all | solution.py:30
  60.6 3.4 %mix.1.mixed = bf16[8,2,16,2560]{3,2,1,0:T(8,128)(2,1)} custom-call(f32[8,8]{1,0:T(8,128)} %convert_reduce_fusion.coef, bf16[2,8,16,2688]{3,2,1,0:T(8,128)(2,1)} %bitcast.25), custom_call_target="tpu_custom_call" | custom-call | tf_op jit(solution)/shard_map/mix/pallas_call | solution.py:278
  64.0 4.1 %all-to-all-start.1 = ((bf16[8,2,16,2560]{3,2,1,0:T(8,128)(2,1)}), bf16[8,2,16,2560]{3,2,1,0:T(8,128)(2,1)S(1)}, u32[]{:S(2)}, u32[]{:S(2)}) async-start(bf16[8,2,16,2560]{3,2,1,0:T(8,128)(2,1)} %mix.1.mixed), calls=%async_computation.1 | async-start | bytes 2621440 | tf_op jit(solution)/shard_map/all_to_all | solution.py:30
  68.6 3.0 %pack_inputs.1 = (bf16[128,2560]{1,0:T(8,128)(2,1)}, bf16[128,2560]{1,0:T(8,128)(2,1)}, bf16[128,512]{1,0:T(8,128)(2,1)}) custom-call(s32[2]{0:T(128)} %pad_add_fusion.place, bf16[128,5120]{1,0:T(8,128)(2,1)} %bitcast.30, bf16[128,384]{1,0:T(8,128)(2,1)} %bitcast.39), custom_call_target="tpu_custom_call" | custom-call | tf_op jit(solution)/shard_map/pack_inputs/pallas_call | solution.py:238
  71.6 4.6 %collective-permute-start = (bf16[128,512]{1,0:T(8,128)(2,1)}, bf16[128,512]{1,0:T(8,128)(2,1)S(1)}, u32[]{:S(2)}, u32[]{:S(2)}) collective-permute-start(bf16[128,512]{1,0:T(8,128)(2,1)} %get-tuple-element.21), channel_id=1, source_target_pairs={{0,1},{1,0},{2,3},{3,2},{4,5},{5,4},{6,7},{7,6},{8,9},{9,8},{10,11... | collective-permute-start | bytes 393224 | tf_op jit(solution)/shard_map/ppermute | solution.py:34
  76.2 8.3 %collective-permute-done = bf16[128,512]{1,0:T(8,128)(2,1)S(1)} collective-permute-done((bf16[128,512]{1,0:T(8,128)(2,1)}, bf16[128,512]{1,0:T(8,128)(2,1)S(1)}, u32[]{:S(2)}, u32[]{:S(2)}) %collective-permute-start) | collective-permute-done | bytes 131104 | tf_op jit(solution)/shard_map/ppermute | solution.py:34
  85.2 2.5 activate.1
  87.7 3.1 %collective-permute-start.1 = (bf16[384,896]{1,0:T(8,128)(2,1)}, bf16[384,896]{1,0:T(8,128)(2,1)S(1)}, u32[]{:S(2)}, u32[]{:S(2)}) collective-permute-start(bf16[384,896]{1,0:T(8,128)(2,1)} %get-tuple-element.22.up_0.refs_0_), channel_id=1, source_target_pairs={{0,2},{2,4},{4,6},{6,0},{1,3},{3,5},{5,7},{7,1},{8,10},{10,12},{12... | collective-permute-start | bytes 2064392 | tf_op jit(solution)/shard_map/ppermute | solution.py:39
  90.8 2.7 %collective-permute-start.2 = (bf16[384,896]{1,0:T(8,128)(2,1)}, bf16[384,896]{1,0:T(8,128)(2,1)S(1)}, u32[]{:S(2)}, u32[]{:S(2)}) collective-permute-start(bf16[384,896]{1,0:T(8,128)(2,1)} %get-tuple-element.22.up_0.refs_0_), channel_id=1, source_target_pairs={{0,4},{2,6},{4,0},{6,2},{1,5},{3,7},{5,1},{7,3},{8,12},{10,14},{12... | collective-permute-start | bytes 2064392 | tf_op jit(solution)/shard_map/ppermute | solution.py:39
  93.5 3.8 %collective-permute-start.3 = (bf16[384,896]{1,0:T(8,128)(2,1)}, bf16[384,896]{1,0:T(8,128)(2,1)}, u32[]{:S(2)}, u32[]{:S(2)}) collective-permute-start(bf16[384,896]{1,0:T(8,128)(2,1)} %get-tuple-element.22.up_0.refs_0_), channel_id=1, source_target_pairs={{0,6},{2,0},{4,2},{6,4},{1,7},{3,1},{5,3},{7,5},{8,14},{10,8},{12,... | collective-permute-start | bytes 2064392 | tf_op jit(solution)/shard_map/ppermute | solution.py:39
  97.3 4.8 %collective-permute-start.4 = (bf16[128,2560]{1,0:T(8,128)(2,1)}, bf16[128,2560]{1,0:T(8,128)(2,1)S(1)}, u32[]{:S(2)}, u32[]{:S(2)}) collective-permute-start(bf16[128,2560]{1,0:T(8,128)(2,1)} %get-tuple-element.24), channel_id=1, source_target_pairs={{0,1},{1,0},{2,3},{3,2},{4,5},{5,4},{6,7},{7,6},{8,9},{9,8},{10,11... | collective-permute-start | bytes 1966088 | tf_op jit(solution)/shard_map/ppermute | solution.py:34
  102.5 4.4 %collective-permute-done.2.up_2.refs_2_ = bf16[384,896]{1,0:T(8,128)(2,1)S(1)} collective-permute-done((bf16[384,896]{1,0:T(8,128)(2,1)}, bf16[384,896]{1,0:T(8,128)(2,1)S(1)}, u32[]{:S(2)}, u32[]{:S(2)}) %collective-permute-start.2) | collective-permute-done | bytes 688160 | tf_op jit(solution)/shard_map/ppermute | solution.py:39
  106.9 19.7 %collective-permute-done.3.up_3.refs_3_ = bf16[384,896]{1,0:T(8,128)(2,1)} collective-permute-done((bf16[384,896]{1,0:T(8,128)(2,1)}, bf16[384,896]{1,0:T(8,128)(2,1)}, u32[]{:S(2)}, u32[]{:S(2)}) %collective-permute-start.3) | collective-permute-done | bytes 688160 | tf_op jit(solution)/shard_map/ppermute | solution.py:39
  126.6 3.4 %up_rows.1.up_half = bf16[384,2560]{1,0:T(8,128)(2,1)} custom-call(s32[2]{0:T(128)} %pad_add_fusion.place, bf16[384,896]{1,0:T(8,128)(2,1)} %get-tuple-element.22.up_0.refs_0_, bf16[384,896]{1,0:T(8,128)(2,1)} %copy-done.3, bf16[384,896]{1,0:T(8,128)(2,1)} %copy-done.4, bf16[384,896]{1,0:T(8,128)(2,1)} %collective-permute-done.3.up_3.refs_3_), custom_call_target="tpu_custom_call" | custom-call | tf_op jit(solution)/shard_map/up_rows/pallas_call | solution.py:268
  130.1 0.9 copy-done.8
  131.0 4.4 %lift.1 = (bf16[8,2,16,2560]{3,2,1,0:T(8,128)(2,1)}, bf16[8,2,16,2560]{3,2,1,0:T(8,128)(2,1)}) custom-call(s32[2]{0:T(128)} %pad_add_fusion.place, bf16[8,16,2560]{2,1,0:T(8,128)(2,1)} %bitcast.31, bf16[8,16,2560]{2,1,0:T(8,128)(2,1)} %bitcast.32, bf16[8,2,16,384]{3,2,1,0:T(8,128)(2,1)} %get-tuple-element.25.act, bf16[384,2560]{1,0:T(8,128)(2,1)} %up_rows.1.up_half, ...), custom_call_target="tpu_custom_call" | custom-call | tf_op jit(solution)/shard_map/lift/pallas_call | solution.py:281
  135.4 25.8 %all-to-all-start.2 = ((bf16[8,2,16,2560]{3,2,1,0:T(8,128)(2,1)}), bf16[8,2,16,2560]{3,2,1,0:T(8,128)(2,1)}, u32[]{:S(2)}, u32[]{:S(2)}) async-start(bf16[8,2,16,2560]{3,2,1,0:T(8,128)(2,1)} %get-tuple-element.37), calls=%async_computation.2 | async-start | bytes 2621440 | tf_op jit(solution)/shard_map/all_to_all | solution.py:30
  161.2 1.6 fusion
  162.8 4.1 %collective-permute-start.5 = (bf16[256,384]{1,0:T(8,128)(2,1)S(1)}, bf16[256,384]{1,0:T(8,128)(2,1)S(1)}, u32[]{:S(2)}, u32[]{:S(2)}) collective-permute-start(bf16[256,384]{1,0:T(8,128)(2,1)S(1)} %get-tuple-element.38), channel_id=1, source_target_pairs={{0,1},{1,0},{2,3},{3,2},{4,5},{5,4},{6,7},{7,6},{8,9},{9,8},{10,11... | collective-permute-start | bytes 589832 | tf_op jit(solution)/shard_map/ppermute | solution.py:34
  167.0 31.7 %collective-permute-done.5.other = bf16[256,384]{1,0:T(8,128)(2,1)S(1)} collective-permute-done((bf16[256,384]{1,0:T(8,128)(2,1)S(1)}, bf16[256,384]{1,0:T(8,128)(2,1)S(1)}, u32[]{:S(2)}, u32[]{:S(2)}) %collective-permute-start.5) | collective-permute-done | bytes 196640 | tf_op jit(solution)/shard_map/ppermute | solution.py:34
  198.7 0.7 copy-done.9
  199.4 4.0 %share.1 = (bf16[256,1664]{1,0:T(8,128)(2,1)}, bf16[256,1664]{1,0:T(8,128)(2,1)}, bf16[256,1664]{1,0:T(8,128)(2,1)}, bf16[256,1664]{1,0:T(8,128)(2,1)}) custom-call(s32[2]{0:T(128)} %pad_add_fusion.place, bf16[8,2,16,2560]{3,2,1,0:T(8,128)(2,1)} %get-tuple-element.26.inputs, bf16[8,2,16,2560]{3,2,1,0:T(8,128)(2,1)} %copy-done.2, ...), custom_call_target="tpu_custom_call" | custom-call | tf_op jit(solution)/shard_map/share/pallas_call | solution.py:296
  203.4 1.9 collective-permute-start.6
  205.3 2.7 %collective-permute-start.7 = (bf16[256,1664]{1,0:T(8,128)(2,1)}, bf16[256,1664]{1,0:T(8,128)(2,1)S(1)}, u32[]{:S(2)}, u32[]{:S(2)}) collective-permute-start(bf16[256,1664]{1,0:T(8,128)(2,1)} %get-tuple-element.32), channel_id=1, source_target_pairs={{0,4},{2,6},{4,0},{6,2},{1,5},{3,7},{5,1},{7,3},{8,12},{10,14},{12... | collective-permute-start | bytes 2555912 | tf_op jit(solution)/shard_map/ppermute | solution.py:39
  208.1 4.0 %collective-permute-start.8 = (bf16[256,1664]{1,0:T(8,128)(2,1)}, bf16[256,1664]{1,0:T(8,128)(2,1)S(1)}, u32[]{:S(2)}, u32[]{:S(2)}) collective-permute-start(bf16[256,1664]{1,0:T(8,128)(2,1)} %get-tuple-element.33), channel_id=1, source_target_pairs={{0,6},{2,0},{4,2},{6,4},{1,7},{3,1},{5,3},{7,5},{8,14},{10,8},{12,... | collective-permute-start | bytes 2555912 | tf_op jit(solution)/shard_map/ppermute | solution.py:39
  212.0 3.2 %gram.1 = f32[64,128]{1,0:T(8,128)} custom-call(bf16[2,8,16,2688]{3,2,1,0:T(8,128)(2,1)} %bitcast.26, bf16[8,2,16,2560]{3,2,1,0:T(8,128)(2,1)} %all-to-all-done.2.outs), custom_call_target="tpu_custom_call" | custom-call | tf_op jit(solution)/shard_map/gram/pallas_call | solution.py:308
  215.2 10.0 %all-to-all-start.3 = ((f32[64,1,128]{2,1,0:T(1,128)}), f32[64,1,128]{2,1,0:T(1,128)S(1)}, u32[]{:S(2)}, u32[]{:S(2)}) async-start(f32[64,1,128]{2,1,0:T(1,128)} %bitcast.36), calls=%async_computation.3 | async-start | bytes 65536 | tf_op jit(solution)/shard_map/all_to_all | solution.py:30
  225.3 2.4 collective-permute-done.7.refs_6_
  227.7 20.7 %collective-permute-done.8.refs_7_ = bf16[256,1664]{1,0:T(8,128)(2,1)S(1)} collective-permute-done((bf16[256,1664]{1,0:T(8,128)(2,1)}, bf16[256,1664]{1,0:T(8,128)(2,1)S(1)}, u32[]{:S(2)}, u32[]{:S(2)}) %collective-permute-start.8) | collective-permute-done | bytes 852000 | tf_op jit(solution)/shard_map/ppermute | solution.py:39
  248.4 0.9 copy-done.7
  249.3 6.4 %weights.3 = (bf16[384,640]{1,0:T(8,128)(2,1)}, bf16[640,384]{1,0:T(8,128)(2,1)}, f32[1,640]{1,0:T(1,128)}) custom-call(bf16[384,896]{1,0:T(8,128)(2,1)} %get-tuple-element.22.up_0.refs_0_, bf16[384,896]{1,0:T(8,128)(2,1)} %copy-done.3, bf16[384,896]{1,0:T(8,128)(2,1)} %copy-done.4, bf16[384,896]{1,0:T(8,128)(2,1)} %collective-permute-done.3.up_3.refs_3_, ...), custom_call_target="tpu_custom_call" | custom-call | tf_op jit(solution)/shard_map/weights/pallas_call | solution.py:317
  (29 shorter events, 3.3 us)
Async XLA Ops:
  59.5 1.1 copy-start.1
  64.0 71.4 %all-to-all-start.1 = ((bf16[8,2,16,2560]{3,2,1,0:T(8,128)(2,1)}), bf16[8,2,16,2560]{3,2,1,0:T(8,128)(2,1)S(1)}, u32[]{:S(2)}, u32[]{:S(2)}) async-start(bf16[8,2,16,2560]{3,2,1,0:T(8,128)(2,1)} %mix.1.mixed), calls=%async_computation.1 | async-start | bytes 2621440 | tf_op jit(solution)/shard_map/all_to_all | solution.py:30
  71.6 12.9 %collective-permute-start = (bf16[128,512]{1,0:T(8,128)(2,1)}, bf16[128,512]{1,0:T(8,128)(2,1)S(1)}, u32[]{:S(2)}, u32[]{:S(2)}) collective-permute-start(bf16[128,512]{1,0:T(8,128)(2,1)} %get-tuple-element.21), channel_id=1, source_target_pairs={{0,1},{1,0},{2,3},{3,2},{4,5},{5,4},{6,7},{7,6},{8,9},{9,8},{10,11... | collective-permute-start | bytes 393224 | tf_op jit(solution)/shard_map/ppermute | solution.py:34
  84.5 0.7 copy-start.10
  87.7 14.8 %collective-permute-start.1 = (bf16[384,896]{1,0:T(8,128)(2,1)}, bf16[384,896]{1,0:T(8,128)(2,1)S(1)}, u32[]{:S(2)}, u32[]{:S(2)}) collective-permute-start(bf16[384,896]{1,0:T(8,128)(2,1)} %get-tuple-element.22.up_0.refs_0_), channel_id=1, source_target_pairs={{0,2},{2,4},{4,6},{6,0},{1,3},{3,5},{5,7},{7,1},{8,10},{10,12},{12... | collective-permute-start | bytes 2064392 | tf_op jit(solution)/shard_map/ppermute | solution.py:39
  90.8 16.1 %collective-permute-start.2 = (bf16[384,896]{1,0:T(8,128)(2,1)}, bf16[384,896]{1,0:T(8,128)(2,1)S(1)}, u32[]{:S(2)}, u32[]{:S(2)}) collective-permute-start(bf16[384,896]{1,0:T(8,128)(2,1)} %get-tuple-element.22.up_0.refs_0_), channel_id=1, source_target_pairs={{0,4},{2,6},{4,0},{6,2},{1,5},{3,7},{5,1},{7,3},{8,12},{10,14},{12... | collective-permute-start | bytes 2064392 | tf_op jit(solution)/shard_map/ppermute | solution.py:39
  93.5 33.1 %collective-permute-start.3 = (bf16[384,896]{1,0:T(8,128)(2,1)}, bf16[384,896]{1,0:T(8,128)(2,1)}, u32[]{:S(2)}, u32[]{:S(2)}) collective-permute-start(bf16[384,896]{1,0:T(8,128)(2,1)} %get-tuple-element.22.up_0.refs_0_), channel_id=1, source_target_pairs={{0,6},{2,0},{4,2},{6,4},{1,7},{3,1},{5,3},{7,5},{8,14},{10,8},{12,... | collective-permute-start | bytes 2064392 | tf_op jit(solution)/shard_map/ppermute | solution.py:39
  97.3 32.7 %collective-permute-start.4 = (bf16[128,2560]{1,0:T(8,128)(2,1)}, bf16[128,2560]{1,0:T(8,128)(2,1)S(1)}, u32[]{:S(2)}, u32[]{:S(2)}) collective-permute-start(bf16[128,2560]{1,0:T(8,128)(2,1)} %get-tuple-element.24), channel_id=1, source_target_pairs={{0,1},{1,0},{2,3},{3,2},{4,5},{5,4},{6,7},{7,6},{8,9},{9,8},{10,11... | collective-permute-start | bytes 1966088 | tf_op jit(solution)/shard_map/ppermute | solution.py:34
  102.5 24.1 %copy-start.3 = (bf16[384,896]{1,0:T(8,128)(2,1)}, bf16[384,896]{1,0:T(8,128)(2,1)S(1)}, u32[]{:S(2)}) copy-start(bf16[384,896]{1,0:T(8,128)(2,1)S(1)} %collective-permute-done.1.up_1.refs_1_) | copy-start | bytes 2064388
  106.9 19.7 %copy-start.4 = (bf16[384,896]{1,0:T(8,128)(2,1)}, bf16[384,896]{1,0:T(8,128)(2,1)S(1)}, u32[]{:S(2)}) copy-start(bf16[384,896]{1,0:T(8,128)(2,1)S(1)} %collective-permute-done.2.up_2.refs_2_) | copy-start | bytes 2064388
  130.1 0.9 copy-start.8
  135.4 25.8 %copy-start.2 = (bf16[8,2,16,2560]{3,2,1,0:T(8,128)(2,1)}, bf16[8,2,16,2560]{3,2,1,0:T(8,128)(2,1)S(1)}, u32[]{:S(2)}) copy-start(bf16[8,2,16,2560]{3,2,1,0:T(8,128)(2,1)S(1)} %all-to-all-done.1.grads) | copy-start | bytes 3932164
  135.4 25.8 %copy-start = (bf16[384,2560]{1,0:T(8,128)(2,1)S(1)}, bf16[384,2560]{1,0:T(8,128)(2,1)}, u32[]{:S(2)}) copy-start(bf16[384,2560]{1,0:T(8,128)(2,1)} %up_rows.1.up_half) | copy-start | bytes 5898244
  135.4 76.6 %all-to-all-start.2 = ((bf16[8,2,16,2560]{3,2,1,0:T(8,128)(2,1)}), bf16[8,2,16,2560]{3,2,1,0:T(8,128)(2,1)}, u32[]{:S(2)}, u32[]{:S(2)}) async-start(bf16[8,2,16,2560]{3,2,1,0:T(8,128)(2,1)} %get-tuple-element.37), calls=%async_computation.2 | async-start | bytes 2621440 | tf_op jit(solution)/shard_map/all_to_all | solution.py:30
  162.8 35.9 %collective-permute-start.5 = (bf16[256,384]{1,0:T(8,128)(2,1)S(1)}, bf16[256,384]{1,0:T(8,128)(2,1)S(1)}, u32[]{:S(2)}, u32[]{:S(2)}) collective-permute-start(bf16[256,384]{1,0:T(8,128)(2,1)S(1)} %get-tuple-element.38), channel_id=1, source_target_pairs={{0,1},{1,0},{2,3},{3,2},{4,5},{5,4},{6,7},{7,6},{8,9},{9,8},{10,11... | collective-permute-start | bytes 589832 | tf_op jit(solution)/shard_map/ppermute | solution.py:34
  198.7 0.7 copy-start.9
  203.4 21.8 %collective-permute-start.6 = (bf16[256,1664]{1,0:T(8,128)(2,1)}, bf16[256,1664]{1,0:T(8,128)(2,1)S(1)}, u32[]{:S(2)}, u32[]{:S(2)}) collective-permute-start(bf16[256,1664]{1,0:T(8,128)(2,1)} %get-tuple-element.31), channel_id=1, source_target_pairs={{0,2},{2,4},{4,6},{6,0},{1,3},{3,5},{5,7},{7,1},{8,10},{10,12},{12... | collective-permute-start | bytes 2555912 | tf_op jit(solution)/shard_map/ppermute | solution.py:39
  205.3 22.4 %collective-permute-start.7 = (bf16[256,1664]{1,0:T(8,128)(2,1)}, bf16[256,1664]{1,0:T(8,128)(2,1)S(1)}, u32[]{:S(2)}, u32[]{:S(2)}) collective-permute-start(bf16[256,1664]{1,0:T(8,128)(2,1)} %get-tuple-element.32), channel_id=1, source_target_pairs={{0,4},{2,6},{4,0},{6,2},{1,5},{3,7},{5,1},{7,3},{8,12},{10,14},{12... | collective-permute-start | bytes 2555912 | tf_op jit(solution)/shard_map/ppermute | solution.py:39
  208.1 40.3 %collective-permute-start.8 = (bf16[256,1664]{1,0:T(8,128)(2,1)}, bf16[256,1664]{1,0:T(8,128)(2,1)S(1)}, u32[]{:S(2)}, u32[]{:S(2)}) collective-permute-start(bf16[256,1664]{1,0:T(8,128)(2,1)} %get-tuple-element.33), channel_id=1, source_target_pairs={{0,6},{2,0},{4,2},{6,4},{1,7},{3,1},{5,3},{7,5},{8,14},{10,8},{12,... | collective-permute-start | bytes 2555912 | tf_op jit(solution)/shard_map/ppermute | solution.py:39
  215.2 40.5 %all-to-all-start.3 = ((f32[64,1,128]{2,1,0:T(1,128)}), f32[64,1,128]{2,1,0:T(1,128)S(1)}, u32[]{:S(2)}, u32[]{:S(2)}) async-start(f32[64,1,128]{2,1,0:T(1,128)} %bitcast.36), calls=%async_computation.3 | async-start | bytes 65536 | tf_op jit(solution)/shard_map/all_to_all | solution.py:30
  225.3 23.1 %copy-start.5 = (bf16[256,1664]{1,0:T(8,128)(2,1)}, bf16[256,1664]{1,0:T(8,128)(2,1)S(1)}, u32[]{:S(2)}) copy-start(bf16[256,1664]{1,0:T(8,128)(2,1)S(1)} %collective-permute-done.6.refs_5_) | copy-start | bytes 2555908
  227.7 20.7 %copy-start.6 = (bf16[256,1664]{1,0:T(8,128)(2,1)}, bf16[256,1664]{1,0:T(8,128)(2,1)S(1)}, u32[]{:S(2)}) copy-start(bf16[256,1664]{1,0:T(8,128)(2,1)S(1)} %collective-permute-done.7.refs_6_) | copy-start | bytes 2555908
  248.4 0.9 copy-start.7

commit v7 on v6

--- a/solution.py
+++ b/solution.py
@@ -73,9 +73,9 @@
             out[half, k, :, cols - LANES :] = tail
 
 
-def pack_inputs_body(place, layer_in, latent, kept, sent, rest):
-    tokens, half_cols = kept.shape
-    ranks = latent.shape[1]
+def pack_inputs_body(place, layer_in, kept, sent):
+    tokens, cols = kept.shape
+    half_cols = cols - LANES
     width = layer_in.shape[1]
     block = BLOCK
     first = place[0] == 0
@@ -93,20 +93,19 @@
         high = layer_in[:, (2 * i + 1) * block : (2 * i + 2) * block]
         kept[:, i * block : (i + 1) * block] = jnp.where(first, low, high)
         sent[:, i * block : (i + 1) * block] = jnp.where(first, high, low)
-    rest[:, :ranks] = latent[...]
-    rest[:, ranks:] = tail.astype(jnp.bfloat16)
-
-
-def activate_body(place, kept, other, up, act, scale, out):
+    tail = tail.astype(jnp.bfloat16)
+    kept[:, half_cols:] = tail
+    sent[:, half_cols:] = tail
+
+
+def activate_body(place, kept, other, up, act, slopes_out, out):
     sections, halves, rows, ranks = act.shape
     first = place[0] == 0
     for half in range(halves):
         near, far = (kept[...], other[...]) if half == 0 else (other[...], kept[...])
-        rest = jnp.where(first, near, far).astype(jnp.float32)
-        values, slopes = gelu_pair(rest[:, :, :ranks])
-        inv_rms = jnp.sum(rest[:, :, ranks:], axis=2, keepdims=True)
+        values, slopes = gelu_pair(jnp.where(first, near, far).astype(jnp.float32))
         act[:, half] = values.astype(jnp.bfloat16)
-        scale[:, half] = slopes * inv_rms
+        slopes_out[:, half] = slopes
     out[:, :BLOCK] = up[...]
     whole_act = act[...].reshape(sections * halves * rows, ranks).astype(jnp.float32)
     out[:, BLOCK:] = jnp.transpose(whole_act).astype(jnp.bfloat16)
@@ -120,11 +119,15 @@
         out[:, i * BLOCK : (i + 1) * BLOCK] = jnp.where(turn < 2, near, far)
 
 
-def lift_body(place, kept, other, act, up_half, mixed, sends, inputs):
+def lift_body(place, kept, other, act, slopes, up_half, mixed, sends, inputs, scale):
     del mixed
     sections, halves, rows, width = sends.shape
     ranks = up_half.shape[0]
     first = place[0] == 0
+    for half in range(halves):
+        near, far = (kept, other) if half == 0 else (other, kept)
+        terms = jnp.where(first, near[:, :, width:], far[:, :, width:]).astype(jnp.float32)
+        scale[:, half] = slopes[:, half] * jnp.sum(terms, axis=2, keepdims=True)
     for at in range(0, width, BLOCK):
         lanes = slice(at, at + BLOCK)
         for half in range(halves):
@@ -234,22 +237,20 @@
     grads = exchange(packed.reshape(zs * sections, rows, half_width + LANES), ("zh", *GROUP))
     grads = grads.reshape(zs, sections, rows, half_width + LANES)
 
-    rest = ranks + LANES
-    kept, sent, kept_rest = pl.pallas_call(
+    full = half_width + LANES
+    kept, sent = pl.pallas_call(
         pack_inputs_body,
-        in_specs=[SMEM, pl.BlockSpec((tokens, width), lambda: (0, 0)), pl.BlockSpec((tokens, ranks), lambda: (0, 0))],
-        out_specs=[pl.BlockSpec((tokens, half_width), lambda: (0, 0))] * 2
-        + [pl.BlockSpec((tokens, rest), lambda: (0, 0))],
-        out_shape=[shape((tokens, half_width))] * 2 + [shape((tokens, rest))],
+        in_specs=[SMEM, pl.BlockSpec((tokens, width), lambda: (0, 0))],
+        out_specs=[pl.BlockSpec((tokens, full), lambda: (0, 0))] * 2,
+        out_shape=[shape((tokens, full))] * 2,
         name="pack_inputs",
-    )(place, layer_in, latent)
-    other_rest = swapped(kept_rest, "zh")
+    )(place, layer_in)
     other = swapped(sent, "zh")
-
-    kept, other, kept_rest, other_rest = [
-        t.reshape(sections, rows, t.shape[1]) for t in (kept, other, kept_rest, other_rest)
+    other_latent = swapped(latent, "zh")
+    kept, other, latent, other_latent = [
+        t.reshape(sections, rows, t.shape[1]) for t in (kept, other, latent, other_latent)
     ]
-    act, scale, up_part = pl.pallas_call(
+    act, slopes, up_part = pl.pallas_call(
         activate_body,
         in_specs=[SMEM] + [VMEM] * 3,
         out_specs=[VMEM] * 3,
@@ -259,8 +260,7 @@
             shape((ranks, block + zs * tokens)),
         ],
         name="activate",
-    )(place, kept_rest, other_rest, up_proj[0])
-    scale = scale.reshape(zs * tokens, ranks)
+    )(place, latent, other_latent, up_proj[0])
 
     ups = [up_part]
     for step in range(1, xs):
@@ -278,13 +278,14 @@
     mixed = pl.pallas_call(mix_body, in_specs=[SMEM, VMEM], out_specs=VMEM, out_shape=chunk, name="mix")(weights, grads)
     arrived = exchange(mixed, GROUP)
 
-    layer_out, inputs = pl.pallas_call(
+    layer_out, inputs, scale = pl.pallas_call(
         lift_body,
-        in_specs=[SMEM] + [VMEM] * 4 + [pl.BlockSpec(memory_space=pl.ANY)],
-        out_specs=[VMEM] * 2,
-        out_shape=[chunk] * 2,
+        in_specs=[SMEM] + [VMEM] * 5 + [pl.BlockSpec(memory_space=pl.ANY)],
+        out_specs=[VMEM] * 3,
+        out_shape=[chunk] * 2 + [shape((sections, zs, rows, ranks), jnp.float32)],
         name="lift",
-    )(place, kept, other, act, up_half, mixed)
+    )(place, kept, other, act, slopes, up_half, mixed)
+    scale = scale.reshape(zs * tokens, ranks)
 
     layer_out, arrived = lax.optimization_barrier((layer_out, arrived))
     outs = exchange(layer_out, GROUP)

time: 257 us -> 256 us (level)
  starting transfers between devices: 71.7 us -> 66.4 us
  waiting for transfers between devices: 87.6 us -> 91.3 us
    all_to_all x3, starting transfers between devices: 39.9 us -> 33.6 us  [exchange(): return lax.all_to_all(pieces, axes, split_axis=0, concat_axis=0, tiled=True)]
    ppermute x3, waiting for transfers between devices: 40 us -> 44.1 us  [swapped(): return lax.ppermute(value, axis, [(0, 1), (1, 0)])]
  transfers between devices with their start and end apart: 12 -> 12, of which waited for: 7 -> 8; matrix products, arithmetic and copies ran while one was open for 1% -> 1% of each run, Pallas kernels for 10% -> 11%
where the time goes in v7:
time: 256 us; the launch traced here: 255 us
  waiting for transfers between devices  91.3 us (36%)
  starting transfers between devices  66.4 us (26%)
  blocking collectives  56.4 us (22%)
  Pallas kernels  33.1 us (13%)
  local copies, waits for them, and re-layouts  4.15 us (2%)
    all_to_all x1, blocking collectives, exchange(): return lax.all_to_all(pieces, axes, split_axis=0, concat_axis=0, tiled=True)  56.4 us
    ppermute x6, waiting for transfers between devices, shifted(): lax.ppermute(value, axis, [(i, (i + steps) % count) for i in range(count)])  47.2 us
    ppermute x3, waiting for transfers between devices, swapped(): return lax.ppermute(value, axis, [(0, 1), (1, 0)])  44.1 us
    all_to_all x3, starting transfers between devices, exchange(): return lax.all_to_all(pieces, axes, split_axis=0, concat_axis=0, tiled=True)  33.6 us
    ppermute x6, starting transfers between devices, shifted(): lax.ppermute(value, axis, [(i, (i + steps) % count) for i in range(count)])  18.5 us
    ppermute x3, starting transfers between devices, swapped(): return lax.ppermute(value, axis, [(0, 1), (1, 0)])  14.2 us
    pallas_call x1, Pallas kernels, whole(): pl.pallas_call(weights_body, in_specs=[VMEM] * (2 * xs + 2), out_specs=[V...  6.37 us
  transfers between devices with their start and end apart: 12, of which 8 were waited for; matrix products, arithmetic and copies ran while one was open for 1% of the time, Pallas kernels for 11%

profile of v7, /device:TPU:11, one launch (start us, length us, event | category | flops | bytes accessed | tf_op | source)
XLA Modules:
  0.0 255.0 jit_solution(16207668885981051277)
XLA Ops:
  0.6 2.5 pack_grads.1
  3.2 56.4 %all_to_all.24 = bf16[16,16,2688]{2,1,0:T(8,128)(2,1)S(1)} all-to-all(bf16[16,16,2688]{2,1,0:T(8,128)(2,1)} %bitcast.28), channel_id=1, replica_groups=mesh['zl'=4,'yh'=2,'r'=8,'x'=4,'zh'=2] {'zh','zl','yh'}, dimensions={0} | all-to-all | bytes 2752512 | tf_op jit(solution)/shard_map/all_to_all | solution.py:30
  60.6 3.4 %mix.1.mixed = bf16[8,2,16,2560]{3,2,1,0:T(8,128)(2,1)} custom-call(f32[8,8]{1,0:T(8,128)} %convert_reduce_fusion.coef, bf16[2,8,16,2688]{3,2,1,0:T(8,128)(2,1)} %bitcast.25), custom_call_target="tpu_custom_call" | custom-call | tf_op jit(solution)/shard_map/mix/pallas_call | solution.py:278
  64.0 4.2 %all-to-all-start.1 = ((bf16[8,2,16,2560]{3,2,1,0:T(8,128)(2,1)}), bf16[8,2,16,2560]{3,2,1,0:T(8,128)(2,1)S(1)}, u32[]{:S(2)}, u32[]{:S(2)}) async-start(bf16[8,2,16,2560]{3,2,1,0:T(8,128)(2,1)} %mix.1.mixed), calls=%async_computation.1 | async-start | bytes 2621440 | tf_op jit(solution)/shard_map/all_to_all | solution.py:30
  68.2 4.7 %collective-permute-start = (bf16[128,384]{1,0:T(8,128)(2,1)S(1)}, bf16[128,384]{1,0:T(8,128)(2,1)S(1)}, u32[]{:S(2)}, u32[]{:S(2)}) collective-permute-start(bf16[128,384]{1,0:T(8,128)(2,1)S(1)} %bitcast.38), channel_id=1, source_target_pairs={{0,1},{1,0},{2,3},{3,2},{4,5},{5,4},{6,7},{7,6},{8,9},{9,8},{10,11... | collective-permute-start | bytes 294920 | tf_op jit(solution)/shard_map/ppermute | solution.py:34
  73.5 2.9 %pack_inputs.1 = (bf16[128,2688]{1,0:T(8,128)(2,1)}, bf16[128,2688]{1,0:T(8,128)(2,1)}) custom-call(s32[2]{0:T(128)} %pad_add_fusion.place, bf16[128,5120]{1,0:T(8,128)(2,1)} %bitcast.30), custom_call_target="tpu_custom_call" | custom-call | tf_op jit(solution)/shard_map/pack_inputs/pallas_call | solution.py:241
  76.4 8.4 %collective-permute-done = bf16[128,384]{1,0:T(8,128)(2,1)S(1)} collective-permute-done((bf16[128,384]{1,0:T(8,128)(2,1)S(1)}, bf16[128,384]{1,0:T(8,128)(2,1)S(1)}, u32[]{:S(2)}, u32[]{:S(2)}) %collective-permute-start) | collective-permute-done | bytes 98336 | tf_op jit(solution)/shard_map/ppermute | solution.py:34
  85.5 2.5 activate.1
  88.0 3.1 %collective-permute-start.1 = (bf16[384,896]{1,0:T(8,128)(2,1)}, bf16[384,896]{1,0:T(8,128)(2,1)S(1)}, u32[]{:S(2)}, u32[]{:S(2)}) collective-permute-start(bf16[384,896]{1,0:T(8,128)(2,1)} %get-tuple-element.21.up_0.refs_0_), channel_id=1, source_target_pairs={{0,2},{2,4},{4,6},{6,0},{1,3},{3,5},{5,7},{7,1},{8,10},{10,12},{12... | collective-permute-start | bytes 2064392 | tf_op jit(solution)/shard_map/ppermute | solution.py:39
  91.1 2.7 %collective-permute-start.2 = (bf16[384,896]{1,0:T(8,128)(2,1)}, bf16[384,896]{1,0:T(8,128)(2,1)S(1)}, u32[]{:S(2)}, u32[]{:S(2)}) collective-permute-start(bf16[384,896]{1,0:T(8,128)(2,1)} %get-tuple-element.21.up_0.refs_0_), channel_id=1, source_target_pairs={{0,4},{2,6},{4,0},{6,2},{1,5},{3,7},{5,1},{7,3},{8,12},{10,14},{12... | collective-permute-start | bytes 2064392 | tf_op jit(solution)/shard_map/ppermute | solution.py:39
  93.9 3.8 %collective-permute-start.3 = (bf16[384,896]{1,0:T(8,128)(2,1)}, bf16[384,896]{1,0:T(8,128)(2,1)}, u32[]{:S(2)}, u32[]{:S(2)}) collective-permute-start(bf16[384,896]{1,0:T(8,128)(2,1)} %get-tuple-element.21.up_0.refs_0_), channel_id=1, source_target_pairs={{0,6},{2,0},{4,2},{6,4},{1,7},{3,1},{5,3},{7,5},{8,14},{10,8},{12,... | collective-permute-start | bytes 2064392 | tf_op jit(solution)/shard_map/ppermute | solution.py:39
  97.7 5.1 %collective-permute-start.4 = (bf16[128,2688]{1,0:T(8,128)(2,1)}, bf16[128,2688]{1,0:T(8,128)(2,1)S(1)}, u32[]{:S(2)}, u32[]{:S(2)}) collective-permute-start(bf16[128,2688]{1,0:T(8,128)(2,1)} %get-tuple-element.23), channel_id=1, source_target_pairs={{0,1},{1,0},{2,3},{3,2},{4,5},{5,4},{6,7},{7,6},{8,9},{9,8},{10,11... | collective-permute-start | bytes 2064392 | tf_op jit(solution)/shard_map/ppermute | solution.py:34
  102.8 1.6 collective-permute-done.1.up_1.refs_1_
  104.5 4.4 %collective-permute-done.2.up_2.refs_2_ = bf16[384,896]{1,0:T(8,128)(2,1)S(1)} collective-permute-done((bf16[384,896]{1,0:T(8,128)(2,1)}, bf16[384,896]{1,0:T(8,128)(2,1)S(1)}, u32[]{:S(2)}, u32[]{:S(2)}) %collective-permute-start.2) | collective-permute-done | bytes 688160 | tf_op jit(solution)/shard_map/ppermute | solution.py:39
  108.9 18.1 %collective-permute-done.3.up_3.refs_3_ = bf16[384,896]{1,0:T(8,128)(2,1)} collective-permute-done((bf16[384,896]{1,0:T(8,128)(2,1)}, bf16[384,896]{1,0:T(8,128)(2,1)}, u32[]{:S(2)}, u32[]{:S(2)}) %collective-permute-start.3) | collective-permute-done | bytes 688160 | tf_op jit(solution)/shard_map/ppermute | solution.py:39
  127.0 3.4 %up_rows.1.up_half = bf16[384,2560]{1,0:T(8,128)(2,1)} custom-call(s32[2]{0:T(128)} %pad_add_fusion.place, bf16[384,896]{1,0:T(8,128)(2,1)} %get-tuple-element.21.up_0.refs_0_, bf16[384,896]{1,0:T(8,128)(2,1)} %copy-done.3, bf16[384,896]{1,0:T(8,128)(2,1)} %copy-done.4, bf16[384,896]{1,0:T(8,128)(2,1)} %collective-permute-done.3.up_3.refs_3_), custom_call_target="tpu_custom_call" | custom-call | tf_op jit(solution)/shard_map/up_rows/pallas_call | solution.py:268
  130.4 4.3 %collective-permute-done.4 = bf16[128,2688]{1,0:T(8,128)(2,1)S(1)} collective-permute-done((bf16[128,2688]{1,0:T(8,128)(2,1)}, bf16[128,2688]{1,0:T(8,128)(2,1)S(1)}, u32[]{:S(2)}, u32[]{:S(2)}) %collective-permute-start.4) | collective-permute-done | bytes 688160 | tf_op jit(solution)/shard_map/ppermute | solution.py:34
  135.6 4.8 %lift.1 = (bf16[8,2,16,2560]{3,2,1,0:T(8,128)(2,1)}, bf16[8,2,16,2560]{3,2,1,0:T(8,128)(2,1)}, f32[8,2,16,384]{3,2,1,0:T(8,128)}) custom-call(s32[2]{0:T(128)} %pad_add_fusion.place, bf16[8,16,2688]{2,1,0:T(8,128)(2,1)} %bitcast.31, bf16[8,16,2688]{2,1,0:T(8,128)(2,1)} %bitcast.32, bf16[8,2,16,384]{3,2,1,0:T(8,128)(2,1)} %get-tuple-element.24.act, ...), custom_call_target="tpu_custom_call" | custom-call | tf_op jit(solution)/shard_map/lift/pallas_call | solution.py:281
  140.4 19.7 %all-to-all-start.2 = ((bf16[8,2,16,2560]{3,2,1,0:T(8,128)(2,1)}), bf16[8,2,16,2560]{3,2,1,0:T(8,128)(2,1)}, u32[]{:S(2)}, u32[]{:S(2)}) async-start(bf16[8,2,16,2560]{3,2,1,0:T(8,128)(2,1)} %get-tuple-element.37), calls=%async_computation.2 | async-start | bytes 2621440 | tf_op jit(solution)/shard_map/all_to_all | solution.py:30
  160.0 1.6 fusion
  161.6 4.4 %collective-permute-start.5 = (bf16[256,384]{1,0:T(8,128)(2,1)S(1)}, bf16[256,384]{1,0:T(8,128)(2,1)S(1)}, u32[]{:S(2)}, u32[]{:S(2)}) collective-permute-start(bf16[256,384]{1,0:T(8,128)(2,1)S(1)} %get-tuple-element.38), channel_id=1, source_target_pairs={{0,1},{1,0},{2,3},{3,2},{4,5},{5,4},{6,7},{7,6},{8,9},{9,8},{10,11... | collective-permute-start | bytes 589832 | tf_op jit(solution)/shard_map/ppermute | solution.py:34
  166.0 31.4 %collective-permute-done.5.other = bf16[256,384]{1,0:T(8,128)(2,1)S(1)} collective-permute-done((bf16[256,384]{1,0:T(8,128)(2,1)S(1)}, bf16[256,384]{1,0:T(8,128)(2,1)S(1)}, u32[]{:S(2)}, u32[]{:S(2)}) %collective-permute-start.5) | collective-permute-done | bytes 196640 | tf_op jit(solution)/shard_map/ppermute | solution.py:34
  198.1 4.0 %share.1 = (bf16[256,1664]{1,0:T(8,128)(2,1)}, bf16[256,1664]{1,0:T(8,128)(2,1)}, bf16[256,1664]{1,0:T(8,128)(2,1)}, bf16[256,1664]{1,0:T(8,128)(2,1)}) custom-call(s32[2]{0:T(128)} %pad_add_fusion.place, bf16[8,2,16,2560]{3,2,1,0:T(8,128)(2,1)} %get-tuple-element.26.inputs, bf16[8,2,16,2560]{3,2,1,0:T(8,128)(2,1)} %copy-done.2, ...), custom_call_target="tpu_custom_call" | custom-call | tf_op jit(solution)/shard_map/share/pallas_call | solution.py:297
  202.1 1.9 collective-permute-start.6
  204.0 3.0 %collective-permute-start.7 = (bf16[256,1664]{1,0:T(8,128)(2,1)}, bf16[256,1664]{1,0:T(8,128)(2,1)S(1)}, u32[]{:S(2)}, u32[]{:S(2)}) collective-permute-start(bf16[256,1664]{1,0:T(8,128)(2,1)} %get-tuple-element.32), channel_id=1, source_target_pairs={{0,4},{2,6},{4,0},{6,2},{1,5},{3,7},{5,1},{7,3},{8,12},{10,14},{12... | collective-permute-start | bytes 2555912 | tf_op jit(solution)/shard_map/ppermute | solution.py:39
  207.1 4.0 %collective-permute-start.8 = (bf16[256,1664]{1,0:T(8,128)(2,1)}, bf16[256,1664]{1,0:T(8,128)(2,1)S(1)}, u32[]{:S(2)}, u32[]{:S(2)}) collective-permute-start(bf16[256,1664]{1,0:T(8,128)(2,1)} %get-tuple-element.33), channel_id=1, source_target_pairs={{0,6},{2,0},{4,2},{6,4},{1,7},{3,1},{5,3},{7,5},{8,14},{10,8},{12,... | collective-permute-start | bytes 2555912 | tf_op jit(solution)/shard_map/ppermute | solution.py:39
  211.1 3.2 %gram.1 = f32[64,128]{1,0:T(8,128)} custom-call(bf16[2,8,16,2688]{3,2,1,0:T(8,128)(2,1)} %bitcast.26, bf16[8,2,16,2560]{3,2,1,0:T(8,128)(2,1)} %all-to-all-done.2.outs), custom_call_target="tpu_custom_call" | custom-call | tf_op jit(solution)/shard_map/gram/pallas_call | solution.py:309
  214.2 9.8 %all-to-all-start.3 = ((f32[64,1,128]{2,1,0:T(1,128)}), f32[64,1,128]{2,1,0:T(1,128)S(1)}, u32[]{:S(2)}, u32[]{:S(2)}) async-start(f32[64,1,128]{2,1,0:T(1,128)} %bitcast.36), calls=%async_computation.3 | async-start | bytes 65536 | tf_op jit(solution)/shard_map/all_to_all | solution.py:30
  224.0 2.1 collective-permute-done.7.refs_6_
  226.1 21.0 %collective-permute-done.8.refs_7_ = bf16[256,1664]{1,0:T(8,128)(2,1)S(1)} collective-permute-done((bf16[256,1664]{1,0:T(8,128)(2,1)}, bf16[256,1664]{1,0:T(8,128)(2,1)S(1)}, u32[]{:S(2)}, u32[]{:S(2)}) %collective-permute-start.8) | collective-permute-done | bytes 852000 | tf_op jit(solution)/shard_map/ppermute | solution.py:39
  247.1 0.9 copy-done.7
  248.0 6.4 %weights.3 = (bf16[384,640]{1,0:T(8,128)(2,1)}, bf16[640,384]{1,0:T(8,128)(2,1)}, f32[1,640]{1,0:T(1,128)}) custom-call(bf16[384,896]{1,0:T(8,128)(2,1)} %get-tuple-element.21.up_0.refs_0_, bf16[384,896]{1,0:T(8,128)(2,1)} %copy-done.3, bf16[384,896]{1,0:T(8,128)(2,1)} %copy-done.4, bf16[384,896]{1,0:T(8,128)(2,1)} %collective-permute-done.3.up_3.refs_3_, ...), custom_call_target="tpu_custom_call" | custom-call | tf_op jit(solution)/shard_map/weights/pallas_call | solution.py:318
  (31 shorter events, 4.6 us)
Async XLA Ops:
  59.5 1.1 copy-start.1
  64.0 4.2 %copy-start.10 = (bf16[1,128,384]{2,1,0:T(8,128)(2,1)S(1)}, bf16[1,128,384]{2,1,0:T(8,128)(2,1)}, u32[]{:S(2)}) copy-start(bf16[1,128,384]{2,1,0:T(8,128)(2,1)} %param.8) | copy-start | bytes 294916
  64.0 76.3 %all-to-all-start.1 = ((bf16[8,2,16,2560]{3,2,1,0:T(8,128)(2,1)}), bf16[8,2,16,2560]{3,2,1,0:T(8,128)(2,1)S(1)}, u32[]{:S(2)}, u32[]{:S(2)}) async-start(bf16[8,2,16,2560]{3,2,1,0:T(8,128)(2,1)} %mix.1.mixed), calls=%async_computation.1 | async-start | bytes 2621440 | tf_op jit(solution)/shard_map/all_to_all | solution.py:30
  68.2 16.7 %collective-permute-start = (bf16[128,384]{1,0:T(8,128)(2,1)S(1)}, bf16[128,384]{1,0:T(8,128)(2,1)S(1)}, u32[]{:S(2)}, u32[]{:S(2)}) collective-permute-start(bf16[128,384]{1,0:T(8,128)(2,1)S(1)} %bitcast.38), channel_id=1, source_target_pairs={{0,1},{1,0},{2,3},{3,2},{4,5},{5,4},{6,7},{7,6},{8,9},{9,8},{10,11... | collective-permute-start | bytes 294920 | tf_op jit(solution)/shard_map/ppermute | solution.py:34
  84.9 0.6 copy-start.11
  88.0 16.4 %collective-permute-start.1 = (bf16[384,896]{1,0:T(8,128)(2,1)}, bf16[384,896]{1,0:T(8,128)(2,1)S(1)}, u32[]{:S(2)}, u32[]{:S(2)}) collective-permute-start(bf16[384,896]{1,0:T(8,128)(2,1)} %get-tuple-element.21.up_0.refs_0_), channel_id=1, source_target_pairs={{0,2},{2,4},{4,6},{6,0},{1,3},{3,5},{5,7},{7,1},{8,10},{10,12},{12... | collective-permute-start | bytes 2064392 | tf_op jit(solution)/shard_map/ppermute | solution.py:39
  91.1 17.7 %collective-permute-start.2 = (bf16[384,896]{1,0:T(8,128)(2,1)}, bf16[384,896]{1,0:T(8,128)(2,1)S(1)}, u32[]{:S(2)}, u32[]{:S(2)}) collective-permute-start(bf16[384,896]{1,0:T(8,128)(2,1)} %get-tuple-element.21.up_0.refs_0_), channel_id=1, source_target_pairs={{0,4},{2,6},{4,0},{6,2},{1,5},{3,7},{5,1},{7,3},{8,12},{10,14},{12... | collective-permute-start | bytes 2064392 | tf_op jit(solution)/shard_map/ppermute | solution.py:39
  93.9 33.1 %collective-permute-start.3 = (bf16[384,896]{1,0:T(8,128)(2,1)}, bf16[384,896]{1,0:T(8,128)(2,1)}, u32[]{:S(2)}, u32[]{:S(2)}) collective-permute-start(bf16[384,896]{1,0:T(8,128)(2,1)} %get-tuple-element.21.up_0.refs_0_), channel_id=1, source_target_pairs={{0,6},{2,0},{4,2},{6,4},{1,7},{3,1},{5,3},{7,5},{8,14},{10,8},{12,... | collective-permute-start | bytes 2064392 | tf_op jit(solution)/shard_map/ppermute | solution.py:39
  97.7 37.0 %collective-permute-start.4 = (bf16[128,2688]{1,0:T(8,128)(2,1)}, bf16[128,2688]{1,0:T(8,128)(2,1)S(1)}, u32[]{:S(2)}, u32[]{:S(2)}) collective-permute-start(bf16[128,2688]{1,0:T(8,128)(2,1)} %get-tuple-element.23), channel_id=1, source_target_pairs={{0,1},{1,0},{2,3},{3,2},{4,5},{5,4},{6,7},{7,6},{8,9},{9,8},{10,11... | collective-permute-start | bytes 2064392 | tf_op jit(solution)/shard_map/ppermute | solution.py:34
  104.5 22.5 %copy-start.3 = (bf16[384,896]{1,0:T(8,128)(2,1)}, bf16[384,896]{1,0:T(8,128)(2,1)S(1)}, u32[]{:S(2)}) copy-start(bf16[384,896]{1,0:T(8,128)(2,1)S(1)} %collective-permute-done.1.up_1.refs_1_) | copy-start | bytes 2064388
  108.9 18.1 %copy-start.4 = (bf16[384,896]{1,0:T(8,128)(2,1)}, bf16[384,896]{1,0:T(8,128)(2,1)S(1)}, u32[]{:S(2)}) copy-start(bf16[384,896]{1,0:T(8,128)(2,1)S(1)} %collective-permute-done.2.up_2.refs_2_) | copy-start | bytes 2064388
  134.7 0.9 copy-start.8
  140.3 19.7 %copy-start.2 = (bf16[8,2,16,2560]{3,2,1,0:T(8,128)(2,1)}, bf16[8,2,16,2560]{3,2,1,0:T(8,128)(2,1)S(1)}, u32[]{:S(2)}) copy-start(bf16[8,2,16,2560]{3,2,1,0:T(8,128)(2,1)S(1)} %all-to-all-done.1.grads) | copy-start | bytes 3932164
  140.3 19.7 %copy-start = (bf16[384,2560]{1,0:T(8,128)(2,1)S(1)}, bf16[384,2560]{1,0:T(8,128)(2,1)}, u32[]{:S(2)}) copy-start(bf16[384,2560]{1,0:T(8,128)(2,1)} %up_rows.1.up_half) | copy-start | bytes 5898244
  140.4 70.7 %all-to-all-start.2 = ((bf16[8,2,16,2560]{3,2,1,0:T(8,128)(2,1)}), bf16[8,2,16,2560]{3,2,1,0:T(8,128)(2,1)}, u32[]{:S(2)}, u32[]{:S(2)}) async-start(bf16[8,2,16,2560]{3,2,1,0:T(8,128)(2,1)} %get-tuple-element.37), calls=%async_computation.2 | async-start | bytes 2621440 | tf_op jit(solution)/shard_map/all_to_all | solution.py:30
  161.6 35.8 %collective-permute-start.5 = (bf16[256,384]{1,0:T(8,128)(2,1)S(1)}, bf16[256,384]{1,0:T(8,128)(2,1)S(1)}, u32[]{:S(2)}, u32[]{:S(2)}) collective-permute-start(bf16[256,384]{1,0:T(8,128)(2,1)S(1)} %get-tuple-element.38), channel_id=1, source_target_pairs={{0,1},{1,0},{2,3},{3,2},{4,5},{5,4},{6,7},{7,6},{8,9},{9,8},{10,11... | collective-permute-start | bytes 589832 | tf_op jit(solution)/shard_map/ppermute | solution.py:34
  197.4 0.7 copy-start.9
  202.1 21.9 %collective-permute-start.6 = (bf16[256,1664]{1,0:T(8,128)(2,1)}, bf16[256,1664]{1,0:T(8,128)(2,1)S(1)}, u32[]{:S(2)}, u32[]{:S(2)}) collective-permute-start(bf16[256,1664]{1,0:T(8,128)(2,1)} %get-tuple-element.31), channel_id=1, source_target_pairs={{0,2},{2,4},{4,6},{6,0},{1,3},{3,5},{5,7},{7,1},{8,10},{10,12},{12... | collective-permute-start | bytes 2555912 | tf_op jit(solution)/shard_map/ppermute | solution.py:39
  204.0 22.1 %collective-permute-start.7 = (bf16[256,1664]{1,0:T(8,128)(2,1)}, bf16[256,1664]{1,0:T(8,128)(2,1)S(1)}, u32[]{:S(2)}, u32[]{:S(2)}) collective-permute-start(bf16[256,1664]{1,0:T(8,128)(2,1)} %get-tuple-element.32), channel_id=1, source_target_pairs={{0,4},{2,6},{4,0},{6,2},{1,5},{3,7},{5,1},{7,3},{8,12},{10,14},{12... | collective-permute-start | bytes 2555912 | tf_op jit(solution)/shard_map/ppermute | solution.py:39
  207.1 40.0 %collective-permute-start.8 = (bf16[256,1664]{1,0:T(8,128)(2,1)}, bf16[256,1664]{1,0:T(8,128)(2,1)S(1)}, u32[]{:S(2)}, u32[]{:S(2)}) collective-permute-start(bf16[256,1664]{1,0:T(8,128)(2,1)} %get-tuple-element.33), channel_id=1, source_target_pairs={{0,6},{2,0},{4,2},{6,4},{1,7},{3,1},{5,3},{7,5},{8,14},{10,8},{12,... | collective-permute-start | bytes 2555912 | tf_op jit(solution)/shard_map/ppermute | solution.py:39
  214.2 40.2 %all-to-all-start.3 = ((f32[64,1,128]{2,1,0:T(1,128)}), f32[64,1,128]{2,1,0:T(1,128)S(1)}, u32[]{:S(2)}, u32[]{:S(2)}) async-start(f32[64,1,128]{2,1,0:T(1,128)} %bitcast.36), calls=%async_computation.3 | async-start | bytes 65536 | tf_op jit(solution)/shard_map/all_to_all | solution.py:30
  224.0 23.1 %copy-start.5 = (bf16[256,1664]{1,0:T(8,128)(2,1)}, bf16[256,1664]{1,0:T(8,128)(2,1)S(1)}, u32[]{:S(2)}) copy-start(bf16[256,1664]{1,0:T(8,128)(2,1)S(1)} %collective-permute-done.6.refs_5_) | copy-start | bytes 2555908
  226.1 21.0 %copy-start.6 = (bf16[256,1664]{1,0:T(8,128)(2,1)}, bf16[256,1664]{1,0:T(8,128)(2,1)S(1)}, u32[]{:S(2)}) copy-start(bf16[256,1664]{1,0:T(8,128)(2,1)S(1)} %collective-permute-done.7.refs_6_) | copy-start | bytes 2555908
  247.1 0.9 copy-start.7

commit v8 on v7

--- a/solution.py
+++ b/solution.py
@@ -119,7 +119,7 @@
         out[:, i * BLOCK : (i + 1) * BLOCK] = jnp.where(turn < 2, near, far)
 
 
-def lift_body(place, kept, other, act, slopes, up_half, mixed, sends, inputs, scale):
+def lift_body(place, kept, other, act, slopes, up_half, mixed, sends, scale, *moved):
     del mixed
     sections, halves, rows, width = sends.shape
     ranks = up_half.shape[0]
@@ -128,12 +128,14 @@
         near, far = (kept, other) if half == 0 else (other, kept)
         terms = jnp.where(first, near[:, :, width:], far[:, :, width:]).astype(jnp.float32)
         scale[:, half] = slopes[:, half] * jnp.sum(terms, axis=2, keepdims=True)
+        for step, out in enumerate(moved):
+            at = pl.multiple_of(lax.rem(place[1] + step, len(moved)) * BLOCK, LANES)
+            out[:, half] = jnp.where(first, near[:, :, pl.ds(at, BLOCK)], far[:, :, pl.ds(at, BLOCK)])
     for at in range(0, width, BLOCK):
         lanes = slice(at, at + BLOCK)
         for half in range(halves):
             near, far = (kept, other) if half == 0 else (other, kept)
             rows_in = jnp.where(first, near[:, :, lanes], far[:, :, lanes])
-            inputs[:, half, :, lanes] = rows_in
             branch = jnp.dot(
                 act[:, half].reshape(sections * rows, ranks), up_half[:, lanes], preferred_element_type=jnp.float32
             ).reshape(sections, rows, BLOCK)
@@ -181,29 +183,26 @@
     )
 
 
-def share_body(place, inputs, grads, partial, other, scale, *outs):
+def share_body(place, grads, partial, other, scale, *outs):
     sections, halves, rows, _ = grads.shape
     count = sections * halves * rows
     latent_grad = ((partial[...] + other[...].astype(jnp.float32)) * scale[...]).astype(jnp.bfloat16)
     for step, out in enumerate(outs):
         at = pl.multiple_of(lax.rem(place[1] + step, len(outs)) * BLOCK, LANES)
-        out[:, :BLOCK] = inputs[:, :, :, pl.ds(at, BLOCK)].reshape(count, BLOCK)
-        out[:, BLOCK : 2 * BLOCK] = grads[:, :, :, pl.ds(at, BLOCK)].reshape(count, BLOCK)
-        out[:, 2 * BLOCK :] = latent_grad
+        out[:, :BLOCK] = grads[:, :, :, pl.ds(at, BLOCK)].reshape(count, BLOCK)
+        out[:, BLOCK:] = latent_grad
 
 
 def weights_body(*refs):
-    half = (len(refs) - 5) // 2
-    acts, shared = refs[:half], refs[half : 2 * half]
-    gain, down, up_out, down_out, gain_out = refs[2 * half :]
+    each = (len(refs) - 5) // 3
+    acts, moved, shared = refs[:each], refs[each : 2 * each], refs[2 * each : 3 * each]
+    gain, down, up_out, down_out, gain_out = refs[3 * each :]
     up_total = jnp.zeros(up_out.shape, jnp.float32)
     down_total = jnp.zeros(down_out.shape, jnp.float32)
-    for act, piece in zip(acts, shared):
-        up_total = up_total + jnp.dot(
-            act[:, BLOCK:], piece[:, BLOCK : 2 * BLOCK], preferred_element_type=jnp.float32
-        )
+    for act, inputs, piece in zip(acts, moved, shared):
+        up_total = up_total + jnp.dot(act[:, BLOCK:], piece[:, :BLOCK], preferred_element_type=jnp.float32)
         down_total = down_total + lax.dot_general(
-            piece[:, :BLOCK], piece[:, 2 * BLOCK :], (((0,), (0,)), ((), ())), preferred_element_type=jnp.float32
+            inputs[...], piece[:, BLOCK:], (((0,), (0,)), ((), ())), preferred_element_type=jnp.float32
         )
     up_out[...] = up_total.astype(jnp.bfloat16)
     gain_cols = jnp.transpose(jnp.broadcast_to(gain[...].astype(jnp.float32), (8, gain.shape[1])))
@@ -278,14 +277,18 @@
     mixed = pl.pallas_call(mix_body, in_specs=[SMEM, VMEM], out_specs=VMEM, out_shape=chunk, name="mix")(weights, grads)
     arrived = exchange(mixed, GROUP)
 
-    layer_out, inputs, scale = pl.pallas_call(
+    layer_out, scale, *moved = pl.pallas_call(
         lift_body,
         in_specs=[SMEM] + [VMEM] * 5 + [pl.BlockSpec(memory_space=pl.ANY)],
-        out_specs=[VMEM] * 3,
-        out_shape=[chunk] * 2 + [shape((sections, zs, rows, ranks), jnp.float32)],
+        out_specs=[VMEM] * (2 + xs),
+        out_shape=[chunk, shape((sections, zs, rows, ranks), jnp.float32)] + [shape((sections, zs, rows, block))] * xs,
         name="lift",
     )(place, kept, other, act, slopes, up_half, mixed)
     scale = scale.reshape(zs * tokens, ranks)
+    for step in range(xs):
+        moved[step] = moved[step].reshape(zs * tokens, block)
+        if step:
+            moved[step] = shifted(moved[step], "x", step)
 
     layer_out, arrived = lax.optimization_barrier((layer_out, arrived))
     outs = exchange(layer_out, GROUP)
@@ -296,11 +299,11 @@
     act_other = swapped(act_partial.astype(jnp.bfloat16), "zh")
     shares = pl.pallas_call(
         share_body,
-        in_specs=[SMEM] + [VMEM] * 5,
+        in_specs=[SMEM] + [VMEM] * 4,
         out_specs=[VMEM] * xs,
-        out_shape=[shape((zs * tokens, 2 * block + ranks))] * xs,
+        out_shape=[shape((zs * tokens, block + ranks))] * xs,
         name="share",
-    )(place, inputs, arrived, act_partial, act_other, scale)
+    )(place, arrived, act_partial, act_other, scale)
     shares = list(shares)
     for step in range(1, xs):
         shares[step] = shifted(shares[step], "x", step)
@@ -317,11 +320,11 @@
 
     up_grad, down_grad, gain_grad = pl.pallas_call(
         weights_body,
-        in_specs=[VMEM] * (2 * xs + 2),
+        in_specs=[VMEM] * (3 * xs + 2),
         out_specs=[VMEM] * 3,
         out_shape=[shape((ranks, block)), shape((block, ranks)), shape((1, block), jnp.float32)],
         name="weights",
-    )(*ups, *shares, norm_gain, down_proj[0])
+    )(*ups, *moved, *shares, norm_gain, down_proj[0])
     return (up_grad[None], down_grad[None], gain_grad, mixing[None])
 
 

time: 256 us -> 253 us (0.988)
  waiting for transfers between devices: 91.3 us -> 79 us
  starting transfers between devices: 66.4 us -> 76.8 us
    ppermute x6 -> x9, waiting for transfers between devices: 47.2 us -> 37.3 us  [shifted(): lax.ppermute(value, axis, [(i, (i + steps) % count) for i in range(count)])]
    ppermute x6 -> x9, starting transfers between devices: 18.5 us -> 26.7 us  [shifted(): lax.ppermute(value, axis, [(i, (i + steps) % count) for i in range(count)])]
  transfers between devices with their start and end apart: 12 -> 15, of which waited for: 8 -> 8; matrix products, arithmetic and copies ran while one was open for 1% -> 1% of each run, Pallas kernels for 11% -> 10%
where the time goes in v8:
time: 253 us
  waiting for transfers between devices  79 us (31%)
  starting transfers between devices  76.8 us (30%)
  blocking collectives  56.4 us (22%)
  Pallas kernels  32.1 us (13%)
  local copies, waits for them, and re-layouts  4.42 us (2%)
    all_to_all x1, blocking collectives, exchange(): return lax.all_to_all(pieces, axes, split_axis=0, concat_axis=0, tiled=True)  56.4 us
    ppermute x3, waiting for transfers between devices, swapped(): return lax.ppermute(value, axis, [(0, 1), (1, 0)])  41.7 us
    ppermute x9, waiting for transfers between devices, shifted(): lax.ppermute(value, axis, [(i, (i + steps) % count) for i in range(count)])  37.3 us
    all_to_all x3, starting transfers between devices, exchange(): return lax.all_to_all(pieces, axes, split_axis=0, concat_axis=0, tiled=True)  35.7 us
    ppermute x9, starting transfers between devices, shifted(): lax.ppermute(value, axis, [(i, (i + steps) % count) for i in range(count)])  26.7 us
    ppermute x3, starting transfers between devices, swapped(): return lax.ppermute(value, axis, [(0, 1), (1, 0)])  14.3 us
    pallas_call x1, Pallas kernels, whole(): pl.pallas_call(weights_body, in_specs=[VMEM] * (3 * xs + 2), out_specs=[V...  6.37 us
  transfers between devices with their start and end apart: 15, of which 8 were waited for; matrix products, arithmetic and copies ran while one was open for 1% of the time, Pallas kernels for 10%

profile of v8, /device:TPU:11, one launch (start us, length us, event | category | flops | bytes accessed | tf_op | source)
XLA Modules:
  0.0 252.5 jit_solution(8476260410512984066)
XLA Ops:
  0.6 2.5 %pack_grads.1 = bf16[2,8,16,2688]{3,2,1,0:T(8,128)(2,1)} custom-call(f32[1,8]{1,0:T(1,128)} %weights.2, bf16[128,5120]{1,0:T(8,128)(2,1)} %bitcast.33), custom_call_target="tpu_custom_call" | custom-call | tf_op jit(solution)/shard_map/pack_grads/pallas_call | solution.py:229
  3.2 56.4 %all_to_all.24 = bf16[16,16,2688]{2,1,0:T(8,128)(2,1)S(1)} all-to-all(bf16[16,16,2688]{2,1,0:T(8,128)(2,1)} %bitcast.32), channel_id=1, replica_groups=mesh['zl'=4,'yh'=2,'r'=8,'x'=4,'zh'=2] {'zh','zl','yh'}, dimensions={0} | all-to-all | bytes 2752512 | tf_op jit(solution)/shard_map/all_to_all | solution.py:30
  60.6 3.4 %mix.1.mixed = bf16[8,2,16,2560]{3,2,1,0:T(8,128)(2,1)} custom-call(f32[8,8]{1,0:T(8,128)} %convert_reduce_fusion.coef, bf16[2,8,16,2688]{3,2,1,0:T(8,128)(2,1)} %bitcast.29), custom_call_target="tpu_custom_call" | custom-call | tf_op jit(solution)/shard_map/mix/pallas_call | solution.py:277
  64.0 4.2 %all-to-all-start.1 = ((bf16[8,2,16,2560]{3,2,1,0:T(8,128)(2,1)}), bf16[8,2,16,2560]{3,2,1,0:T(8,128)(2,1)S(1)}, u32[]{:S(2)}, u32[]{:S(2)}) async-start(bf16[8,2,16,2560]{3,2,1,0:T(8,128)(2,1)} %mix.1.mixed), calls=%async_computation.1 | async-start | bytes 2621440 | tf_op jit(solution)/shard_map/all_to_all | solution.py:30
  68.2 4.7 %collective-permute-start = (bf16[128,384]{1,0:T(8,128)(2,1)S(1)}, bf16[128,384]{1,0:T(8,128)(2,1)S(1)}, u32[]{:S(2)}, u32[]{:S(2)}) collective-permute-start(bf16[128,384]{1,0:T(8,128)(2,1)S(1)} %bitcast.42), channel_id=1, source_target_pairs={{0,1},{1,0},{2,3},{3,2},{4,5},{5,4},{6,7},{7,6},{8,9},{9,8},{10,11... | collective-permute-start | bytes 294920 | tf_op jit(solution)/shard_map/ppermute | solution.py:34
  73.5 2.8 %pack_inputs.1 = (bf16[128,2688]{1,0:T(8,128)(2,1)}, bf16[128,2688]{1,0:T(8,128)(2,1)}) custom-call(s32[2]{0:T(128)} %pad_add_fusion.place, bf16[128,5120]{1,0:T(8,128)(2,1)} %bitcast.34), custom_call_target="tpu_custom_call" | custom-call | tf_op jit(solution)/shard_map/pack_inputs/pallas_call | solution.py:240
  76.3 8.5 %collective-permute-done = bf16[128,384]{1,0:T(8,128)(2,1)S(1)} collective-permute-done((bf16[128,384]{1,0:T(8,128)(2,1)S(1)}, bf16[128,384]{1,0:T(8,128)(2,1)S(1)}, u32[]{:S(2)}, u32[]{:S(2)}) %collective-permute-start) | collective-permute-done | bytes 98336 | tf_op jit(solution)/shard_map/ppermute | solution.py:34
  85.5 2.6 %activate.1 = (bf16[8,2,16,384]{3,2,1,0:T(8,128)(2,1)}, f32[8,2,16,384]{3,2,1,0:T(8,128)}, bf16[384,896]{1,0:T(8,128)(2,1)}) custom-call(s32[2]{0:T(128)} %pad_add_fusion.place, bf16[8,16,384]{2,1,0:T(8,128)(2,1)} %bitcast.41, bf16[8,16,384]{2,1,0:T(8,128)(2,1)} %bitcast.43, bf16[384,640]{1,0:T(8,128)(2,1)} %bitcast.36), custom_call_target="tpu_custom_call" | custom-call | tf_op jit(solution)/shard_map/activate/pallas_call | solution.py:252
  88.1 3.1 %collective-permute-start.1 = (bf16[384,896]{1,0:T(8,128)(2,1)}, bf16[384,896]{1,0:T(8,128)(2,1)S(1)}, u32[]{:S(2)}, u32[]{:S(2)}) collective-permute-start(bf16[384,896]{1,0:T(8,128)(2,1)} %get-tuple-element.24.up_0.refs_0_), channel_id=1, source_target_pairs={{0,2},{2,4},{4,6},{6,0},{1,3},{3,5},{5,7},{7,1},{8,10},{10,12},{12... | collective-permute-start | bytes 2064392 | tf_op jit(solution)/shard_map/ppermute | solution.py:39
  91.2 2.7 %collective-permute-start.2 = (bf16[384,896]{1,0:T(8,128)(2,1)}, bf16[384,896]{1,0:T(8,128)(2,1)S(1)}, u32[]{:S(2)}, u32[]{:S(2)}) collective-permute-start(bf16[384,896]{1,0:T(8,128)(2,1)} %get-tuple-element.24.up_0.refs_0_), channel_id=1, source_target_pairs={{0,4},{2,6},{4,0},{6,2},{1,5},{3,7},{5,1},{7,3},{8,12},{10,14},{12... | collective-permute-start | bytes 2064392 | tf_op jit(solution)/shard_map/ppermute | solution.py:39
  94.0 3.8 %collective-permute-start.3 = (bf16[384,896]{1,0:T(8,128)(2,1)}, bf16[384,896]{1,0:T(8,128)(2,1)S(1)}, u32[]{:S(2)}, u32[]{:S(2)}) collective-permute-start(bf16[384,896]{1,0:T(8,128)(2,1)} %get-tuple-element.24.up_0.refs_0_), channel_id=1, source_target_pairs={{0,6},{2,0},{4,2},{6,4},{1,7},{3,1},{5,3},{7,5},{8,14},{10,8},{12,... | collective-permute-start | bytes 2064392 | tf_op jit(solution)/shard_map/ppermute | solution.py:39
  97.7 5.1 %collective-permute-start.4 = (bf16[128,2688]{1,0:T(8,128)(2,1)}, bf16[128,2688]{1,0:T(8,128)(2,1)}, u32[]{:S(2)}, u32[]{:S(2)}) collective-permute-start(bf16[128,2688]{1,0:T(8,128)(2,1)} %get-tuple-element.26), channel_id=1, source_target_pairs={{0,1},{1,0},{2,3},{3,2},{4,5},{5,4},{6,7},{7,6},{8,9},{9,8},{10,11... | collective-permute-start | bytes 2064392 | tf_op jit(solution)/shard_map/ppermute | solution.py:34
  104.5 4.4 %collective-permute-done.2.up_2.refs_2_ = bf16[384,896]{1,0:T(8,128)(2,1)S(1)} collective-permute-done((bf16[384,896]{1,0:T(8,128)(2,1)}, bf16[384,896]{1,0:T(8,128)(2,1)S(1)}, u32[]{:S(2)}, u32[]{:S(2)}) %collective-permute-start.2) | collective-permute-done | bytes 688160 | tf_op jit(solution)/shard_map/ppermute | solution.py:39
  109.0 18.1 %collective-permute-done.3.up_3.refs_3_ = bf16[384,896]{1,0:T(8,128)(2,1)S(1)} collective-permute-done((bf16[384,896]{1,0:T(8,128)(2,1)}, bf16[384,896]{1,0:T(8,128)(2,1)S(1)}, u32[]{:S(2)}, u32[]{:S(2)}) %collective-permute-start.3) | collective-permute-done | bytes 688160 | tf_op jit(solution)/shard_map/ppermute | solution.py:39
  127.9 3.4 %up_rows.1.up_half = bf16[384,2560]{1,0:T(8,128)(2,1)} custom-call(s32[2]{0:T(128)} %pad_add_fusion.place, bf16[384,896]{1,0:T(8,128)(2,1)} %get-tuple-element.24.up_0.refs_0_, bf16[384,896]{1,0:T(8,128)(2,1)} %copy-done.3, bf16[384,896]{1,0:T(8,128)(2,1)} %copy-done.4, bf16[384,896]{1,0:T(8,128)(2,1)} %copy-done.5), custom_call_target="tpu_custom_call" | custom-call | tf_op jit(solution)/shard_map/up_rows/pallas_call | solution.py:267
  131.3 3.6 %collective-permute-done.4 = bf16[128,2688]{1,0:T(8,128)(2,1)} collective-permute-done((bf16[128,2688]{1,0:T(8,128)(2,1)}, bf16[128,2688]{1,0:T(8,128)(2,1)}, u32[]{:S(2)}, u32[]{:S(2)}) %collective-permute-start.4) | collective-permute-done | bytes 688160 | tf_op jit(solution)/shard_map/ppermute | solution.py:34
  134.9 4.7 %lift.1 = (bf16[8,2,16,2560]{3,2,1,0:T(8,128)(2,1)}, f32[8,2,16,384]{3,2,1,0:T(8,128)}, bf16[8,2,16,640]{3,2,1,0:T(8,128)(2,1)}, bf16[8,2,16,640]{3,2,1,0:T(8,12...) custom-call(s32[2]{0:T(128)} %pad_add_fusion.place, bf16[8,16,2688]{2,1,0:T(8,128)(2,1)} %bitcast.35, ...), custom_call_target="tpu_custom_call" | custom-call | tf_op jit(solution)/shard_map/lift/pallas_call | solution.py:280
  139.7 20.2 %all-to-all-start.2 = ((bf16[8,2,16,2560]{3,2,1,0:T(8,128)(2,1)}), bf16[8,2,16,2560]{3,2,1,0:T(8,128)(2,1)}, u32[]{:S(2)}, u32[]{:S(2)}) async-start(bf16[8,2,16,2560]{3,2,1,0:T(8,128)(2,1)} %get-tuple-element.43), calls=%async_computation.2 | async-start | bytes 2621440 | tf_op jit(solution)/shard_map/all_to_all | solution.py:30
  161.5 4.5 %collective-permute-start.8 = (bf16[256,384]{1,0:T(8,128)(2,1)S(1)}, bf16[256,384]{1,0:T(8,128)(2,1)S(1)}, u32[]{:S(2)}, u32[]{:S(2)}) collective-permute-start(bf16[256,384]{1,0:T(8,128)(2,1)S(1)} %get-tuple-element.44), channel_id=1, source_target_pairs={{0,1},{1,0},{2,3},{3,2},{4,5},{5,4},{6,7},{7,6},{8,9},{9,8},{10,11... | collective-permute-start | bytes 589832 | tf_op jit(solution)/shard_map/ppermute | solution.py:34
  166.0 1.9 collective-permute-start.5
  168.0 29.5 %collective-permute-done.8.other = bf16[256,384]{1,0:T(8,128)(2,1)S(1)} collective-permute-done((bf16[256,384]{1,0:T(8,128)(2,1)S(1)}, bf16[256,384]{1,0:T(8,128)(2,1)S(1)}, u32[]{:S(2)}, u32[]{:S(2)}) %collective-permute-start.8) | collective-permute-done | bytes 196640 | tf_op jit(solution)/shard_map/ppermute | solution.py:34
  198.1 3.1 %share.1 = (bf16[256,1024]{1,0:T(8,128)(2,1)}, bf16[256,1024]{1,0:T(8,128)(2,1)}, bf16[256,1024]{1,0:T(8,128)(2,1)}, bf16[256,1024]{1,0:T(8,128)(2,1)}) custom-call(s32[2]{0:T(128)} %pad_add_fusion.place, bf16[8,2,16,2560]{3,2,1,0:T(8,128)(2,1)} %copy-done.2, f32[256,384]{1,0:T(8,128)} %get-tuple-element.45.partial, bf16[256,384]{1,0:T(8,128)(2,1)} %copy-done.12, ...), custom_call_target="tpu_custom_call" | custom-call | tf_op jit(solution)/shard_map/share/pallas_call | solution.py:300
  201.2 2.6 %collective-permute-start.10 = (bf16[256,1024]{1,0:T(8,128)(2,1)}, bf16[256,1024]{1,0:T(8,128)(2,1)S(1)}, u32[]{:S(2)}, u32[]{:S(2)}) collective-permute-start(bf16[256,1024]{1,0:T(8,128)(2,1)} %get-tuple-element.38), channel_id=1, source_target_pairs={{0,4},{2,6},{4,0},{6,2},{1,5},{3,7},{5,1},{7,3},{8,12},{10,14},{12... | collective-permute-start | bytes 1572872 | tf_op jit(solution)/shard_map/ppermute | solution.py:39
  203.8 1.9 collective-permute-start.11
  205.7 3.4 %collective-permute-start.9 = (bf16[256,1024]{1,0:T(8,128)(2,1)}, bf16[256,1024]{1,0:T(8,128)(2,1)S(1)}, u32[]{:S(2)}, u32[]{:S(2)}) collective-permute-start(bf16[256,1024]{1,0:T(8,128)(2,1)} %get-tuple-element.37), channel_id=1, source_target_pairs={{0,2},{2,4},{4,6},{6,0},{1,3},{3,5},{5,7},{7,1},{8,10},{10,12},{12... | collective-permute-start | bytes 1572872 | tf_op jit(solution)/shard_map/ppermute | solution.py:39
  209.1 5.4 %collective-permute-start.6 = (bf16[256,640]{1,0:T(8,128)(2,1)S(1)}, bf16[256,640]{1,0:T(8,128)(2,1)S(1)}, u32[]{:S(2)}, u32[]{:S(2)}) collective-permute-start(bf16[256,640]{1,0:T(8,128)(2,1)S(1)} %bitcast.47), channel_id=1, source_target_pairs={{0,4},{2,6},{4,0},{6,2},{1,5},{3,7},{5,1},{7,3},{8,12},{10,14},{12... | collective-permute-start | bytes 983048 | tf_op jit(solution)/shard_map/ppermute | solution.py:39
  214.6 1.9 collective-permute-start.7
  216.5 3.2 %gram.1 = f32[64,128]{1,0:T(8,128)} custom-call(bf16[2,8,16,2688]{3,2,1,0:T(8,128)(2,1)} %bitcast.30, bf16[8,2,16,2560]{3,2,1,0:T(8,128)(2,1)} %all-to-all-done.2.outs), custom_call_target="tpu_custom_call" | custom-call | tf_op jit(solution)/shard_map/gram/pallas_call | solution.py:312
  219.7 11.4 %all-to-all-start.3 = ((f32[64,1,128]{2,1,0:T(1,128)}), f32[64,1,128]{2,1,0:T(1,128)S(1)}, u32[]{:S(2)}, u32[]{:S(2)}) async-start(f32[64,1,128]{2,1,0:T(1,128)} %bitcast.40), calls=%async_computation.3 | async-start | bytes 65536 | tf_op jit(solution)/shard_map/all_to_all | solution.py:30
  231.0 3.6 %collective-permute-done.6.refs_6_ = bf16[256,640]{1,0:T(8,128)(2,1)S(1)} collective-permute-done((bf16[256,640]{1,0:T(8,128)(2,1)S(1)}, bf16[256,640]{1,0:T(8,128)(2,1)S(1)}, u32[]{:S(2)}, u32[]{:S(2)}) %collective-permute-start.6) | collective-permute-done | bytes 327712 | tf_op jit(solution)/shard_map/ppermute | solution.py:39
  234.7 9.6 %collective-permute-done.7.refs_7_ = bf16[256,640]{1,0:T(8,128)(2,1)S(1)} collective-permute-done((bf16[256,640]{1,0:T(8,128)(2,1)S(1)}, bf16[256,640]{1,0:T(8,128)(2,1)S(1)}, u32[]{:S(2)}, u32[]{:S(2)}) %collective-permute-start.7) | collective-permute-done | bytes 327712 | tf_op jit(solution)/shard_map/ppermute | solution.py:39
  245.5 6.4 %weights.3 = (bf16[384,640]{1,0:T(8,128)(2,1)}, bf16[640,384]{1,0:T(8,128)(2,1)}, f32[1,640]{1,0:T(1,128)}) custom-call(bf16[384,896]{1,0:T(8,128)(2,1)} %get-tuple-element.24.up_0.refs_0_, bf16[384,896]{1,0:T(8,128)(2,1)} %copy-done.3, bf16[384,896]{1,0:T(8,128)(2,1)} %copy-done.4, bf16[384,896]{1,0:T(8,128)(2,1)} %copy-done.5, bf16[256,640]{1,0:T(8,128)(2,1)} %bitcast.39, ...), custom_call_target="tpu_custom_call" | custom-call | tf_op jit(solution)/shard_map/weights/pallas_call | solution.py:321
  (47 shorter events, 9.0 us)
Async XLA Ops:
  59.5 1.1 copy-start.1
  64.0 4.2 %copy-start.13 = (bf16[1,128,384]{2,1,0:T(8,128)(2,1)S(1)}, bf16[1,128,384]{2,1,0:T(8,128)(2,1)}, u32[]{:S(2)}) copy-start(bf16[1,128,384]{2,1,0:T(8,128)(2,1)} %param.8) | copy-start | bytes 294916
  64.0 75.6 %all-to-all-start.1 = ((bf16[8,2,16,2560]{3,2,1,0:T(8,128)(2,1)}), bf16[8,2,16,2560]{3,2,1,0:T(8,128)(2,1)S(1)}, u32[]{:S(2)}, u32[]{:S(2)}) async-start(bf16[8,2,16,2560]{3,2,1,0:T(8,128)(2,1)} %mix.1.mixed), calls=%async_computation.1 | async-start | bytes 2621440 | tf_op jit(solution)/shard_map/all_to_all | solution.py:30
  68.2 16.7 %collective-permute-start = (bf16[128,384]{1,0:T(8,128)(2,1)S(1)}, bf16[128,384]{1,0:T(8,128)(2,1)S(1)}, u32[]{:S(2)}, u32[]{:S(2)}) collective-permute-start(bf16[128,384]{1,0:T(8,128)(2,1)S(1)} %bitcast.42), channel_id=1, source_target_pairs={{0,1},{1,0},{2,3},{3,2},{4,5},{5,4},{6,7},{7,6},{8,9},{9,8},{10,11... | collective-permute-start | bytes 294920 | tf_op jit(solution)/shard_map/ppermute | solution.py:34
  84.9 0.6 copy-start.14
  88.1 16.4 %collective-permute-start.1 = (bf16[384,896]{1,0:T(8,128)(2,1)}, bf16[384,896]{1,0:T(8,128)(2,1)S(1)}, u32[]{:S(2)}, u32[]{:S(2)}) collective-permute-start(bf16[384,896]{1,0:T(8,128)(2,1)} %get-tuple-element.24.up_0.refs_0_), channel_id=1, source_target_pairs={{0,2},{2,4},{4,6},{6,0},{1,3},{3,5},{5,7},{7,1},{8,10},{10,12},{12... | collective-permute-start | bytes 2064392 | tf_op jit(solution)/shard_map/ppermute | solution.py:39
  91.2 17.7 %collective-permute-start.2 = (bf16[384,896]{1,0:T(8,128)(2,1)}, bf16[384,896]{1,0:T(8,128)(2,1)S(1)}, u32[]{:S(2)}, u32[]{:S(2)}) collective-permute-start(bf16[384,896]{1,0:T(8,128)(2,1)} %get-tuple-element.24.up_0.refs_0_), channel_id=1, source_target_pairs={{0,4},{2,6},{4,0},{6,2},{1,5},{3,7},{5,1},{7,3},{8,12},{10,14},{12... | collective-permute-start | bytes 2064392 | tf_op jit(solution)/shard_map/ppermute | solution.py:39
  94.0 33.1 %collective-permute-start.3 = (bf16[384,896]{1,0:T(8,128)(2,1)}, bf16[384,896]{1,0:T(8,128)(2,1)S(1)}, u32[]{:S(2)}, u32[]{:S(2)}) collective-permute-start(bf16[384,896]{1,0:T(8,128)(2,1)} %get-tuple-element.24.up_0.refs_0_), channel_id=1, source_target_pairs={{0,6},{2,0},{4,2},{6,4},{1,7},{3,1},{5,3},{7,5},{8,14},{10,8},{12,... | collective-permute-start | bytes 2064392 | tf_op jit(solution)/shard_map/ppermute | solution.py:39
  97.7 37.2 %collective-permute-start.4 = (bf16[128,2688]{1,0:T(8,128)(2,1)}, bf16[128,2688]{1,0:T(8,128)(2,1)}, u32[]{:S(2)}, u32[]{:S(2)}) collective-permute-start(bf16[128,2688]{1,0:T(8,128)(2,1)} %get-tuple-element.26), channel_id=1, source_target_pairs={{0,1},{1,0},{2,3},{3,2},{4,5},{5,4},{6,7},{7,6},{8,9},{9,8},{10,11... | collective-permute-start | bytes 2064392 | tf_op jit(solution)/shard_map/ppermute | solution.py:34
  104.5 22.5 %copy-start.3 = (bf16[384,896]{1,0:T(8,128)(2,1)}, bf16[384,896]{1,0:T(8,128)(2,1)S(1)}, u32[]{:S(2)}) copy-start(bf16[384,896]{1,0:T(8,128)(2,1)S(1)} %collective-permute-done.1.up_1.refs_1_) | copy-start | bytes 2064388
  109.0 18.1 %copy-start.4 = (bf16[384,896]{1,0:T(8,128)(2,1)}, bf16[384,896]{1,0:T(8,128)(2,1)S(1)}, u32[]{:S(2)}) copy-start(bf16[384,896]{1,0:T(8,128)(2,1)S(1)} %collective-permute-done.2.up_2.refs_2_) | copy-start | bytes 2064388
  127.0 0.8 copy-start.5
  139.7 20.2 %copy-start.2 = (bf16[8,2,16,2560]{3,2,1,0:T(8,128)(2,1)}, bf16[8,2,16,2560]{3,2,1,0:T(8,128)(2,1)S(1)}, u32[]{:S(2)}) copy-start(bf16[8,2,16,2560]{3,2,1,0:T(8,128)(2,1)S(1)} %all-to-all-done.1.grads) | copy-start | bytes 3932164
  139.7 20.2 %copy-start = (bf16[384,2560]{1,0:T(8,128)(2,1)S(1)}, bf16[384,2560]{1,0:T(8,128)(2,1)}, u32[]{:S(2)}) copy-start(bf16[384,2560]{1,0:T(8,128)(2,1)} %up_rows.1.up_half) | copy-start | bytes 5898244
  139.7 76.8 %all-to-all-start.2 = ((bf16[8,2,16,2560]{3,2,1,0:T(8,128)(2,1)}), bf16[8,2,16,2560]{3,2,1,0:T(8,128)(2,1)}, u32[]{:S(2)}, u32[]{:S(2)}) async-start(bf16[8,2,16,2560]{3,2,1,0:T(8,128)(2,1)} %get-tuple-element.43), calls=%async_computation.2 | async-start | bytes 2621440 | tf_op jit(solution)/shard_map/all_to_all | solution.py:30
  161.5 47.6 %copy-start.16 = (bf16[8,2,16,640]{3,2,1,0:T(8,128)(2,1)S(1)}, bf16[8,2,16,640]{3,2,1,0:T(8,128)(2,1)}, u32[]{:S(2)}) copy-start(bf16[8,2,16,640]{3,2,1,0:T(8,128)(2,1)} %get-tuple-element.31) | copy-start | bytes 983044
  161.5 53.1 %copy-start.15 = (bf16[8,2,16,640]{3,2,1,0:T(8,128)(2,1)S(1)}, bf16[8,2,16,640]{3,2,1,0:T(8,128)(2,1)}, u32[]{:S(2)}) copy-start(bf16[8,2,16,640]{3,2,1,0:T(8,128)(2,1)} %get-tuple-element.32) | copy-start | bytes 983044
  161.5 36.0 %collective-permute-start.8 = (bf16[256,384]{1,0:T(8,128)(2,1)S(1)}, bf16[256,384]{1,0:T(8,128)(2,1)S(1)}, u32[]{:S(2)}, u32[]{:S(2)}) collective-permute-start(bf16[256,384]{1,0:T(8,128)(2,1)S(1)} %get-tuple-element.44), channel_id=1, source_target_pairs={{0,1},{1,0},{2,3},{3,2},{4,5},{5,4},{6,7},{7,6},{8,9},{9,8},{10,11... | collective-permute-start | bytes 589832 | tf_op jit(solution)/shard_map/ppermute | solution.py:34
  166.0 48.5 %collective-permute-start.5 = (bf16[256,640]{1,0:T(8,128)(2,1)}, bf16[256,640]{1,0:T(8,128)(2,1)S(1)}, u32[]{:S(2)}, u32[]{:S(2)}) collective-permute-start(bf16[256,640]{1,0:T(8,128)(2,1)} %bitcast.13), channel_id=1, source_target_pairs={{0,2},{2,4},{4,6},{6,0},{1,3},{3,5},{5,7},{7,1},{8,10},{10,12},{12... | collective-permute-start | bytes 983048 | tf_op jit(solution)/shard_map/ppermute | solution.py:39
  197.5 0.7 copy-start.12
  201.2 43.0 %collective-permute-start.10 = (bf16[256,1024]{1,0:T(8,128)(2,1)}, bf16[256,1024]{1,0:T(8,128)(2,1)S(1)}, u32[]{:S(2)}, u32[]{:S(2)}) collective-permute-start(bf16[256,1024]{1,0:T(8,128)(2,1)} %get-tuple-element.38), channel_id=1, source_target_pairs={{0,4},{2,6},{4,0},{6,2},{1,5},{3,7},{5,1},{7,3},{8,12},{10,14},{12... | collective-permute-start | bytes 1572872 | tf_op jit(solution)/shard_map/ppermute | solution.py:39
  203.8 40.4 %collective-permute-start.11 = (bf16[256,1024]{1,0:T(8,128)(2,1)}, bf16[256,1024]{1,0:T(8,128)(2,1)S(1)}, u32[]{:S(2)}, u32[]{:S(2)}) collective-permute-start(bf16[256,1024]{1,0:T(8,128)(2,1)} %get-tuple-element.39), channel_id=1, source_target_pairs={{0,6},{2,0},{4,2},{6,4},{1,7},{3,1},{5,3},{7,5},{8,14},{10,8},{12,... | collective-permute-start | bytes 1572872 | tf_op jit(solution)/shard_map/ppermute | solution.py:39
  205.7 38.5 %collective-permute-start.9 = (bf16[256,1024]{1,0:T(8,128)(2,1)}, bf16[256,1024]{1,0:T(8,128)(2,1)S(1)}, u32[]{:S(2)}, u32[]{:S(2)}) collective-permute-start(bf16[256,1024]{1,0:T(8,128)(2,1)} %get-tuple-element.37), channel_id=1, source_target_pairs={{0,2},{2,4},{4,6},{6,0},{1,3},{3,5},{5,7},{7,1},{8,10},{10,12},{12... | collective-permute-start | bytes 1572872 | tf_op jit(solution)/shard_map/ppermute | solution.py:39
  209.1 25.6 %collective-permute-start.6 = (bf16[256,640]{1,0:T(8,128)(2,1)S(1)}, bf16[256,640]{1,0:T(8,128)(2,1)S(1)}, u32[]{:S(2)}, u32[]{:S(2)}) collective-permute-start(bf16[256,640]{1,0:T(8,128)(2,1)S(1)} %bitcast.47), channel_id=1, source_target_pairs={{0,4},{2,6},{4,0},{6,2},{1,5},{3,7},{5,1},{7,3},{8,12},{10,14},{12... | collective-permute-start | bytes 983048 | tf_op jit(solution)/shard_map/ppermute | solution.py:39
  214.5 5.1 %copy-start.9 = (bf16[256,640]{1,0:T(8,128)(2,1)}, bf16[256,640]{1,0:T(8,128)(2,1)S(1)}, u32[]{:S(2)}) copy-start(bf16[256,640]{1,0:T(8,128)(2,1)S(1)} %collective-permute-done.5.refs_5_) | copy-start | bytes 983044
  214.6 29.7 %collective-permute-start.7 = (bf16[256,640]{1,0:T(8,128)(2,1)S(1)}, bf16[256,640]{1,0:T(8,128)(2,1)S(1)}, u32[]{:S(2)}, u32[]{:S(2)}) collective-permute-start(bf16[256,640]{1,0:T(8,128)(2,1)S(1)} %bitcast.46), channel_id=1, source_target_pairs={{0,6},{2,0},{4,2},{6,4},{1,7},{3,1},{5,3},{7,5},{8,14},{10,8},{12,... | collective-permute-start | bytes 983048 | tf_op jit(solution)/shard_map/ppermute | solution.py:39
  219.7 32.2 %all-to-all-start.3 = ((f32[64,1,128]{2,1,0:T(1,128)}), f32[64,1,128]{2,1,0:T(1,128)S(1)}, u32[]{:S(2)}, u32[]{:S(2)}) async-start(f32[64,1,128]{2,1,0:T(1,128)} %bitcast.40), calls=%async_computation.3 | async-start | bytes 65536 | tf_op jit(solution)/shard_map/all_to_all | solution.py:30
  234.7 9.6 %copy-start.10 = (bf16[256,640]{1,0:T(8,128)(2,1)}, bf16[256,640]{1,0:T(8,128)(2,1)S(1)}, u32[]{:S(2)}) copy-start(bf16[256,640]{1,0:T(8,128)(2,1)S(1)} %collective-permute-done.6.refs_6_) | copy-start | bytes 983044
  244.2 0.7 copy-start.11
  244.2 0.9 copy-start.6
  244.2 1.1 copy-start.7
  244.3 1.3 copy-start.8

commit v9 on v8

--- a/solution.py
+++ b/solution.py
@@ -111,7 +111,8 @@
     out[:, BLOCK:] = jnp.transpose(whole_act).astype(jnp.bfloat16)
 
 
-def up_rows_body(place, up_0, up_1, up_2, up_3, out):
+def up_rows_body(place, up_0, up_1, up_2, up_3, mixed, out):
+    del mixed
     for i in range(4):
         turn = lax.rem(place[1] - i + 4, 4)
         pieces = [up[:, :BLOCK] for up in (up_0, up_1, up_2, up_3)]
@@ -142,7 +143,8 @@
             sends[:, half, :, lanes] = (rows_in.astype(jnp.float32) + branch).astype(jnp.bfloat16)
 
 
-def mix_body(coef, grads, out):
+def mix_body(place, coef, grads, *refs):
+    outs, out = refs[:-1], refs[-1]
     sections, halves, _, cols = out.shape
     for half in range(halves):
         for at in range(0, cols, LANES):
@@ -153,6 +155,14 @@
                 for m in range(1, sections - k):
                     total = total + coef[k, m] * tiles[k + m]
                 out[k, half, :, lanes] = total.astype(jnp.bfloat16)
+    for step, ref in enumerate(outs):
+        ref[...] = out[lax.bitwise_xor(place[2], step)]
+
+
+def order_body(place, *refs):
+    pieces, out = refs[:-1], refs[-1]
+    for step, piece in enumerate(pieces):
+        out[lax.bitwise_xor(place[2], step)] = piece[...]
 
 
 def gram_body(grads, outs, result):
@@ -224,7 +234,8 @@
     block = width // (xs * zs)
     half_width = xs * block
     rows = tokens // sections
-    place = jnp.stack([lax.axis_index("zh"), lax.axis_index("x")]).astype(jnp.int32)
+    at_group = lax.axis_index("zl") * lax.axis_size("yh") + lax.axis_index("yh")
+    place = jnp.stack([lax.axis_index("zh"), lax.axis_index("x"), at_group]).astype(jnp.int32)
 
     packed = pl.pallas_call(
         pack_grads_body,
@@ -264,33 +275,43 @@
     ups = [up_part]
     for step in range(1, xs):
         ups.append(shifted(up_part, "x", step))
+    weights = jnp.sum(grads[0, :, :TERMS, half_width : half_width + MIXES].astype(jnp.float32), axis=1)
+    chunk = shape((sections, zs, rows, half_width))
+    mixed = pl.pallas_call(
+        mix_body,
+        in_specs=[SMEM, SMEM, VMEM],
+        out_specs=[VMEM] * sections,
+        out_shape=[shape(chunk.shape[1:])] * sections,
+        scratch_shapes=[pltpu.VMEM(chunk.shape, jnp.bfloat16)],
+        name="mix",
+    )(place, weights, grads)
+    arrived = [mixed[0]]
+    for step in range(1, sections):
+        arrived.append(lax.ppermute(mixed[step], GROUP, [(k, k ^ step) for k in range(sections)]))
+    arrived = pl.pallas_call(
+        order_body, in_specs=[SMEM] + [VMEM] * sections, out_specs=VMEM, out_shape=chunk, name="order"
+    )(place, *arrived)
+
     up_half = pl.pallas_call(
         up_rows_body,
-        in_specs=[SMEM] + [VMEM] * xs,
+        in_specs=[SMEM] + [VMEM] * xs + [pl.BlockSpec(memory_space=pl.ANY)],
         out_specs=VMEM,
         out_shape=shape((ranks, half_width)),
         name="up_rows",
-    )(place, *ups)
-
-    weights = jnp.sum(grads[0, :, :TERMS, half_width : half_width + MIXES].astype(jnp.float32), axis=1)
-    chunk = shape((sections, zs, rows, half_width))
-    mixed = pl.pallas_call(mix_body, in_specs=[SMEM, VMEM], out_specs=VMEM, out_shape=chunk, name="mix")(weights, grads)
-    arrived = exchange(mixed, GROUP)
-
+    )(place, *ups, mixed[0])
     layer_out, scale, *moved = pl.pallas_call(
         lift_body,
         in_specs=[SMEM] + [VMEM] * 5 + [pl.BlockSpec(memory_space=pl.ANY)],
         out_specs=[VMEM] * (2 + xs),
         out_shape=[chunk, shape((sections, zs, rows, ranks), jnp.float32)] + [shape((sections, zs, rows, block))] * xs,
         name="lift",
-    )(place, kept, other, act, slopes, up_half, mixed)
+    )(place, kept, other, act, slopes, up_half, mixed[0])
     scale = scale.reshape(zs * tokens, ranks)
     for step in range(xs):
         moved[step] = moved[step].reshape(zs * tokens, block)
         if step:
             moved[step] = shifted(moved[step], "x", step)
 
-    layer_out, arrived = lax.optimization_barrier((layer_out, arrived))
     outs = exchange(layer_out, GROUP)
 
     act_partial = jnp.einsum(

time: 253 us -> 272 us (1.075)
  the two profiles are of different devices: /device:TPU:11 before, /device:TPU:59 now
where the time goes in v9:
time: 272 us; the launch traced here: 271 us
  starting transfers between devices  115 us (42%)
  waiting for transfers between devices  110 us (40%)
  Pallas kernels  34.7 us (13%)
  local copies, waits for them, and re-layouts  5.98 us (2%)
  matrix products  2.92 us (1%)
    all_to_all x3, starting transfers between devices, exchange(): return lax.all_to_all(pieces, axes, split_axis=0, concat_axis=0, tiled=True)  44.9 us
    ppermute x3, waiting for transfers between devices, swapped(): return lax.ppermute(value, axis, [(0, 1), (1, 0)])  41.5 us
    ppermute x7, waiting for transfers between devices, whole(): lax.ppermute(mixed[step], GROUP, [(k, k ^ step) for k in range(sections)])  34.7 us
    ppermute x9, waiting for transfers between devices, shifted(): lax.ppermute(value, axis, [(i, (i + steps) % count) for i in range(count)])  33.7 us
    ppermute x7, starting transfers between devices, whole(): lax.ppermute(mixed[step], GROUP, [(k, k ^ step) for k in range(sections)])  30.1 us
    ppermute x9, starting transfers between devices, shifted(): lax.ppermute(value, axis, [(i, (i + steps) % count) for i in range(count)])  29.3 us
    ppermute x3, starting transfers between devices, swapped(): return lax.ppermute(value, axis, [(0, 1), (1, 0)])  10.8 us
    pallas_call x1, Pallas kernels, whole(): pl.pallas_call(weights_body, in_specs=[VMEM] * (3 * xs + 2), out_specs=[V...  6.37 us
  transfers between devices with their start and end apart: 22, of which 9 were waited for; matrix products, arithmetic and copies ran while one was open for 2% of the time, Pallas kernels for 10%

profile of v9, /device:TPU:59, one launch (start us, length us, event | category | flops | bytes accessed | tf_op | source)
XLA Modules:
  0.0 271.0 jit_solution(9152707708330480408)
XLA Ops:
  3.2 15.3 %all-to-all-start = ((bf16[16,16,2688]{2,1,0:T(8,128)(2,1)}), bf16[16,16,2688]{2,1,0:T(8,128)(2,1)S(1)}, u32[]{:S(2)}, u32[]{:S(2)}) async-start(bf16[16,16,2688]{2,1,0:T(8,128)(2,1)} %bitcast.33), calls=%async_computation | async-start | bytes 2752512 | tf_op jit(solution)/shard_map/all_to_all | solution.py:30
  18.4 7.0 %collective-permute-start = (bf16[128,384]{1,0:T(8,128)(2,1)S(1)}, bf16[128,384]{1,0:T(8,128)(2,1)S(1)}, u32[]{:S(2)}, u32[]{:S(2)}) collective-permute-start(bf16[128,384]{1,0:T(8,128)(2,1)S(1)} %bitcast.43), channel_id=1, source_target_pairs={{0,1},{1,0},{2,3},{3,2},{4,5},{5,4},{6,7},{7,6},{8,9},{9,8},{10,11... | collective-permute-start | bytes 294920 | tf_op jit(solution)/shard_map/ppermute | solution.py:34
  26.1 34.6 %collective-permute-done = bf16[128,384]{1,0:T(8,128)(2,1)S(1)} collective-permute-done((bf16[128,384]{1,0:T(8,128)(2,1)S(1)}, bf16[128,384]{1,0:T(8,128)(2,1)S(1)}, u32[]{:S(2)}, u32[]{:S(2)}) %collective-permute-start) | collective-permute-done | bytes 98336 | tf_op jit(solution)/shard_map/ppermute | solution.py:34
  63.9 3.1 %collective-permute-start.1 = (bf16[384,896]{1,0:T(8,128)(2,1)}, bf16[384,896]{1,0:T(8,128)(2,1)S(1)}, u32[]{:S(2)}, u32[]{:S(2)}) collective-permute-start(bf16[384,896]{1,0:T(8,128)(2,1)} %get-tuple-element.30.up_0.refs_0_), channel_id=1, source_target_pairs={{0,2},{2,4},{4,6},{6,0},{1,3},{3,5},{5,7},{7,1},{8,10},{10,12},{12... | collective-permute-start | bytes 2064392 | tf_op jit(solution)/shard_map/ppermute | solution.py:39
  67.0 2.7 %collective-permute-start.2 = (bf16[384,896]{1,0:T(8,128)(2,1)}, bf16[384,896]{1,0:T(8,128)(2,1)S(1)}, u32[]{:S(2)}, u32[]{:S(2)}) collective-permute-start(bf16[384,896]{1,0:T(8,128)(2,1)} %get-tuple-element.30.up_0.refs_0_), channel_id=1, source_target_pairs={{0,4},{2,6},{4,0},{6,2},{1,5},{3,7},{5,1},{7,3},{8,12},{10,14},{12... | collective-permute-start | bytes 2064392 | tf_op jit(solution)/shard_map/ppermute | solution.py:39
  69.7 3.8 %collective-permute-start.3 = (bf16[384,896]{1,0:T(8,128)(2,1)}, bf16[384,896]{1,0:T(8,128)(2,1)S(1)}, u32[]{:S(2)}, u32[]{:S(2)}) collective-permute-start(bf16[384,896]{1,0:T(8,128)(2,1)} %get-tuple-element.30.up_0.refs_0_), channel_id=1, source_target_pairs={{0,6},{2,0},{4,2},{6,4},{1,7},{3,1},{5,3},{7,5},{8,14},{10,8},{12,... | collective-permute-start | bytes 2064392 | tf_op jit(solution)/shard_map/ppermute | solution.py:39
  73.5 2.9 %pack_inputs.1 = (bf16[128,2688]{1,0:T(8,128)(2,1)}, bf16[128,2688]{1,0:T(8,128)(2,1)}) custom-call(s32[3]{0:T(128)} %pad_add_fusion.place, bf16[128,5120]{1,0:T(8,128)(2,1)} %bitcast.35), custom_call_target="tpu_custom_call" | custom-call | tf_op jit(solution)/shard_map/pack_inputs/pallas_call | solution.py:251
  79.4 3.4 %mix.1 = (bf16[2,16,2560]{2,1,0:T(8,128)(2,1)}, bf16[2,16,2560]{2,1,0:T(8,128)(2,1)}, bf16[2,16,2560]{2,1,0:T(8,128)(2,1)}, bf16[2,16,2560]{2,1,0:T(8,128)(2,1)}...) custom-call(s32[3]{0:T(128)} %pad_add_fusion.place, ...), custom_call_target="tpu_custom_call" | custom-call | tf_op jit(solution)/shard_map/mix/pallas_call | solution.py:280
  82.8 3.2 %collective-permute-done.2.up_2.refs_2_ = bf16[384,896]{1,0:T(8,128)(2,1)S(1)} collective-permute-done((bf16[384,896]{1,0:T(8,128)(2,1)}, bf16[384,896]{1,0:T(8,128)(2,1)S(1)}, u32[]{:S(2)}, u32[]{:S(2)}) %collective-permute-start.2) | collective-permute-done | bytes 688160 | tf_op jit(solution)/shard_map/ppermute | solution.py:39
  86.0 16.8 %collective-permute-done.3.up_3.refs_3_ = bf16[384,896]{1,0:T(8,128)(2,1)S(1)} collective-permute-done((bf16[384,896]{1,0:T(8,128)(2,1)}, bf16[384,896]{1,0:T(8,128)(2,1)S(1)}, u32[]{:S(2)}, u32[]{:S(2)}) %collective-permute-start.3) | collective-permute-done | bytes 688160 | tf_op jit(solution)/shard_map/ppermute | solution.py:39
  103.7 3.5 %up_rows.1.up_half = bf16[384,2560]{1,0:T(8,128)(2,1)} custom-call(s32[3]{0:T(128)} %pad_add_fusion.place, bf16[384,896]{1,0:T(8,128)(2,1)} %get-tuple-element.30.up_0.refs_0_, bf16[384,896]{1,0:T(8,128)(2,1)} %copy-done.3, bf16[384,896]{1,0:T(8,128)(2,1)} %copy-done.4, bf16[384,896]{1,0:T(8,128)(2,1)} %copy-done.5, ...), custom_call_target="tpu_custom_call" | custom-call | tf_op jit(solution)/shard_map/up_rows/pallas_call | solution.py:295
  107.1 4.7 %lift.1 = (bf16[8,2,16,2560]{3,2,1,0:T(8,128)(2,1)}, f32[8,2,16,384]{3,2,1,0:T(8,128)}, bf16[8,2,16,640]{3,2,1,0:T(8,128)(2,1)}, bf16[8,2,16,640]{3,2,1,0:T(8,12...) custom-call(s32[3]{0:T(128)} %pad_add_fusion.place, bf16[8,16,2688]{2,1,0:T(8,128)(2,1)} %bitcast.36, ...), custom_call_target="tpu_custom_call" | custom-call | tf_op jit(solution)/shard_map/lift/pallas_call | solution.py:302
  111.9 15.9 %all-to-all-start.1 = ((bf16[8,2,16,2560]{3,2,1,0:T(8,128)(2,1)}), bf16[8,2,16,2560]{3,2,1,0:T(8,128)(2,1)S(1)}, u32[]{:S(2)}, u32[]{:S(2)}) async-start(bf16[8,2,16,2560]{3,2,1,0:T(8,128)(2,1)} %get-tuple-element.55), calls=%async_computation.1 | async-start | bytes 2621440 | tf_op jit(solution)/shard_map/all_to_all | solution.py:30
  129.7 3.4 %collective-permute-start.9 = (bf16[2,16,2560]{2,1,0:T(8,128)(2,1)S(1)}, bf16[2,16,2560]{2,1,0:T(8,128)(2,1)S(1)}, u32[]{:S(2)}, u32[]{:S(2)}) collective-permute-start(bf16[2,16,2560]{2,1,0:T(8,128)(2,1)S(1)} %copy-done.16), channel_id=1, source_target_pairs={{0,128},{64,192},{128,0},{192,64},{256,384},{320,448},{384,256},{4... | collective-permute-start | bytes 491528 | tf_op jit(solution)/shard_map/ppermute | solution.py:290
  133.1 7.0 %collective-permute-start.10 = (bf16[2,16,2560]{2,1,0:T(8,128)(2,1)}, bf16[2,16,2560]{2,1,0:T(8,128)(2,1)}, u32[]{:S(2)}, u32[]{:S(2)}) collective-permute-start(bf16[2,16,2560]{2,1,0:T(8,128)(2,1)} %get-tuple-element.42), channel_id=1, source_target_pairs={{0,192},{64,128},{128,64},{192,0},{256,448},{320,384},{384,320},{4... | collective-permute-start | bytes 491528 | tf_op jit(solution)/shard_map/ppermute | solution.py:290
  140.1 4.0 %collective-permute-start.11 = (bf16[2,16,2560]{2,1,0:T(8,128)(2,1)}, bf16[2,16,2560]{2,1,0:T(8,128)(2,1)}, u32[]{:S(2)}, u32[]{:S(2)}) collective-permute-start(bf16[2,16,2560]{2,1,0:T(8,128)(2,1)} %get-tuple-element.43), channel_id=1, source_target_pairs={{0,256},{64,320},{128,384},{192,448},{256,0},{320,64},{384,128},{4... | collective-permute-start | bytes 491528 | tf_op jit(solution)/shard_map/ppermute | solution.py:290
  146.0 20.8 %collective-permute-done.8.refs_1_ = bf16[2,16,2560]{2,1,0:T(8,128)(2,1)S(1)} collective-permute-done((bf16[2,16,2560]{2,1,0:T(8,128)(2,1)S(1)}, bf16[2,16,2560]{2,1,0:T(8,128)(2,1)S(1)}, u32[]{:S(2)}, u32[]{:S(2)}) %collective-permute-start.8) | collective-permute-done | bytes 163872 | tf_op jit(solution)/shard_map/ppermute | solution.py:290
  166.8 8.0 %collective-permute-start.13 = (bf16[2,16,2560]{2,1,0:T(8,128)(2,1)}, bf16[2,16,2560]{2,1,0:T(8,128)(2,1)}, u32[]{:S(2)}, u32[]{:S(2)}) collective-permute-start(bf16[2,16,2560]{2,1,0:T(8,128)(2,1)} %get-tuple-element.45), channel_id=1, source_target_pairs={{0,384},{64,448},{128,256},{192,320},{256,128},{320,192},{384,0},{... | collective-permute-start | bytes 491528 | tf_op jit(solution)/shard_map/ppermute | solution.py:290
  175.5 3.9 %collective-permute-start.14 = (bf16[2,16,2560]{2,1,0:T(8,128)(2,1)}, bf16[2,16,2560]{2,1,0:T(8,128)(2,1)}, u32[]{:S(2)}, u32[]{:S(2)}) collective-permute-start(bf16[2,16,2560]{2,1,0:T(8,128)(2,1)} %get-tuple-element.46), channel_id=1, source_target_pairs={{0,448},{64,384},{128,320},{192,256},{256,192},{320,128},{384,64},... | collective-permute-start | bytes 491528 | tf_op jit(solution)/shard_map/ppermute | solution.py:290
  180.9 12.4 %collective-permute-done.13.refs_6_ = bf16[2,16,2560]{2,1,0:T(8,128)(2,1)} collective-permute-done((bf16[2,16,2560]{2,1,0:T(8,128)(2,1)}, bf16[2,16,2560]{2,1,0:T(8,128)(2,1)}, u32[]{:S(2)}, u32[]{:S(2)}) %collective-permute-start.13) | collective-permute-done | bytes 163872 | tf_op jit(solution)/shard_map/ppermute | solution.py:290
  195.9 2.9 %fusion = (bf16[256,384]{1,0:T(8,128)(2,1)S(1)}, f32[256,384]{1,0:T(8,128)}) fusion(bf16[256,2560]{1,0:T(8,128)(2,1)} %bitcast.32, bf16[384,2560]{1,0:T(8,128)(2,1)S(1)} %copy-done), kind=kOutput, calls=%fused_computation.3 | convolution fusion | flops 503414784 | bytes 3866624 | tf_op jit(solution)/shard_map/tc,rc->tr/dot_general | solution.py:317
  200.7 3.0 %collective-permute-start.5 = (bf16[256,640]{1,0:T(8,128)(2,1)}, bf16[256,640]{1,0:T(8,128)(2,1)S(1)}, u32[]{:S(2)}, u32[]{:S(2)}) collective-permute-start(bf16[256,640]{1,0:T(8,128)(2,1)} %bitcast.14), channel_id=1, source_target_pairs={{0,2},{2,4},{4,6},{6,0},{1,3},{3,5},{5,7},{7,1},{8,10},{10,12},{12... | collective-permute-start | bytes 983048 | tf_op jit(solution)/shard_map/ppermute | solution.py:39
  203.7 6.9 %collective-permute-done.15.other = bf16[256,384]{1,0:T(8,128)(2,1)S(1)} collective-permute-done((bf16[256,384]{1,0:T(8,128)(2,1)S(1)}, bf16[256,384]{1,0:T(8,128)(2,1)S(1)}, u32[]{:S(2)}, u32[]{:S(2)}) %collective-permute-start.15) | collective-permute-done | bytes 196640 | tf_op jit(solution)/shard_map/ppermute | solution.py:34
  211.3 3.1 %share.1 = (bf16[256,1024]{1,0:T(8,128)(2,1)}, bf16[256,1024]{1,0:T(8,128)(2,1)}, bf16[256,1024]{1,0:T(8,128)(2,1)}, bf16[256,1024]{1,0:T(8,128)(2,1)}) custom-call(s32[3]{0:T(128)} %pad_add_fusion.place, bf16[8,2,16,2560]{3,2,1,0:T(8,128)(2,1)} %order.1.grads, f32[256,384]{1,0:T(8,128)} %get-tuple-element.57.partial, bf16[256,384]{1,0:T(8,128)(2,1)} %copy-done.11, ...), custom_call_target="tpu_custom_call" | custom-call | tf_op jit(solution)/shard_map/share/pallas_call | solution.py:321
  214.5 5.2 %collective-permute-start.16 = (bf16[256,1024]{1,0:T(8,128)(2,1)}, bf16[256,1024]{1,0:T(8,128)(2,1)S(1)}, u32[]{:S(2)}, u32[]{:S(2)}) collective-permute-start(bf16[256,1024]{1,0:T(8,128)(2,1)} %get-tuple-element.49), channel_id=1, source_target_pairs={{0,2},{2,4},{4,6},{6,0},{1,3},{3,5},{5,7},{7,1},{8,10},{10,12},{12... | collective-permute-start | bytes 1572872 | tf_op jit(solution)/shard_map/ppermute | solution.py:39
  222.1 4.0 %collective-permute-start.18 = (bf16[256,1024]{1,0:T(8,128)(2,1)}, bf16[256,1024]{1,0:T(8,128)(2,1)S(1)}, u32[]{:S(2)}, u32[]{:S(2)}) collective-permute-start(bf16[256,1024]{1,0:T(8,128)(2,1)} %get-tuple-element.51), channel_id=1, source_target_pairs={{0,6},{2,0},{4,2},{6,4},{1,7},{3,1},{5,3},{7,5},{8,14},{10,8},{12,... | collective-permute-start | bytes 1572872 | tf_op jit(solution)/shard_map/ppermute | solution.py:39
  228.4 2.8 %collective-permute-start.7 = (bf16[256,640]{1,0:T(8,128)(2,1)}, bf16[256,640]{1,0:T(8,128)(2,1)}, u32[]{:S(2)}, u32[]{:S(2)}) collective-permute-start(bf16[256,640]{1,0:T(8,128)(2,1)} %bitcast.47), channel_id=1, source_target_pairs={{0,6},{2,0},{4,2},{6,4},{1,7},{3,1},{5,3},{7,5},{8,14},{10,8},{12,... | collective-permute-start | bytes 983048 | tf_op jit(solution)/shard_map/ppermute | solution.py:39
  232.3 3.2 %gram.1 = f32[64,128]{1,0:T(8,128)} custom-call(bf16[2,8,16,2688]{3,2,1,0:T(8,128)(2,1)} %bitcast.31, bf16[8,2,16,2560]{3,2,1,0:T(8,128)(2,1)} %copy-done.2), custom_call_target="tpu_custom_call" | custom-call | tf_op jit(solution)/shard_map/gram/pallas_call | solution.py:333
  235.4 13.7 %all-to-all-start.2 = ((f32[64,1,128]{2,1,0:T(1,128)}), f32[64,1,128]{2,1,0:T(1,128)S(1)}, u32[]{:S(2)}, u32[]{:S(2)}) async-start(f32[64,1,128]{2,1,0:T(1,128)} %bitcast.41), calls=%async_computation.2 | async-start | bytes 65536 | tf_op jit(solution)/shard_map/all_to_all | solution.py:30
  249.1 4.2 %collective-permute-done.6.refs_6_ = bf16[256,640]{1,0:T(8,128)(2,1)S(1)} collective-permute-done((bf16[256,640]{1,0:T(8,128)(2,1)}, bf16[256,640]{1,0:T(8,128)(2,1)S(1)}, u32[]{:S(2)}, u32[]{:S(2)}) %collective-permute-start.6) | collective-permute-done | bytes 327712 | tf_op jit(solution)/shard_map/ppermute | solution.py:39
  253.3 9.5 %collective-permute-done.7.refs_7_ = bf16[256,640]{1,0:T(8,128)(2,1)} collective-permute-done((bf16[256,640]{1,0:T(8,128)(2,1)}, bf16[256,640]{1,0:T(8,128)(2,1)}, u32[]{:S(2)}, u32[]{:S(2)}) %collective-permute-start.7) | collective-permute-done | bytes 327712 | tf_op jit(solution)/shard_map/ppermute | solution.py:39
  264.0 6.4 %weights.3 = (bf16[384,640]{1,0:T(8,128)(2,1)}, bf16[640,384]{1,0:T(8,128)(2,1)}, f32[1,640]{1,0:T(1,128)}) custom-call(bf16[384,896]{1,0:T(8,128)(2,1)} %get-tuple-element.30.up_0.refs_0_, bf16[384,896]{1,0:T(8,128)(2,1)} %copy-done.3, bf16[384,896]{1,0:T(8,128)(2,1)} %copy-done.4, bf16[384,896]{1,0:T(8,128)(2,1)} %copy-done.5, bf16[256,640]{1,0:T(8,128)(2,1)} %bitcast.40, ...), custom_call_target="tpu_custom_call" | custom-call | tf_op jit(solution)/shard_map/weights/pallas_call | solution.py:342
  (63 shorter events, 28.9 us)
Async XLA Ops:
  3.2 15.3 %copy-start.14 = (bf16[1,128,384]{2,1,0:T(8,128)(2,1)S(1)}, bf16[1,128,384]{2,1,0:T(8,128)(2,1)}, u32[]{:S(2)}) copy-start(bf16[1,128,384]{2,1,0:T(8,128)(2,1)} %param.8) | copy-start | bytes 294916
  3.2 75.1 %all-to-all-start = ((bf16[16,16,2688]{2,1,0:T(8,128)(2,1)}), bf16[16,16,2688]{2,1,0:T(8,128)(2,1)S(1)}, u32[]{:S(2)}, u32[]{:S(2)}) async-start(bf16[16,16,2688]{2,1,0:T(8,128)(2,1)} %bitcast.33), calls=%async_computation | async-start | bytes 2752512 | tf_op jit(solution)/shard_map/all_to_all | solution.py:30
  18.4 42.3 %collective-permute-start = (bf16[128,384]{1,0:T(8,128)(2,1)S(1)}, bf16[128,384]{1,0:T(8,128)(2,1)S(1)}, u32[]{:S(2)}, u32[]{:S(2)}) collective-permute-start(bf16[128,384]{1,0:T(8,128)(2,1)S(1)} %bitcast.43), channel_id=1, source_target_pairs={{0,1},{1,0},{2,3},{3,2},{4,5},{5,4},{6,7},{7,6},{8,9},{9,8},{10,11... | collective-permute-start | bytes 294920 | tf_op jit(solution)/shard_map/ppermute | solution.py:34
  63.9 18.9 %collective-permute-start.1 = (bf16[384,896]{1,0:T(8,128)(2,1)}, bf16[384,896]{1,0:T(8,128)(2,1)S(1)}, u32[]{:S(2)}, u32[]{:S(2)}) collective-permute-start(bf16[384,896]{1,0:T(8,128)(2,1)} %get-tuple-element.30.up_0.refs_0_), channel_id=1, source_target_pairs={{0,2},{2,4},{4,6},{6,0},{1,3},{3,5},{5,7},{7,1},{8,10},{10,12},{12... | collective-permute-start | bytes 2064392 | tf_op jit(solution)/shard_map/ppermute | solution.py:39
  67.0 19.0 %collective-permute-start.2 = (bf16[384,896]{1,0:T(8,128)(2,1)}, bf16[384,896]{1,0:T(8,128)(2,1)S(1)}, u32[]{:S(2)}, u32[]{:S(2)}) collective-permute-start(bf16[384,896]{1,0:T(8,128)(2,1)} %get-tuple-element.30.up_0.refs_0_), channel_id=1, source_target_pairs={{0,4},{2,6},{4,0},{6,2},{1,5},{3,7},{5,1},{7,3},{8,12},{10,14},{12... | collective-permute-start | bytes 2064392 | tf_op jit(solution)/shard_map/ppermute | solution.py:39
  69.7 33.1 %collective-permute-start.3 = (bf16[384,896]{1,0:T(8,128)(2,1)}, bf16[384,896]{1,0:T(8,128)(2,1)S(1)}, u32[]{:S(2)}, u32[]{:S(2)}) collective-permute-start(bf16[384,896]{1,0:T(8,128)(2,1)} %get-tuple-element.30.up_0.refs_0_), channel_id=1, source_target_pairs={{0,6},{2,0},{4,2},{6,4},{1,7},{3,1},{5,3},{7,5},{8,14},{10,8},{12,... | collective-permute-start | bytes 2064392 | tf_op jit(solution)/shard_map/ppermute | solution.py:39
  76.4 30.8 %collective-permute-start.4 = (bf16[128,2688]{1,0:T(8,128)(2,1)}, bf16[128,2688]{1,0:T(8,128)(2,1)}, u32[]{:S(2)}, u32[]{:S(2)}) collective-permute-start(bf16[128,2688]{1,0:T(8,128)(2,1)} %get-tuple-element.32), channel_id=1, source_target_pairs={{0,1},{1,0},{2,3},{3,2},{4,5},{5,4},{6,7},{7,6},{8,9},{9,8},{10,11... | collective-permute-start | bytes 2064392 | tf_op jit(solution)/shard_map/ppermute | solution.py:34
  82.8 20.0 %copy-start.3 = (bf16[384,896]{1,0:T(8,128)(2,1)}, bf16[384,896]{1,0:T(8,128)(2,1)S(1)}, u32[]{:S(2)}) copy-start(bf16[384,896]{1,0:T(8,128)(2,1)S(1)} %collective-permute-done.1.up_1.refs_1_) | copy-start | bytes 2064388
  86.0 16.8 %copy-start.4 = (bf16[384,896]{1,0:T(8,128)(2,1)}, bf16[384,896]{1,0:T(8,128)(2,1)S(1)}, u32[]{:S(2)}) copy-start(bf16[384,896]{1,0:T(8,128)(2,1)S(1)} %collective-permute-done.2.up_2.refs_2_) | copy-start | bytes 2064388
  111.9 15.9 %copy-start.17 = (bf16[2,16,2560]{2,1,0:T(8,128)(2,1)S(1)}, bf16[2,16,2560]{2,1,0:T(8,128)(2,1)}, u32[]{:S(2)}) copy-start(bf16[2,16,2560]{2,1,0:T(8,128)(2,1)} %get-tuple-element.40) | copy-start | bytes 491524
  111.9 17.8 %copy-start.16 = (bf16[2,16,2560]{2,1,0:T(8,128)(2,1)S(1)}, bf16[2,16,2560]{2,1,0:T(8,128)(2,1)}, u32[]{:S(2)}) copy-start(bf16[2,16,2560]{2,1,0:T(8,128)(2,1)} %get-tuple-element.41) | copy-start | bytes 491524
  111.9 119.3 %all-to-all-start.1 = ((bf16[8,2,16,2560]{3,2,1,0:T(8,128)(2,1)}), bf16[8,2,16,2560]{3,2,1,0:T(8,128)(2,1)S(1)}, u32[]{:S(2)}, u32[]{:S(2)}) async-start(bf16[8,2,16,2560]{3,2,1,0:T(8,128)(2,1)} %get-tuple-element.55), calls=%async_computation.1 | async-start | bytes 2621440 | tf_op jit(solution)/shard_map/all_to_all | solution.py:30
  127.8 39.1 %collective-permute-start.8 = (bf16[2,16,2560]{2,1,0:T(8,128)(2,1)S(1)}, bf16[2,16,2560]{2,1,0:T(8,128)(2,1)S(1)}, u32[]{:S(2)}, u32[]{:S(2)}) collective-permute-start(bf16[2,16,2560]{2,1,0:T(8,128)(2,1)S(1)} %copy-done.17), channel_id=1, source_target_pairs={{0,64},{64,0},{128,192},{192,128},{256,320},{320,256},{384,448},{4... | collective-permute-start | bytes 491528 | tf_op jit(solution)/shard_map/ppermute | solution.py:290
  129.7 45.2 %collective-permute-start.9 = (bf16[2,16,2560]{2,1,0:T(8,128)(2,1)S(1)}, bf16[2,16,2560]{2,1,0:T(8,128)(2,1)S(1)}, u32[]{:S(2)}, u32[]{:S(2)}) collective-permute-start(bf16[2,16,2560]{2,1,0:T(8,128)(2,1)S(1)} %copy-done.16), channel_id=1, source_target_pairs={{0,128},{64,192},{128,0},{192,64},{256,384},{320,448},{384,256},{4... | collective-permute-start | bytes 491528 | tf_op jit(solution)/shard_map/ppermute | solution.py:290
  133.1 46.4 %collective-permute-start.10 = (bf16[2,16,2560]{2,1,0:T(8,128)(2,1)}, bf16[2,16,2560]{2,1,0:T(8,128)(2,1)}, u32[]{:S(2)}, u32[]{:S(2)}) collective-permute-start(bf16[2,16,2560]{2,1,0:T(8,128)(2,1)} %get-tuple-element.42), channel_id=1, source_target_pairs={{0,192},{64,128},{128,64},{192,0},{256,448},{320,384},{384,320},{4... | collective-permute-start | bytes 491528 | tf_op jit(solution)/shard_map/ppermute | solution.py:290
  140.1 39.4 %collective-permute-start.11 = (bf16[2,16,2560]{2,1,0:T(8,128)(2,1)}, bf16[2,16,2560]{2,1,0:T(8,128)(2,1)}, u32[]{:S(2)}, u32[]{:S(2)}) collective-permute-start(bf16[2,16,2560]{2,1,0:T(8,128)(2,1)} %get-tuple-element.43), channel_id=1, source_target_pairs={{0,256},{64,320},{128,384},{192,448},{256,0},{320,64},{384,128},{4... | collective-permute-start | bytes 491528 | tf_op jit(solution)/shard_map/ppermute | solution.py:290
  144.1 36.9 %collective-permute-start.12 = (bf16[2,16,2560]{2,1,0:T(8,128)(2,1)}, bf16[2,16,2560]{2,1,0:T(8,128)(2,1)}, u32[]{:S(2)}, u32[]{:S(2)}) collective-permute-start(bf16[2,16,2560]{2,1,0:T(8,128)(2,1)} %get-tuple-element.44), channel_id=1, source_target_pairs={{0,320},{64,256},{128,448},{192,384},{256,64},{320,0},{384,192},{4... | collective-permute-start | bytes 491528 | tf_op jit(solution)/shard_map/ppermute | solution.py:290
  166.8 26.5 %copy-start.12 = (bf16[2,16,2560]{2,1,0:T(8,128)(2,1)}, bf16[2,16,2560]{2,1,0:T(8,128)(2,1)S(1)}, u32[]{:S(2)}) copy-start(bf16[2,16,2560]{2,1,0:T(8,128)(2,1)S(1)} %collective-permute-done.8.refs_1_) | copy-start | bytes 491524
  166.8 26.5 %collective-permute-start.13 = (bf16[2,16,2560]{2,1,0:T(8,128)(2,1)}, bf16[2,16,2560]{2,1,0:T(8,128)(2,1)}, u32[]{:S(2)}, u32[]{:S(2)}) collective-permute-start(bf16[2,16,2560]{2,1,0:T(8,128)(2,1)} %get-tuple-element.45), channel_id=1, source_target_pairs={{0,384},{64,448},{128,256},{192,320},{256,128},{320,192},{384,0},{... | collective-permute-start | bytes 491528 | tf_op jit(solution)/shard_map/ppermute | solution.py:290
  175.5 20.3 %copy-start = (bf16[384,2560]{1,0:T(8,128)(2,1)S(1)}, bf16[384,2560]{1,0:T(8,128)(2,1)}, u32[]{:S(2)}) copy-start(bf16[384,2560]{1,0:T(8,128)(2,1)} %up_rows.1.up_half) | copy-start | bytes 5898244
  175.5 17.8 %collective-permute-start.14 = (bf16[2,16,2560]{2,1,0:T(8,128)(2,1)}, bf16[2,16,2560]{2,1,0:T(8,128)(2,1)}, u32[]{:S(2)}, u32[]{:S(2)}) collective-permute-start(bf16[2,16,2560]{2,1,0:T(8,128)(2,1)} %get-tuple-element.46), channel_id=1, source_target_pairs={{0,448},{64,384},{128,320},{192,256},{256,192},{320,128},{384,64},... | collective-permute-start | bytes 491528 | tf_op jit(solution)/shard_map/ppermute | solution.py:290
  198.8 11.8 %collective-permute-start.15 = (bf16[256,384]{1,0:T(8,128)(2,1)S(1)}, bf16[256,384]{1,0:T(8,128)(2,1)S(1)}, u32[]{:S(2)}, u32[]{:S(2)}) collective-permute-start(bf16[256,384]{1,0:T(8,128)(2,1)S(1)} %get-tuple-element.56), channel_id=1, source_target_pairs={{0,1},{1,0},{2,3},{3,2},{4,5},{5,4},{6,7},{7,6},{8,9},{9,8},{10,11... | collective-permute-start | bytes 589832 | tf_op jit(solution)/shard_map/ppermute | solution.py:34
  200.7 27.7 %collective-permute-start.5 = (bf16[256,640]{1,0:T(8,128)(2,1)}, bf16[256,640]{1,0:T(8,128)(2,1)S(1)}, u32[]{:S(2)}, u32[]{:S(2)}) collective-permute-start(bf16[256,640]{1,0:T(8,128)(2,1)} %bitcast.14), channel_id=1, source_target_pairs={{0,2},{2,4},{4,6},{6,0},{1,3},{3,5},{5,7},{7,1},{8,10},{10,12},{12... | collective-permute-start | bytes 983048 | tf_op jit(solution)/shard_map/ppermute | solution.py:39
  214.5 48.4 %collective-permute-start.16 = (bf16[256,1024]{1,0:T(8,128)(2,1)}, bf16[256,1024]{1,0:T(8,128)(2,1)S(1)}, u32[]{:S(2)}, u32[]{:S(2)}) collective-permute-start(bf16[256,1024]{1,0:T(8,128)(2,1)} %get-tuple-element.49), channel_id=1, source_target_pairs={{0,2},{2,4},{4,6},{6,0},{1,3},{3,5},{5,7},{7,1},{8,10},{10,12},{12... | collective-permute-start | bytes 1572872 | tf_op jit(solution)/shard_map/ppermute | solution.py:39
  219.7 43.2 %collective-permute-start.17 = (bf16[256,1024]{1,0:T(8,128)(2,1)}, bf16[256,1024]{1,0:T(8,128)(2,1)S(1)}, u32[]{:S(2)}, u32[]{:S(2)}) collective-permute-start(bf16[256,1024]{1,0:T(8,128)(2,1)} %get-tuple-element.50), channel_id=1, source_target_pairs={{0,4},{2,6},{4,0},{6,2},{1,5},{3,7},{5,1},{7,3},{8,12},{10,14},{12... | collective-permute-start | bytes 1572872 | tf_op jit(solution)/shard_map/ppermute | solution.py:39
  222.1 40.8 %collective-permute-start.18 = (bf16[256,1024]{1,0:T(8,128)(2,1)}, bf16[256,1024]{1,0:T(8,128)(2,1)S(1)}, u32[]{:S(2)}, u32[]{:S(2)}) collective-permute-start(bf16[256,1024]{1,0:T(8,128)(2,1)} %get-tuple-element.51), channel_id=1, source_target_pairs={{0,6},{2,0},{4,2},{6,4},{1,7},{3,1},{5,3},{7,5},{8,14},{10,8},{12,... | collective-permute-start | bytes 1572872 | tf_op jit(solution)/shard_map/ppermute | solution.py:39
  226.0 27.3 %collective-permute-start.6 = (bf16[256,640]{1,0:T(8,128)(2,1)}, bf16[256,640]{1,0:T(8,128)(2,1)S(1)}, u32[]{:S(2)}, u32[]{:S(2)}) collective-permute-start(bf16[256,640]{1,0:T(8,128)(2,1)} %bitcast.48), channel_id=1, source_target_pairs={{0,4},{2,6},{4,0},{6,2},{1,5},{3,7},{5,1},{7,3},{8,12},{10,14},{12... | collective-permute-start | bytes 983048 | tf_op jit(solution)/shard_map/ppermute | solution.py:39
  228.4 34.5 %copy-start.9 = (bf16[256,640]{1,0:T(8,128)(2,1)}, bf16[256,640]{1,0:T(8,128)(2,1)S(1)}, u32[]{:S(2)}) copy-start(bf16[256,640]{1,0:T(8,128)(2,1)S(1)} %collective-permute-done.5.refs_5_) | copy-start | bytes 983044
  228.4 34.4 %collective-permute-start.7 = (bf16[256,640]{1,0:T(8,128)(2,1)}, bf16[256,640]{1,0:T(8,128)(2,1)}, u32[]{:S(2)}, u32[]{:S(2)}) collective-permute-start(bf16[256,640]{1,0:T(8,128)(2,1)} %bitcast.47), channel_id=1, source_target_pairs={{0,6},{2,0},{4,2},{6,4},{1,7},{3,1},{5,3},{7,5},{8,14},{10,8},{12,... | collective-permute-start | bytes 983048 | tf_op jit(solution)/shard_map/ppermute | solution.py:39
  235.4 35.0 %all-to-all-start.2 = ((f32[64,1,128]{2,1,0:T(1,128)}), f32[64,1,128]{2,1,0:T(1,128)S(1)}, u32[]{:S(2)}, u32[]{:S(2)}) async-start(f32[64,1,128]{2,1,0:T(1,128)} %bitcast.41), calls=%async_computation.2 | async-start | bytes 65536 | tf_op jit(solution)/shard_map/all_to_all | solution.py:30
  253.3 9.6 %copy-start.10 = (bf16[256,640]{1,0:T(8,128)(2,1)}, bf16[256,640]{1,0:T(8,128)(2,1)S(1)}, u32[]{:S(2)}) copy-start(bf16[256,640]{1,0:T(8,128)(2,1)S(1)} %collective-permute-done.6.refs_6_) | copy-start | bytes 983044
  262.9 1.2 copy-start.8
  (8 other events, 6.8 us)
